TPU v7x, 128 devices: a whole 4x4x4 slice. The times are simulated.
128 devices in a mesh: gx: 8 (over y, x_lo), gy: 4 (over x_hi, core), gz: 4 (over z).
Axes of the slice: x: 4 (x_hi: 2, x_lo: 2; x = x_hi * 2 + x_lo), y: 4, z: 4, core: 2. Of those that a mesh axis runs over, the one named last changes fastest.
Arguments:
- features: bfloat16 [24, 8, 32, 8, 128], P('gx', 'gy', 'gz'), may hold values from -6 to 6
- positions: float32 [24, 8, 32, 24], P('gx', 'gy', 'gz'), may hold values from 0 to 256, as said below
- grid_anchor: int32 [24, 8, 32, 24], P('gx', 'gy', 'gz'), may hold values from -1 to 254, as said below
- species: int32 [24, 8, 32, 8], P('gx', 'gy', 'gz'), may hold values from 0 to 1
- neighbours: int32 [24, 8, 32, 512], P('gx', 'gy', 'gz'), may hold values from 0 to 49151, as said below
- neighbour_count: int32 [24, 8, 32, 8], P('gx', 'gy', 'gz'), may hold values from 32 to 64
- w_self: bfloat16 [128, 128], replicated, may hold values from -0.5 to 0.5
- w_neighbour: bfloat16 [128, 128], replicated, may hold values from -0.5 to 0.5
- w_radial: bfloat16 [8, 128], replicated, may hold values from -2 to 2
- radial_rates: float32 [8], replicated, may hold values from 0.05 to 2
- w_pair1: bfloat16 [128, 128], replicated, may hold values from -0.5 to 0.5
- w_pair2: bfloat16 [128, 128], replicated, may hold values from -0.5 to 0.5
- w_vector: bfloat16 [128, 128], replicated, may hold values from -0.5 to 0.5
- w_out: bfloat16 [128, 128], replicated, may hold values from -0.5 to 0.5
- w_charge: bfloat16 [128], replicated, may hold values from -0.5 to 0.5
- species_charge: float32 [2], replicated, may hold values from -1 to 1
Outputs:
- features_out: bfloat16 [24, 8, 32, 8, 128], P('gx', 'gy', 'gz')
- site_potential: float32 [24, 8, 32, 8], P('gx', 'gy', 'gz')
Inputs may be any that keep to these rules, and one draw needn't show every extreme that they name: `positions`: component d of slot s of cell (cx, cy, cz) lies in that cell: between c_d * 8 and (c_d + 1) * 8. `grid_anchor`: at the same place as in positions, the whole part of the coordinate minus 1; the coordinate lies between grid_anchor + 1 and grid_anchor + 2. `neighbours`: each entry is the index ((cx * 8 + cy) * 32 + cz) * 8 + s of an atom whose cell differs from the listing atom's cell by at most one along each dimension, periodically; never the listing atom itself.
All inputs are finite; a program needn't handle non-finite values.
Results may differ from a plain program's by a relative error of at most 0.0039.
The roundings to bfloat16 on the way count: a program that leaves them out, or rounds other values in their place, can miss the bound.
Values may be sent and summed in bfloat16 or wider, within the bound.
A program may use at most 64 MiB of HBM per device.

v0:
```python
import functools

import jax
import jax.numpy as jnp
import numpy as np
from jax import lax
from jax.experimental import pallas as pl
from jax.experimental.pallas import tpu as pltpu
from jax.sharding import PartitionSpec as P


coulomb_scale = 0.25
smearing = 1.0


def padded_2(block, sides, width):
    for axis, dim in sides:
        count = lax.axis_size(axis)
        forward = [(i, i + 1) for i in range(count - 1)]
        forward.append((count - 1, 0))
        backward = [(target, source) for source, target in forward]
        low = lax.ppermute(
            lax.slice_in_dim(block, block.shape[dim] - width, None, axis=dim), axis, forward
        )
        high = lax.ppermute(lax.slice_in_dim(block, 0, width, axis=dim), axis, backward)
        block = jnp.concatenate([low, block, high], axis=dim)
    return block


NT = (((1,), (1,)), ((), ()))


def pair_kernel(
    unroll,
    feat_ref,
    pos_ref,
    nbr_ref,
    count_ref,
    wn_ref,
    ws_ref,
    wr_ref,
    rate_ref,
    w1_ref,
    w2_ref,
    wv_ref,
    wo_ref,
    hid_ref,
    out_ref,
    feat32,
    first_w,
    pair1_w,
    pair2_w,
    hot_row,
    lane_row,
    live_row,
    sums,
):
    f32, bf16 = jnp.float32, jnp.bfloat16
    feat32[...] = feat_ref[...].astype(f32)
    first_w[:, 0:128] = (wn_ref[...].astype(f32) * 0.5).T.astype(bf16)
    first_w[:, 128:256] = (ws_ref[...].astype(f32) * 0.5).T.astype(bf16)
    pair1_w[...] = (w1_ref[...].astype(f32) * 0.5).T.astype(bf16)
    pair2_w[...] = (w2_ref[...].astype(f32) * 0.5).T.astype(bf16)
    radial_pad = jnp.concatenate(
        [jnp.zeros((88, 128), f32), wr_ref[...].astype(f32) * 0.5, jnp.zeros((32, 128), f32)], axis=0
    ).T
    cell_x0 = lax.axis_index("gx") * 3
    cell_y0 = lax.axis_index("gy") * 2
    cell_z0 = lax.axis_index("gz") * 8
    rates = rate_ref[...]

    sub8 = lax.broadcasted_iota(jnp.int32, (8, 512), 0)
    lane8 = lax.broadcasted_iota(jnp.int32, (8, 512), 1)
    sub_l = lax.broadcasted_iota(jnp.int32, (8, 128), 0)
    own_mask = (lane8 // 64) == sub8
    own_hot = jnp.where(own_mask, 1.0, 0.0).astype(f32)
    own_hot32 = jnp.concatenate([own_hot, own_hot, jnp.zeros((16, 512), f32)], axis=0).astype(bf16)
    lane_t = lax.broadcasted_iota(jnp.int32, (128, 128), 1)
    low_part = (lane_t >= 104) & (lane_t < 112)
    half_sub = sub_l // 4
    axis_sub = sub_l % 4
    box = jnp.where(axis_sub == 0, 192.0, jnp.where(axis_sub == 1, 64.0, 256.0)).astype(f32)
    box_inv = 1.0 / box
    atom_lane = lax.broadcasted_iota(jnp.int32, (8, 128), 1) // 64

    def column(col, carry):
        cx = col // 2
        cy = col % 2
        ids = nbr_ref[col]
        slot = ids & 7
        z = (ids >> 3) & 31
        y = (ids >> 8) & 7
        x = ids >> 11
        dz = (z - (cell_z0 + sub8) + 1) & 31
        dy = (y - (cell_y0 + cy) + 1) & 7
        dx = x - (cell_x0 + cx) + 1
        dx = jnp.where(dx < 0, dx + 24, dx)
        dx = jnp.where(dx >= 24, dx - 24, dx)
        strip = dx * 3 + dy
        hot_row[...] = strip * 24 + dz * 8 + slot
        lane_row[...] = ((dz + sub8) * 8 + slot) * 16 + strip
        counts = count_ref[col]
        pieces = []
        for g in range(4):
            owner = atom_lane + 2 * g
            count_g = jnp.take_along_axis(counts, owner, axis=1)
            slot_g = lax.broadcasted_iota(jnp.int32, (8, 128), 1) % 64
            pieces.append(jnp.where(slot_g < count_g, 1.0, 0.0).astype(f32))
        live_row[...] = jnp.concatenate(pieces, axis=1)

        def cell(cz):
            rows = []
            for dx_ in range(3):
                for dy_ in range(3):
                    base = ((cx + dx_) * 4 + cy + dy_) * 80 + cz * 8
                    rows.append(feat32[pl.ds(pl.multiple_of(base, 8), 24), :])
            own_base = ((cx + 1) * 4 + cy + 1) * 80 + cz * 8 + 8
            own = feat32[pl.ds(pl.multiple_of(own_base, 8), 8), :]
            left = jnp.concatenate(rows + [jnp.zeros((40, 128), f32)], axis=0)
            right = jnp.concatenate(
                [jnp.zeros((224, 128), f32), own, own, jnp.zeros((16, 128), f32)], axis=0
            )
            table = jnp.concatenate([left, right], axis=1).astype(bf16)
            proj = lax.dot_general(first_w[...], table, NT, preferred_element_type=f32)
            tail = proj[:, 128:256]
            tail_hi = tail.astype(bf16).astype(f32)
            tail = jnp.where(low_part, tail - tail_hi, tail_hi) + radial_pad
            lhs = jnp.concatenate([proj[:, 0:128].astype(bf16), tail.astype(bf16)], axis=1)

            place = []
            hot = hot_row[pl.ds(cz, 1), :]
            packed = lane_row[pl.ds(cz, 1), :]
            live = live_row[pl.ds(cz, 1), :]
            for g in range(4):
                packed_g = jnp.broadcast_to(packed[:, g * 128 : g * 128 + 128], (8, 128))
                where_g = packed_g >> 4
                strip_g = packed_g & 15
                got = jnp.zeros((8, 128), f32)
                for t in range(5):
                    hit = strip_g == (2 * t + half_sub)
                    got = jnp.where(
                        hit,
                        jnp.take_along_axis(pos_ref[col, t * 8 : t * 8 + 8, :], where_g, axis=1),
                        got,
                    )
                got = got + pltpu.roll(got, 4, 0)
                mine = jnp.take_along_axis(
                    pos_ref[col, 40:48, :], atom_lane + 2 * g + (cz + 1) * 8, axis=1
                )
                gap = got - mine
                gap = gap - box * jnp.floor(gap * box_inv + 0.5)
                place.append(gap * 0.125)
            scaled = jnp.concatenate(place, axis=1)
            square = scaled * scaled
            square = square[0:1] + square[1:2] + square[2:3]
            basis = jnp.exp(-jnp.broadcast_to(square, (8, 512)) * rates)
            cell_iota = lax.broadcasted_iota(jnp.int32, (216, 512), 0)
            hots = jnp.where(cell_iota == hot, 1.0, 0.0).astype(f32)
            rhs = jnp.concatenate(
                [jnp.concatenate([hots, basis], axis=0).astype(bf16), own_hot32], axis=0
            )
            half = jnp.dot(lhs, rhs, preferred_element_type=f32)
            latent = (half + half * jnp.tanh(half)).astype(bf16)
            half = jnp.dot(pair1_w[...], latent, preferred_element_type=f32)
            second = (half + half * jnp.tanh(half)).astype(bf16)
            half = jnp.dot(pair2_w[...], second, preferred_element_type=f32)
            third = (half + half * jnp.tanh(half)).astype(bf16)

            weighted = scaled * live
            w_hi = weighted.astype(bf16).astype(f32)
            w_lo = weighted - w_hi
            parts = [live]
            for d in range(3):
                parts += [w_hi[d : d + 1], w_lo[d : d + 1]]
            spread = jnp.concatenate(
                [jnp.where(own_mask, jnp.broadcast_to(p, (8, 512)), 0.0) for p in parts]
                + [jnp.zeros((8, 512), f32)],
                axis=0,
            ).astype(bf16)
            total = lax.dot_general(spread, third, NT, preferred_element_type=f32)
            at = pl.multiple_of((col * 8 + cz) * 8, 8)
            sums[0, pl.ds(at, 8), :] = total[0:8]
            for d in range(3):
                sums[1 + d, pl.ds(at, 8), :] = (
                    total[8 + 16 * d : 16 + 16 * d] + total[16 + 16 * d : 24 + 16 * d]
                )

        def step(i, c):
            for u in range(unroll):
                cell(i * unroll + u)
            return c

        lax.fori_loop(0, 8 // unroll, step, 0)
        return carry

    lax.fori_loop(0, 6, column, 0)
    wv = wv_ref[...]
    invariant = jnp.zeros((384, 128), f32)
    for d in range(3):
        t = sums[1 + d]
        hi = t.astype(bf16)
        lo = (t - hi.astype(f32)).astype(bf16)
        vec = jnp.dot(hi, wv, preferred_element_type=f32) + jnp.dot(
            lo, wv, preferred_element_type=f32
        )
        invariant = invariant + vec * vec
    update = (sums[0] * (1.0 / 64.0) + invariant * (1.0 / 64.0)).astype(bf16)
    out_ref[...] = (
        hid_ref[...].astype(f32) + jnp.dot(update, wo_ref[...], preferred_element_type=f32)
    ).astype(bf16)


def pair_update(
    feat_ext, pos_tab, nbr, counts, wn, ws, wr, rates, w1, w2, wv, wo, hidden, unroll=2
):
    f32, bf16 = jnp.float32, jnp.bfloat16
    vm = pl.BlockSpec(memory_space=pltpu.VMEM)
    return pl.pallas_call(
        functools.partial(pair_kernel, unroll),
        out_shape=jax.ShapeDtypeStruct((384, 128), bf16),
        in_specs=[vm] * 13,
        out_specs=vm,
        scratch_shapes=[
            pltpu.VMEM((1600, 128), f32),
            pltpu.VMEM((128, 256), bf16),
            pltpu.VMEM((128, 128), bf16),
            pltpu.VMEM((128, 128), bf16),
            pltpu.VMEM((8, 512), jnp.int32),
            pltpu.VMEM((8, 512), jnp.int32),
            pltpu.VMEM((8, 512), f32),
            pltpu.VMEM((4, 384, 128), f32),
        ],
        compiler_params=pltpu.CompilerParams(vmem_limit_bytes=40 * 1024 * 1024),
        name="pair_update",
    )(feat_ext, pos_tab, nbr, counts, wn, ws, wr, rates, w1, w2, wv, wo, hidden)

def real_basis(length):
    modes = np.arange(length)[:, None]
    cells = np.arange(length)[None, :]
    turns = 2.0 * np.pi * ((modes * cells) % length) / length
    flipped = 2.0 * np.pi * (((length - modes) * cells) % length) / length
    return np.where(modes <= length // 2, np.cos(turns), np.sin(flipped))


def two_parts(table):
    table = np.asarray(table, np.float32)
    high = table.astype(jnp.bfloat16)
    low = (table - high.astype(np.float32)).astype(jnp.bfloat16)
    return np.stack([high, low])


def mode_tables(length):
    modes = np.arange(length)
    signed = np.where(modes > length // 2, modes - length, modes)
    wave = signed * (2.0 * np.pi / length)
    modulus = ((4.0 + 2.0 * np.cos(2.0 * np.pi * modes / length)) / 6.0) ** 2
    weight = np.where((modes == 0) | (modes == length // 2), 1.0, 2.0) / length
    return np.exp(-0.5 * smearing * smearing * wave * wave) / modulus * weight, wave * wave


def ewald_tables():
    basis_z = two_parts(real_basis(256))
    order_y = np.array([4 * p + i for i in range(4) for p in range(16)])
    forward_y = real_basis(64)[:, order_y]
    basis_y = np.stack([two_parts(forward_y), two_parts(forward_y.T)])
    wide = np.zeros((256, 256))
    full_x = real_basis(192)
    for g in range(8):
        wide[:192, 32 * g : 32 * g + 27] = full_x[:, (24 * g - 1 + np.arange(27)) % 192]
    basis_x = two_parts(wide)
    green_x = np.zeros((2, 8, 256))
    gain, square = mode_tables(192)
    green_x[0, :, :192] = gain * (coulomb_scale * 4.0 * np.pi)
    green_x[1, :, :192] = square
    green_x[1, :, 192:] = 1.0
    green_y = np.repeat(np.stack(mode_tables(64))[:, :, None], 128, 2)
    green_z = np.repeat(np.stack(mode_tables(256))[:, :, None], 128, 2)
    return (
        basis_z,
        basis_y,
        basis_x,
        green_x.astype(np.float32),
        green_y.astype(np.float32),
        green_z.astype(np.float32),
    )


def split(value):
    high = value.astype(jnp.bfloat16)
    return high, (value - high.astype(jnp.float32)).astype(jnp.bfloat16)


def dot3(a, b, dims=(((1,), (0,)), ((), ()))):
    def one(u, v):
        return lax.dot_general(u, v, dims, preferred_element_type=jnp.float32)

    return one(a[0], b[0]) + (one(a[0], b[1]) + one(a[1], b[0]))


def swap_groups(pieces, shift):
    lane = lax.broadcasted_iota(jnp.int32, pieces[0].shape, 1) // 32
    out = None
    for k, piece in enumerate(pieces):
        moved = pltpu.roll(piece, (32 * (k - shift)) % 128, 1) if k != shift else piece
        out = moved if out is None else jnp.where(lane == k, moved, out)
    return out


def tap_rows(fraction):
    square = fraction * fraction
    cube = square * fraction
    remain = 1.0 - fraction
    return (
        remain * remain * remain / 6.0,
        (3.0 * cube - 6.0 * square + 4.0) / 6.0,
        (-3.0 * cube + 3.0 * square + 3.0 * fraction + 1.0) / 6.0,
        cube / 6.0,
    )


def pick_taps(offset, taps):
    out = jnp.zeros(offset.shape, jnp.float32)
    for t in range(4):
        out = jnp.where(offset == t, taps[t], out)
    return out


def ewald_kernel(
    atoms_ref,
    bz_ref,
    by_ref,
    bx_ref,
    gx_ref,
    gy_ref,
    gz_ref,
    out_ref,
    rx_atoms,
    z_high,
    z_low,
    stencil,
    tx_b,
    rx_b,
    tx_c,
    rx_c,
    tx_c2,
    rx_c2,
    tx_b2,
    rx_b2,
    parts,
    rx_parts,
    sa,
    ra,
    sb,
    rb,
    sc,
    rc,
    sc2,
    rc2,
    sb2,
    rb2,
    sp,
    rp,
):
    f32 = jnp.float32
    MESH = pl.DeviceIdType.MESH
    ix, iy, iz = lax.axis_index("gx"), lax.axis_index("gy"), lax.axis_index("gz")
    me = iy * 4 + iz
    barrier = pltpu.get_barrier_semaphore()

    def yz_peer(r):
        other = lax.rem(me + r, 16)
        return other, (ix, other // 4, lax.rem(other, 4))

    def x_peer(r):
        other = lax.rem(ix + r, 8)
        return other, (other, iy, iz)

    def greet_yz(r, c):
        pl.semaphore_signal(barrier, inc=1, device_id=yz_peer(r)[1], device_id_type=MESH)
        return c

    def greet_x(r, c):
        pl.semaphore_signal(barrier, inc=1, device_id=x_peer(r)[1], device_id_type=MESH)
        return c

    lax.fori_loop(1, 16, greet_yz, 0)
    lax.fori_loop(1, 8, greet_x, 0)
    pl.semaphore_wait(barrier, 22)

    routes = [(0, 3, 3, 1), (0, 0, 0, 1), (0, 1, 0, 0), (0, 2, 0, 0)]
    routes += [(1, 1, 0, 1), (1, 2, 0, 1), (1, 3, 0, 0), (1, 0, 1, 0)]

    def atom_copy(half, to_z, step_y, place):
        return pltpu.make_async_remote_copy(
            src_ref=atoms_ref.at[half],
            dst_ref=rx_atoms.at[iz, place],
            send_sem=sa.at[half, to_z],
            recv_sem=ra.at[iz, place],
            device_id=(ix, lax.rem(iy + step_y, 4), to_z),
            device_id_type=MESH,
        )

    for half, to_z, step_y, place in routes:
        if step_y:
            atom_copy(half, to_z, step_y, place).start()
        else:

            @pl.when(iz != to_z)
            def _():
                atom_copy(half, to_z, step_y, place).start()

            @pl.when(iz == to_z)
            def _():
                rx_atoms[iz, place] = atoms_ref[half]

    from_y = [
        lax.rem(iy + jnp.where(iz == 0, 3, 0), 4),
        lax.rem(iy + jnp.where(iz == 3, 1, 0), 4),
    ]
    edge = jnp.where((iz == 0) | (iz == 3), 1, 0)
    from_half = [edge, 1 - edge]

    def atom_wait(s, u):
        @pl.when((s != iz) | (from_y[u] != iy))
        def _():
            pltpu.make_async_remote_copy(
                src_ref=atoms_ref.at[0],
                dst_ref=rx_atoms.at[s, u],
                send_sem=sa.at[0, 0],
                recv_sem=ra.at[s, u],
                device_id=(ix, from_y[u], s),
                device_id_type=MESH,
            ).wait_recv()

    for s in range(4):
        for u in range(2):
            atom_wait(s, u)

    z_ids = lax.broadcasted_iota(jnp.int32, (256, 256), 0)
    x_ids = lax.broadcasted_iota(jnp.int32, (32, 256), 0) + (ix * 24 - 1)
    y_first = iy * 16 + iz * 4

    def spread(slot, total):
        rows = rx_atoms[slot // 2, lax.rem(slot, 2)]
        anchor = rows[3:6].astype(jnp.int32)
        weights_z = pick_taps((z_ids - anchor[2:3]) & 255, tap_rows(rows[2:3]))
        high, low = split(weights_z)
        at = pl.ds(pl.multiple_of(slot * 256, 256), 256)
        z_high[:, at] = high
        z_low[:, at] = low
        weights_x = pick_taps(x_ids - anchor[0:1], tap_rows(rows[0:1]))
        taps_y = tap_rows(rows[1:2])
        blocks = [
            weights_x * pick_taps((y_first + i - anchor[1:2]) & 63, taps_y) for i in range(4)
        ]
        both = jnp.concatenate(blocks, axis=0)
        stencil[:, at] = both
        return total + dot3((high, low), split(both * rows[6:7]), NT)

    lines = lax.fori_loop(0, 8, spread, jnp.zeros((256, 128), f32))
    spectrum = dot3((bz_ref[0], bz_ref[1]), split(lines))
    tx_b[...] = spectrum.reshape(16, 16, 128)
    rx_b[me] = tx_b[me]

    def exchange(tx, rx, send, recv, peer, count, mine):
        def copy(r):
            other, where = peer(r)
            return pltpu.make_async_remote_copy(
                src_ref=tx.at[other],
                dst_ref=rx.at[mine],
                send_sem=send.at[other],
                recv_sem=recv.at[mine],
                device_id=where,
                device_id_type=MESH,
            )

        def arrival(r):
            other, where = peer(r)
            return pltpu.make_async_remote_copy(
                src_ref=tx.at[other],
                dst_ref=rx.at[other],
                send_sem=send.at[other],
                recv_sem=recv.at[other],
                device_id=where,
                device_id_type=MESH,
            )

        def start(r, c):
            copy(r).start()
            return c

        def wait(r, c):
            arrival(r).wait_recv()
            return c

        def drain(r, c):
            copy(r).wait_send()
            return c

        lax.fori_loop(1, count, start, 0)
        return (
            lambda: lax.fori_loop(1, count, wait, 0),
            lambda: lax.fori_loop(1, count, drain, 0),
        )

    arrive_b, drain_b = exchange(tx_b, rx_b, sb, rb, yz_peer, 16, me)
    arrive_b()
    flat_b = rx_b.reshape(256, 128)
    columns = []
    for group in range(4):
        pieces = [flat_b[pl.ds(group * 4 + k, 16, 16), :] for k in range(4)]
        columns.append(jnp.concatenate([swap_groups(pieces, i) for i in range(4)], axis=0))
    lines_y = jnp.concatenate(columns, axis=1)
    modes_y = dot3((by_ref[0, 0], by_ref[0, 1]), split(lines_y))
    tx_c[...] = modes_y.reshape(8, 8, 512)
    rx_c[ix] = tx_c[ix]
    arrive_c, drain_c = exchange(tx_c, rx_c, sc, rc, x_peer, 8, ix)

    gain_z = gz_ref[0, pl.ds(pl.multiple_of(me * 16, 16), 16), :]
    square_z = gz_ref[1, pl.ds(pl.multiple_of(me * 16, 16), 16), :]
    gain_y = gy_ref[0, pl.ds(pl.multiple_of(ix * 8, 8), 8), :]
    square_y = gy_ref[1, pl.ds(pl.multiple_of(ix * 8, 8), 8), :]
    gain_yz = (gain_z[:, None, :] * gain_y[None, :, :]).reshape(128, 128)
    square_yz = (square_z[:, None, :] + square_y[None, :, :]).reshape(128, 128)
    greens = []
    for h in range(2):
        lanes = slice(128 * h, 128 * h + 128)
        total = square_yz + gx_ref[1, 0:1, lanes]
        value = gain_yz * gx_ref[0, 0:1, lanes] / (total + 1.0 / 1024.0)
        greens.append(jnp.where(total == 0.0, 0.0, value))
    green = jnp.concatenate(greens, axis=1)

    arrive_c()
    rows_x = []
    for group in range(4):
        for k in range(4):
            halves = [
                swap_groups(
                    [rx_c[4 * h + g, :, group * 128 : group * 128 + 128] for g in range(4)], k
                )
                for h in range(2)
            ]
            rows_x.append(jnp.concatenate(halves, axis=1))
    lines_x = jnp.concatenate(rows_x, axis=0)
    basis_x = (bx_ref[0], bx_ref[1])
    filtered = dot3(split(lines_x), basis_x, NT) * green
    back_x = dot3(split(filtered), basis_x)
    for g in range(8):
        half = g // 4
        for group in range(4):
            pieces = [
                back_x[(group * 4 + k) * 8 : (group * 4 + k) * 8 + 8, half * 128 : half * 128 + 128]
                for k in range(4)
            ]
            tx_c2[g, :, group * 128 : group * 128 + 128] = swap_groups(pieces, g % 4)
    rx_c2[ix] = tx_c2[ix]
    arrive_c2, drain_c2 = exchange(tx_c2, rx_c2, sc2, rc2, x_peer, 8, ix)
    arrive_c2()
    back_y = dot3((by_ref[1, 0], by_ref[1, 1]), split(rx_c2[...].reshape(64, 512)))
    flat_b2 = tx_b2.reshape(256, 128)
    for group in range(4):
        pieces = [back_y[16 * i : 16 * i + 16, group * 128 : group * 128 + 128] for i in range(4)]
        for k in range(4):
            flat_b2[pl.ds(group * 4 + k, 16, 16), :] = swap_groups(pieces, k)
    rx_b2[me] = tx_b2[me]
    arrive_b2, drain_b2 = exchange(tx_b2, rx_b2, sb2, rb2, yz_peer, 16, me)
    arrive_b2()
    back_z = rx_b2[...].reshape(256, 128).T
    potential = split(dot3(split(back_z), (bz_ref[0], bz_ref[1])))

    def sample(slot, c):
        at = pl.ds(pl.multiple_of(slot * 256, 256), 256)
        values = dot3(potential, (z_high[:, at], z_low[:, at]))
        parts[slot] = jnp.sum(values * stencil[:, at], axis=0, keepdims=True)
        return c

    lax.fori_loop(0, 8, sample, 0)

    def part_copy(s, u):
        return pltpu.make_async_remote_copy(
            src_ref=parts.at[2 * s + u],
            dst_ref=rx_parts.at[from_half[u], iz],
            send_sem=sp.at[s, u],
            recv_sem=rp.at[from_half[u], iz],
            device_id=(ix, from_y[u], s),
            device_id_type=MESH,
        )

    for s in range(4):
        for u in range(2):

            @pl.when((s != iz) | (from_y[u] != iy))
            def _():
                part_copy(s, u).start()

            @pl.when((s == iz) & (from_y[u] == iy))
            def _():
                rx_parts[from_half[u], iz] = parts[2 * s + u]

    def part_wait(half, to_z, step_y):
        pltpu.make_async_remote_copy(
            src_ref=parts.at[0],
            dst_ref=rx_parts.at[half, to_z],
            send_sem=sp.at[0, 0],
            recv_sem=rp.at[half, to_z],
            device_id=(ix, lax.rem(iy + step_y, 4), to_z),
            device_id_type=MESH,
        ).wait_recv()

    for half, to_z, step_y, place in routes:
        if step_y:
            part_wait(half, to_z, step_y)
        else:

            @pl.when(iz != to_z)
            def _():
                part_wait(half, to_z, step_y)

    for half in range(2):
        out_ref[half] = (
            (rx_parts[half, 0] + rx_parts[half, 1]) + (rx_parts[half, 2] + rx_parts[half, 3])
        )

    for half, to_z, step_y, place in routes:
        if step_y:
            atom_copy(half, to_z, step_y, place).wait_send()
        else:

            @pl.when(iz != to_z)
            def _():
                atom_copy(half, to_z, step_y, place).wait_send()

    drain_b()
    drain_c()
    drain_c2()
    drain_b2()
    for s in range(4):
        for u in range(2):

            @pl.when((s != iz) | (from_y[u] != iy))
            def _():
                part_copy(s, u).wait_send()


def ewald(atoms):
    f32, bf16 = jnp.float32, jnp.bfloat16
    vm = pl.BlockSpec(memory_space=pltpu.VMEM)
    dma = pltpu.SemaphoreType.DMA
    tables = [jnp.asarray(t) for t in ewald_tables()]
    return pl.pallas_call(
        ewald_kernel,
        out_shape=jax.ShapeDtypeStruct((2, 1, 256), f32),
        in_specs=[vm] * 7,
        out_specs=vm,
        scratch_shapes=[
            pltpu.VMEM((4, 2, 8, 256), f32),
            pltpu.VMEM((256, 2048), bf16),
            pltpu.VMEM((256, 2048), bf16),
            pltpu.VMEM((128, 2048), f32),
            pltpu.VMEM((16, 16, 128), f32),
            pltpu.VMEM((16, 16, 128), f32),
            pltpu.VMEM((8, 8, 512), f32),
            pltpu.VMEM((8, 8, 512), f32),
            pltpu.VMEM((8, 8, 512), f32),
            pltpu.VMEM((8, 8, 512), f32),
            pltpu.VMEM((16, 16, 128), f32),
            pltpu.VMEM((16, 16, 128), f32),
            pltpu.VMEM((8, 1, 256), f32),
            pltpu.VMEM((2, 4, 1, 256), f32),
            dma((2, 4)),
            dma((4, 2)),
            dma((16,)),
            dma((16,)),
            dma((8,)),
            dma((8,)),
            dma((8,)),
            dma((8,)),
            dma((16,)),
            dma((16,)),
            dma((4, 2)),
            dma((2, 4)),
        ],
        compiler_params=pltpu.CompilerParams(
            collective_id=0, has_side_effects=True, vmem_limit_bytes=40 * 1024 * 1024
        ),
        name="ewald",
    )(atoms, *tables)


def shards(
    features,
    positions,
    grid_anchor,
    species,
    neighbours,
    neighbour_count,
    w_self,
    w_neighbour,
    w_radial,
    radial_rates,
    w_pair1,
    w_pair2,
    w_vector,
    w_out,
    w_charge,
    species_charge,
):
    cells_x, cells_y, cells_z, slot_count, channels = features.shape
    atom_count = cells_x * cells_y * cells_z * slot_count
    hidden_rows = features.reshape(atom_count, channels)
    species_rows = species.reshape(atom_count)
    kind_ids = jnp.arange(species_charge.shape[0], dtype=jnp.int32)
    base_charge = jnp.sum(
        jnp.where(species_rows[:, None] == kind_ids[None, :], species_charge[None, :], 0.0), axis=1
    )
    charge = base_charge + jnp.dot(hidden_rows, w_charge, preferred_element_type=jnp.float32)
    feat_ext = padded_2(features, (("gx", 0), ("gy", 1), ("gz", 2)), 1)
    rim_ext = padded_2(positions, (("gx", 0), ("gy", 1), ("gz", 2)), 1)

    def by_half(values, width):
        grouped = values.reshape(cells_x, cells_y, cells_z, width, slot_count)
        return grouped.transpose(1, 3, 0, 2, 4).reshape(cells_y, width, -1)

    place = by_half(positions, 3)
    anchor = by_half(grid_anchor, 3).astype(jnp.float32)
    atoms = jnp.concatenate(
        [place - (anchor + 1.0), anchor, by_half(charge, 1), jnp.zeros((2, 1, 192), jnp.float32)],
        axis=1,
    )
    site = ewald(jnp.pad(atoms, ((0, 0), (0, 0), (0, 64))))
    site_potential = site[:, 0, :192].reshape(cells_y, cells_x, cells_z, slot_count)
    site_potential = site_potential.transpose(1, 0, 2, 3)
    strips = rim_ext.reshape(cells_x + 2, cells_y + 2, cells_z + 2, 3, slot_count)
    strips = jnp.moveaxis(strips, 3, 2).reshape(cells_x + 2, cells_y + 2, 3, 80)
    strips = jnp.pad(strips, ((0, 0), (0, 0), (0, 1), (0, 48)))
    columns = []
    for cx in range(cells_x):
        for cy in range(cells_y):
            near = strips[cx : cx + 3, cy : cy + 3].reshape(9, 4, 128)
            columns.append(jnp.concatenate([near, near[4:5], near[4:5], near[4:5]]))
    pos_tab = jnp.stack(columns).reshape(6, 48, 128)
    counts = jnp.pad(neighbour_count.reshape(6, 8, 8), ((0, 0), (0, 0), (0, 120)))
    updated = pair_update(
        feat_ext.reshape(-1, channels),
        pos_tab,
        neighbours.reshape(6, 8, 512),
        counts,
        w_neighbour,
        w_self,
        w_radial,
        radial_rates.reshape(8, 1),
        w_pair1,
        w_pair2,
        w_vector,
        w_out,
        hidden_rows,
    )
    features_out = updated.reshape(cells_x, cells_y, cells_z, slot_count, channels)
    return (features_out, site_potential)


def solution(mesh):
    return jax.shard_map(
        shards,
        mesh=mesh,
        in_specs=(
            P("gx", "gy", "gz", None, None),
            P("gx", "gy", "gz", None),
            P("gx", "gy", "gz", None),
            P("gx", "gy", "gz", None),
            P("gx", "gy", "gz", None),
            P("gx", "gy", "gz", None),
            P(),
            P(),
            P(),
            P(),
            P(),
            P(),
            P(),
            P(),
            P(),
            P(),
        ),
        out_specs=(P("gx", "gy", "gz", None, None), P("gx", "gy", "gz", None)),
        check_vma=False,
    )
```

profile of v0, /device:TPU:1, one launch (start us, length us, event | category | flops | bytes accessed | tf_op | source)
XLA Modules:
  0.0 116.1 jit_solution(816889176954271474)
XLA Ops:
  0.6 0.7 fusion.6
  1.4 2.0 %collective-permute-start.6 = (f32[1,2,8,24]{3,2,1,0:T(8,128)S(1)}, f32[1,2,8,24]{3,2,1,0:T(8,128)S(1)}, u32[]{:S(2)}, u32[]{:S(2)}) collective-permute-start(f32[1,2,8,24]{3,2,1,0:T(8,128)S(1)} %get-tuple-element.19), channel_id=1, source_target_pairs={{0,16},{16,32},{32,48},{48,64},{64,80},{80,96},{96,112},{112,0},{1... | collective-permute-start | bytes 4616 | tf_op jit(solution)/shard_map/ppermute | solution.py:22
  3.4 2.5 %collective-permute-start.7 = (f32[1,2,8,24]{3,2,1,0:T(8,128)S(1)}, f32[1,2,8,24]{3,2,1,0:T(8,128)S(1)}, u32[]{:S(2)}, u32[]{:S(2)}) collective-permute-start(f32[1,2,8,24]{3,2,1,0:T(8,128)S(1)} %get-tuple-element.18), channel_id=1, source_target_pairs={{16,0},{32,16},{48,32},{64,48},{80,64},{96,80},{112,96},{0,112},{1... | collective-permute-start | bytes 4616 | tf_op jit(solution)/shard_map/ppermute | solution.py:25
  5.9 0.8 fusion.4
  6.7 3.6 %collective-permute-start.1 = (bf16[1,2,8,8,128]{4,3,2,1,0:T(8,128)(2,1)S(1)}, bf16[1,2,8,8,128]{4,3,2,1,0:T(8,128)(2,1)S(1)}, u32[]{:S(2)}, u32[]{:S(2)}) collective-permute-start(bf16[1,2,8,8,128]{4,3,2,1,0:T(8,128)(2,1)S(1)} %get-tuple-element.8), channel_id=1, source_target_pairs={{16,0},{32,16},{48,32},{64,48},{80,64},{96,80},{112,96},{0,112},{1... | collective-permute-start | bytes 98312 | tf_op jit(solution)/shard_map/ppermute | solution.py:25
  10.3 0.1 reshape.91
  10.4 0.1 convert_element_type.17
  10.8 0.6 copy-done.19
  11.6 0.2 convolution_reduce_fusion
  12.2 4.3 %collective-permute-start.8 = (f32[5,1,8,24]{3,2,1,0:T(8,128)S(1)}, f32[5,1,8,24]{3,2,1,0:T(8,128)S(1)}, u32[]{:S(2)}, u32[]{:S(2)}) collective-permute-start(f32[5,1,8,24]{3,2,1,0:T(8,128)S(1)} %get-tuple-element.10), channel_id=1, source_target_pairs={{0,4},{4,8},{8,12},{12,0},{1,5},{5,9},{9,13},{13,1},{2,6},{6,10},{... | collective-permute-start | bytes 11528 | tf_op jit(solution)/shard_map/ppermute | solution.py:22
  16.6 0.7 copy-done.14
  17.3 40.9 %ewald.1 = f32[2,1,256]{2,1,0:T(1,128)S(1)} custom-call(f32[2,8,256]{2,1,0:T(8,128)S(1)} %pad.14.atoms_ref, bf16[2,256,256]{2,1,0:T(8,128)(2,1)S(1)} %copy-done.2, bf16[2,2,64,64]{3,2,1,0:T(8,128)(2,1)S(1)} %copy-done.6, bf16[2,256,256]{2,1,0:T(8,128)(2,1)S(1)} %copy-done.3, f32[2,8,256]{2,1,0:T(8,128)S(1)} %copy-done.14, f32[2,64,128]{2,1,0:T(8,128)S(1)} %copy-done.7, ...), custom_call_target="tpu_custom_call" | custom-call | tf_op jit(solution)/shard_map/ewald/pallas_call | solution.py:650
  58.2 0.1 copy.77
  58.4 0.1 fusion.2
  58.5 1.3 %collective-permute-start.10 = (f32[5,4,1,24]{2,3,1,0:T(8,128)S(1)}, f32[5,4,1,24]{2,3,1,0:T(8,128)S(1)}, u32[]{:S(2)}, u32[]{:S(2)}) collective-permute-start(f32[5,4,1,24]{2,3,1,0:T(8,128)S(1)} %get-tuple-element.4), channel_id=1, source_target_pairs={{0,1},{1,2},{2,3},{3,0},{4,5},{5,6},{6,7},{7,4},{8,9},{9,10},{10,1... | collective-permute-start | bytes 5768 | tf_op jit(solution)/shard_map/ppermute | solution.py:22
  59.8 1.5 %collective-permute-start.11 = (f32[5,4,1,24]{2,3,1,0:T(8,128)S(1)}, f32[5,4,1,24]{2,3,1,0:T(8,128)S(1)}, u32[]{:S(2)}, u32[]{:S(2)}) collective-permute-start(f32[5,4,1,24]{2,3,1,0:T(8,128)S(1)} %get-tuple-element.5), channel_id=1, source_target_pairs={{1,0},{2,1},{3,2},{0,3},{5,4},{6,5},{7,6},{4,7},{9,8},{10,9},{11,1... | collective-permute-start | bytes 5768 | tf_op jit(solution)/shard_map/ppermute | solution.py:25
  61.3 0.6 copy-done.21
  62.1 0.6 copy.100
  62.7 0.1 copy-done.18
  62.8 3.3 %collective-permute-done.10 = f32[5,4,1,24]{2,3,1,0:T(8,128)S(1)} collective-permute-done((f32[5,4,1,24]{2,3,1,0:T(8,128)S(1)}, f32[5,4,1,24]{2,3,1,0:T(8,128)S(1)}, u32[]{:S(2)}, u32[]{:S(2)}) %collective-permute-start.10) | collective-permute-done | bytes 1952 | tf_op jit(solution)/shard_map/ppermute | solution.py:22
  66.1 0.3 collective-permute-done.11
  66.5 0.2 maximum_bitcast_fusion
  66.7 0.4 copy.80
  67.1 0.2 reshape.79
  67.7 3.2 %collective-permute-start.2 = (bf16[5,1,8,8,128]{4,3,2,1,0:T(8,128)(2,1)S(1)}, bf16[5,1,8,8,128]{4,3,2,1,0:T(8,128)(2,1)S(1)}, u32[]{:S(2)}, u32[]{:S(2)}) collective-permute-start(bf16[5,1,8,8,128]{4,3,2,1,0:T(8,128)(2,1)S(1)} %get-tuple-element.6), channel_id=1, source_target_pairs={{0,4},{4,8},{8,12},{12,0},{1,5},{5,9},{9,13},{13,1},{2,6},{6,10},{... | collective-permute-start | bytes 245768 | tf_op jit(solution)/shard_map/ppermute | solution.py:22
  70.9 1.5 %collective-permute-done.2 = bf16[5,1,8,8,128]{4,3,2,1,0:T(8,128)(2,1)S(1)} collective-permute-done((bf16[5,1,8,8,128]{4,3,2,1,0:T(8,128)(2,1)S(1)}, bf16[5,1,8,8,128]{4,3,2,1,0:T(8,128)(2,1)S(1)}, u32[]{:S(2)}, u32[]{:S(2)}) %collective-permute-start.2) | collective-permute-done | bytes 81952 | tf_op jit(solution)/shard_map/ppermute | solution.py:22
  72.4 3.9 %collective-permute-done.3 = bf16[5,1,8,8,128]{4,3,2,1,0:T(8,128)(2,1)S(1)} collective-permute-done((bf16[5,1,8,8,128]{4,3,2,1,0:T(8,128)(2,1)S(1)}, bf16[5,1,8,8,128]{4,3,2,1,0:T(8,128)(2,1)S(1)}, u32[]{:S(2)}, u32[]{:S(2)}) %collective-permute-start.3) | collective-permute-done | bytes 81952 | tf_op jit(solution)/shard_map/ppermute | solution.py:25
  76.3 0.4 collective-permute-start.4
  76.7 2.5 %collective-permute-start.5 = (bf16[5,4,1,8,128]{4,3,2,1,0:T(8,128)(2,1)S(1)}, bf16[5,4,1,8,128]{4,3,2,1,0:T(8,128)(2,1)S(1)}, u32[]{:S(2)}, u32[]{:S(2)}) collective-permute-start(bf16[5,4,1,8,128]{4,3,2,1,0:T(8,128)(2,1)S(1)} %get-tuple-element.3), channel_id=1, source_target_pairs={{1,0},{2,1},{3,2},{0,3},{5,4},{6,5},{7,6},{4,7},{9,8},{10,9},{11,1... | collective-permute-start | bytes 122888 | tf_op jit(solution)/shard_map/ppermute | solution.py:25
  79.2 1.2 %collective-permute-done.4 = bf16[5,4,1,8,128]{4,3,2,1,0:T(8,128)(2,1)S(1)} collective-permute-done((bf16[5,4,1,8,128]{4,3,2,1,0:T(8,128)(2,1)S(1)}, bf16[5,4,1,8,128]{4,3,2,1,0:T(8,128)(2,1)S(1)}, u32[]{:S(2)}, u32[]{:S(2)}) %collective-permute-start.4) | collective-permute-done | bytes 40992 | tf_op jit(solution)/shard_map/ppermute | solution.py:22
  80.6 0.6 copy-done.15
  81.2 34.9 %pair_update.1 = bf16[384,128]{1,0:T(8,128)(2,1)} custom-call(bf16[1600,128]{1,0:T(8,128)(2,1)S(1)} %bitcast.61, f32[6,48,128]{2,1,0:T(8,128)S(1)} %constant_dynamic-update-slice_fusion.6.pos_ref, s32[6,8,512]{2,1,0:T(8,128)S(1)} %bitcast.64, s32[6,8,128]{2,1,0:T(8,128)S(1)} %pad.13.count_ref, bf16[128,128]{1,0:T(8,128)(2,1)S(1)} %copy-done.8, ...), custom_call_target="tpu_custom_call" | custom-call | tf_op jit(solution)/shard_map/pair_update/pallas_call | solution.py:218
  (104 shorter events, 1.4 us)
Async XLA Ops:
  0.6 10.9 %copy-start = (bf16[128]{0:T(256)(128)(2,1)S(1)}, bf16[128]{0:T(256)(128)(2,1)}, u32[]{:S(2)}) copy-start(bf16[128]{0:T(256)(128)(2,1)} %param.36) | copy-start | bytes 772
  1.4 10.7 %collective-permute-start.6 = (f32[1,2,8,24]{3,2,1,0:T(8,128)S(1)}, f32[1,2,8,24]{3,2,1,0:T(8,128)S(1)}, u32[]{:S(2)}, u32[]{:S(2)}) collective-permute-start(f32[1,2,8,24]{3,2,1,0:T(8,128)S(1)} %get-tuple-element.19), channel_id=1, source_target_pairs={{0,16},{16,32},{32,48},{48,64},{64,80},{80,96},{96,112},{112,0},{1... | collective-permute-start | bytes 4616 | tf_op jit(solution)/shard_map/ppermute | solution.py:22
  3.4 6.9 %copy-start.16 = (f32[3,2,8,24]{3,2,1,0:T(8,128)S(1)}, f32[3,2,8,24]{3,2,1,0:T(8,128)}, u32[]{:S(2)}) copy-start(f32[3,2,8,24]{3,2,1,0:T(8,128)} %param.23) | copy-start | bytes 13828
  3.4 8.7 %collective-permute-start.7 = (f32[1,2,8,24]{3,2,1,0:T(8,128)S(1)}, f32[1,2,8,24]{3,2,1,0:T(8,128)S(1)}, u32[]{:S(2)}, u32[]{:S(2)}) collective-permute-start(f32[1,2,8,24]{3,2,1,0:T(8,128)S(1)} %get-tuple-element.18), channel_id=1, source_target_pairs={{16,0},{32,16},{48,32},{64,48},{80,64},{96,80},{112,96},{0,112},{1... | collective-permute-start | bytes 4616 | tf_op jit(solution)/shard_map/ppermute | solution.py:25
  6.7 61.0 %collective-permute-start = (bf16[1,2,8,8,128]{4,3,2,1,0:T(8,128)(2,1)S(1)}, bf16[1,2,8,8,128]{4,3,2,1,0:T(8,128)(2,1)S(1)}, u32[]{:S(2)}, u32[]{:S(2)}) collective-permute-start(bf16[1,2,8,8,128]{4,3,2,1,0:T(8,128)(2,1)S(1)} %get-tuple-element.9), channel_id=1, source_target_pairs={{0,16},{16,32},{32,48},{48,64},{64,80},{80,96},{96,112},{112,0},{1... | collective-permute-start | bytes 98312 | tf_op jit(solution)/shard_map/ppermute | solution.py:22
  6.7 3.7 %copy-start.17 = (s32[3,2,8,24]{3,2,1,0:T(8,128)S(1)}, s32[3,2,8,24]{3,2,1,0:T(8,128)}, u32[]{:S(2)}) copy-start(s32[3,2,8,24]{3,2,1,0:T(8,128)} %param.24) | copy-start | bytes 13828
  6.7 61.0 %collective-permute-start.1 = (bf16[1,2,8,8,128]{4,3,2,1,0:T(8,128)(2,1)S(1)}, bf16[1,2,8,8,128]{4,3,2,1,0:T(8,128)(2,1)S(1)}, u32[]{:S(2)}, u32[]{:S(2)}) collective-permute-start(bf16[1,2,8,8,128]{4,3,2,1,0:T(8,128)(2,1)S(1)} %get-tuple-element.8), channel_id=1, source_target_pairs={{16,0},{32,16},{48,32},{64,48},{80,64},{96,80},{112,96},{0,112},{1... | collective-permute-start | bytes 98312 | tf_op jit(solution)/shard_map/ppermute | solution.py:25
  10.4 6.2 %copy-start.4 = (f32[2,256,128]{2,1,0:T(8,128)S(1)}, f32[2,256,128]{2,1,0:T(8,128)}, u32[]{:S(2)}) copy-start(f32[2,256,128]{2,1,0:T(8,128)} %constant.25.clone.gz_ref) | copy-start | bytes 786436
  10.5 6.1 %copy-start.3 = (bf16[2,256,256]{2,1,0:T(8,128)(2,1)S(1)}, bf16[2,256,256]{2,1,0:T(8,128)(2,1)}, u32[]{:S(2)}) copy-start(bf16[2,256,256]{2,1,0:T(8,128)(2,1)} %constant.22.clone.bx_ref) | copy-start | bytes 786436
  10.6 0.7 copy-start.19
  10.7 0.9 copy-start.1
  10.7 1.1 copy-start.20
  11.4 5.2 %copy-start.2 = (bf16[2,256,256]{2,1,0:T(8,128)(2,1)S(1)}, bf16[2,256,256]{2,1,0:T(8,128)(2,1)}, u32[]{:S(2)}) copy-start(bf16[2,256,256]{2,1,0:T(8,128)(2,1)} %constant.20.clone.bz_ref) | copy-start | bytes 786436
  12.1 4.5 %copy-start.6 = (bf16[2,2,64,64]{3,2,1,0:T(8,128)(2,1)S(1)}, bf16[2,2,64,64]{3,2,1,0:T(8,128)(2,1)}, u32[]{:S(2)}) copy-start(bf16[2,2,64,64]{3,2,1,0:T(8,128)(2,1)} %constant.21.clone.by_ref) | copy-start | bytes 98308
  12.1 4.5 %copy-start.7 = (f32[2,64,128]{2,1,0:T(8,128)S(1)}, f32[2,64,128]{2,1,0:T(8,128)}, u32[]{:S(2)}) copy-start(f32[2,64,128]{2,1,0:T(8,128)} %constant.24.clone.gy_ref) | copy-start | bytes 196612
  12.2 46.0 %collective-permute-start.8 = (f32[5,1,8,24]{3,2,1,0:T(8,128)S(1)}, f32[5,1,8,24]{3,2,1,0:T(8,128)S(1)}, u32[]{:S(2)}, u32[]{:S(2)}) collective-permute-start(f32[5,1,8,24]{3,2,1,0:T(8,128)S(1)} %get-tuple-element.10), channel_id=1, source_target_pairs={{0,4},{4,8},{8,12},{12,0},{1,5},{5,9},{9,13},{13,1},{2,6},{6,10},{... | collective-permute-start | bytes 11528 | tf_op jit(solution)/shard_map/ppermute | solution.py:22
  16.5 41.7 %collective-permute-start.9 = (f32[5,1,8,24]{3,2,1,0:T(8,128)S(1)}, f32[5,1,8,24]{3,2,1,0:T(8,128)S(1)}, u32[]{:S(2)}, u32[]{:S(2)}) collective-permute-start(f32[5,1,8,24]{3,2,1,0:T(8,128)S(1)} %get-tuple-element.11), channel_id=1, source_target_pairs={{4,0},{8,4},{12,8},{0,12},{5,1},{9,5},{13,9},{1,13},{6,2},{10,6},{... | collective-permute-start | bytes 11528 | tf_op jit(solution)/shard_map/ppermute | solution.py:25
  16.6 0.7 copy-start.14
  58.5 7.7 %collective-permute-start.10 = (f32[5,4,1,24]{2,3,1,0:T(8,128)S(1)}, f32[5,4,1,24]{2,3,1,0:T(8,128)S(1)}, u32[]{:S(2)}, u32[]{:S(2)}) collective-permute-start(f32[5,4,1,24]{2,3,1,0:T(8,128)S(1)} %get-tuple-element.4), channel_id=1, source_target_pairs={{0,1},{1,2},{2,3},{3,0},{4,5},{5,6},{6,7},{7,4},{8,9},{9,10},{10,1... | collective-permute-start | bytes 5768 | tf_op jit(solution)/shard_map/ppermute | solution.py:22
  59.8 6.7 %collective-permute-start.11 = (f32[5,4,1,24]{2,3,1,0:T(8,128)S(1)}, f32[5,4,1,24]{2,3,1,0:T(8,128)S(1)}, u32[]{:S(2)}, u32[]{:S(2)}) collective-permute-start(f32[5,4,1,24]{2,3,1,0:T(8,128)S(1)} %get-tuple-element.5), channel_id=1, source_target_pairs={{1,0},{2,1},{3,2},{0,3},{5,4},{6,5},{7,6},{4,7},{9,8},{10,9},{11,1... | collective-permute-start | bytes 5768 | tf_op jit(solution)/shard_map/ppermute | solution.py:25
  62.1 0.7 copy-start.18
  67.7 4.7 %collective-permute-start.2 = (bf16[5,1,8,8,128]{4,3,2,1,0:T(8,128)(2,1)S(1)}, bf16[5,1,8,8,128]{4,3,2,1,0:T(8,128)(2,1)S(1)}, u32[]{:S(2)}, u32[]{:S(2)}) collective-permute-start(bf16[5,1,8,8,128]{4,3,2,1,0:T(8,128)(2,1)S(1)} %get-tuple-element.6), channel_id=1, source_target_pairs={{0,4},{4,8},{8,12},{12,0},{1,5},{5,9},{9,13},{13,1},{2,6},{6,10},{... | collective-permute-start | bytes 245768 | tf_op jit(solution)/shard_map/ppermute | solution.py:22
  70.9 5.4 %collective-permute-start.3 = (bf16[5,1,8,8,128]{4,3,2,1,0:T(8,128)(2,1)S(1)}, bf16[5,1,8,8,128]{4,3,2,1,0:T(8,128)(2,1)S(1)}, u32[]{:S(2)}, u32[]{:S(2)}) collective-permute-start(bf16[5,1,8,8,128]{4,3,2,1,0:T(8,128)(2,1)S(1)} %get-tuple-element.7), channel_id=1, source_target_pairs={{4,0},{8,4},{12,8},{0,12},{5,1},{9,5},{13,9},{1,13},{6,2},{10,6},{... | collective-permute-start | bytes 245768 | tf_op jit(solution)/shard_map/ppermute | solution.py:25
  76.3 4.1 %collective-permute-start.4 = (bf16[5,4,1,8,128]{4,3,2,1,0:T(8,128)(2,1)S(1)}, bf16[5,4,1,8,128]{4,3,2,1,0:T(8,128)(2,1)S(1)}, u32[]{:S(2)}, u32[]{:S(2)}) collective-permute-start(bf16[5,4,1,8,128]{4,3,2,1,0:T(8,128)(2,1)S(1)} %get-tuple-element.2), channel_id=1, source_target_pairs={{0,1},{1,2},{2,3},{3,0},{4,5},{5,6},{6,7},{7,4},{8,9},{9,10},{10,1... | collective-permute-start | bytes 122888 | tf_op jit(solution)/shard_map/ppermute | solution.py:22
  76.7 3.8 %collective-permute-start.5 = (bf16[5,4,1,8,128]{4,3,2,1,0:T(8,128)(2,1)S(1)}, bf16[5,4,1,8,128]{4,3,2,1,0:T(8,128)(2,1)S(1)}, u32[]{:S(2)}, u32[]{:S(2)}) collective-permute-start(bf16[5,4,1,8,128]{4,3,2,1,0:T(8,128)(2,1)S(1)} %get-tuple-element.3), channel_id=1, source_target_pairs={{1,0},{2,1},{3,2},{0,3},{5,4},{6,5},{7,6},{4,7},{9,8},{10,9},{11,1... | collective-permute-start | bytes 122888 | tf_op jit(solution)/shard_map/ppermute | solution.py:25
  79.2 1.4 %copy-start.5 = (s32[3,2,8,512]{3,2,1,0:T(8,128)S(1)}, s32[3,2,8,512]{3,2,1,0:T(8,128)}, u32[]{:S(2)}) copy-start(s32[3,2,8,512]{3,2,1,0:T(8,128)} %param.26) | copy-start | bytes 294916
  79.2 1.4 %copy-start.8 = (bf16[128,128]{1,0:T(8,128)(2,1)S(1)}, bf16[128,128]{1,0:T(8,128)(2,1)}, u32[]{:S(2)}) copy-start(bf16[128,128]{1,0:T(8,128)(2,1)} %wn_ref.1) | copy-start | bytes 98308
  79.2 1.4 %copy-start.9 = (bf16[128,128]{1,0:T(8,128)(2,1)S(1)}, bf16[128,128]{1,0:T(8,128)(2,1)}, u32[]{:S(2)}) copy-start(bf16[128,128]{1,0:T(8,128)(2,1)} %ws_ref.1) | copy-start | bytes 98308
  79.2 1.4 %copy-start.10 = (bf16[128,128]{1,0:T(8,128)(2,1)S(1)}, bf16[128,128]{1,0:T(8,128)(2,1)}, u32[]{:S(2)}) copy-start(bf16[128,128]{1,0:T(8,128)(2,1)} %w1_ref.1) | copy-start | bytes 98308
  79.2 1.4 %copy-start.11 = (bf16[128,128]{1,0:T(8,128)(2,1)S(1)}, bf16[128,128]{1,0:T(8,128)(2,1)}, u32[]{:S(2)}) copy-start(bf16[128,128]{1,0:T(8,128)(2,1)} %w2_ref.1) | copy-start | bytes 98308
  79.2 1.4 %copy-start.12 = (bf16[128,128]{1,0:T(8,128)(2,1)S(1)}, bf16[128,128]{1,0:T(8,128)(2,1)}, u32[]{:S(2)}) copy-start(bf16[128,128]{1,0:T(8,128)(2,1)} %wv_ref.1) | copy-start | bytes 98308
  79.2 1.4 %copy-start.13 = (bf16[128,128]{1,0:T(8,128)(2,1)S(1)}, bf16[128,128]{1,0:T(8,128)(2,1)}, u32[]{:S(2)}) copy-start(bf16[128,128]{1,0:T(8,128)(2,1)} %wo_ref.1) | copy-start | bytes 98308
  (2 other events, 1.3 us)
where the time goes:
time: 117 us; the launch traced here: 116 us
  Pallas kernels  75.7 us (65%)
  starting transfers between devices  21.2 us (18%)
  waiting for transfers between devices  10.3 us (9%)
  local copies, waits for them, and re-layouts  6.88 us (6%)
  between operations  1.3 us (1%)
    pallas_call x1, Pallas kernels, ewald(): pl.pallas_call(ewald_kernel, out_shape=jax.ShapeDtypeStruct((2, 1, 256),...  40.9 us
    pallas_call x1, Pallas kernels, pair_update(): pl.pallas_call(functools.partial(pair_kernel, unroll), out_shape=jax.Shap...  34.9 us
    ppermute x6, starting transfers between devices, padded_2(): lax.ppermute(lax.slice_in_dim(block, block.shape[dim] - width, None, axis...  11.2 us
    ppermute x6, starting transfers between devices, padded_2(): lax.ppermute(lax.slice_in_dim(block, 0, width, axis=dim), axis, backward)  10 us
    ppermute x6, waiting for transfers between devices, padded_2(): lax.ppermute(lax.slice_in_dim(block, block.shape[dim] - width, None, axis...  6.05 us
    ppermute x6, waiting for transfers between devices, padded_2(): lax.ppermute(lax.slice_in_dim(block, 0, width, axis=dim), axis, backward)  4.22 us
    unnamed x53, local copies, waits for them, and re-layouts  2.85 us
  transfers between devices with their start and end apart: 12, of which 5 were waited for; matrix products, arithmetic and copies ran while one was open for 3% of the time, Pallas kernels for 35%

commit v1 on v0

v1 whole, which is shorter than its diff:
```python
import functools

import jax
import jax.numpy as jnp
import numpy as np
from jax import lax
from jax.experimental import pallas as pl
from jax.experimental.pallas import tpu as pltpu
from jax.sharding import PartitionSpec as P


coulomb_scale = 0.25
smearing = 1.0


NT = (((1,), (1,)), ((), ()))


def real_basis(length):
    modes = np.arange(length)[:, None]
    cells = np.arange(length)[None, :]
    turns = 2.0 * np.pi * ((modes * cells) % length) / length
    flipped = 2.0 * np.pi * (((length - modes) * cells) % length) / length
    return np.where(modes <= length // 2, np.cos(turns), np.sin(flipped))


def two_parts(table):
    table = np.asarray(table, np.float32)
    high = table.astype(jnp.bfloat16)
    low = (table - high.astype(np.float32)).astype(jnp.bfloat16)
    return np.stack([high, low])


def mode_tables(length):
    modes = np.arange(length)
    signed = np.where(modes > length // 2, modes - length, modes)
    wave = signed * (2.0 * np.pi / length)
    modulus = ((4.0 + 2.0 * np.cos(2.0 * np.pi * modes / length)) / 6.0) ** 2
    weight = np.where((modes == 0) | (modes == length // 2), 1.0, 2.0) / length
    return np.exp(-0.5 * smearing * smearing * wave * wave) / modulus * weight, wave * wave


def ewald_tables():
    basis_z = two_parts(real_basis(256))
    order_y = np.array([4 * p + i for i in range(4) for p in range(16)])
    forward_y = real_basis(64)[:, order_y]
    basis_y = np.stack([two_parts(forward_y), two_parts(forward_y.T)])
    wide = np.zeros((256, 256))
    full_x = real_basis(192)
    for g in range(8):
        wide[:192, 32 * g : 32 * g + 27] = full_x[:, (24 * g - 1 + np.arange(27)) % 192]
    basis_x = two_parts(wide)
    green_x = np.zeros((2, 8, 256))
    gain, square = mode_tables(192)
    green_x[0, :, :192] = gain * (coulomb_scale * 4.0 * np.pi)
    green_x[1, :, :192] = square
    green_x[1, :, 192:] = 1.0
    green_y = np.repeat(np.stack(mode_tables(64))[:, :, None], 128, 2)
    green_z = np.repeat(np.stack(mode_tables(256))[:, :, None], 128, 2)
    return (
        basis_z,
        basis_y,
        basis_x,
        green_x.astype(np.float32),
        green_y.astype(np.float32),
        green_z.astype(np.float32),
    )


def split(value):
    high = value.astype(jnp.bfloat16)
    return high, (value - high.astype(jnp.float32)).astype(jnp.bfloat16)


def dot3(a, b, dims=(((1,), (0,)), ((), ()))):
    def one(u, v):
        return lax.dot_general(u, v, dims, preferred_element_type=jnp.float32)

    return one(a[0], b[0]) + (one(a[0], b[1]) + one(a[1], b[0]))


def swap_groups(pieces, shift):
    lane = lax.broadcasted_iota(jnp.int32, pieces[0].shape, 1) // 32
    out = None
    for k, piece in enumerate(pieces):
        moved = pltpu.roll(piece, (32 * (k - shift)) % 128, 1) if k != shift else piece
        out = moved if out is None else jnp.where(lane == k, moved, out)
    return out


def tap_rows(fraction):
    square = fraction * fraction
    cube = square * fraction
    remain = 1.0 - fraction
    return (
        remain * remain * remain / 6.0,
        (3.0 * cube - 6.0 * square + 4.0) / 6.0,
        (-3.0 * cube + 3.0 * square + 3.0 * fraction + 1.0) / 6.0,
        cube / 6.0,
    )


def pick_taps(offset, taps):
    out = jnp.zeros(offset.shape, jnp.float32)
    for t in range(4):
        out = jnp.where(offset == t, taps[t], out)
    return out


def layer_kernel(
    unroll,
    feat_ref,
    pos_ref,
    atoms_ref,
    nbr_ref,
    count_ref,
    wn_ref,
    ws_ref,
    wr_ref,
    rate_ref,
    w1_ref,
    w2_ref,
    wv_ref,
    wo_ref,
    wc_ref,
    kind_ref,
    bz_ref,
    by_ref,
    bx_ref,
    gx_ref,
    gy_ref,
    gz_ref,
    out_ref,
    site_ref,
    feat_ext,
    pos_ext,
    pos_tab,
    feat32,
    first_w,
    pair1_w,
    pair2_w,
    hot_row,
    lane_row,
    live_row,
    sums,
    tx_atoms,
    rx_atoms,
    z_high,
    z_low,
    stencil,
    tx_b,
    rx_b,
    tx_c,
    rx_c,
    tx_c2,
    rx_c2,
    tx_b2,
    rx_b2,
    parts,
    rx_parts,
    sa,
    ra,
    sb,
    rb,
    sc,
    rc,
    sc2,
    rc2,
    sb2,
    rb2,
    sp,
    rp,
    sf,
    rf,
    sq,
    rq,
):
    bf16 = jnp.bfloat16
    f32 = jnp.float32
    MESH = pl.DeviceIdType.MESH
    ix, iy, iz = lax.axis_index("gx"), lax.axis_index("gy"), lax.axis_index("gz")
    me = iy * 4 + iz
    barrier = pltpu.get_barrier_semaphore()

    def yz_peer(r):
        other = lax.rem(me + r, 16)
        return other, (ix, other // 4, lax.rem(other, 4))

    def x_peer(r):
        other = lax.rem(ix + r, 8)
        return other, (other, iy, iz)

    def greet_yz(r, c):
        pl.semaphore_signal(barrier, inc=1, device_id=yz_peer(r)[1], device_id_type=MESH)
        return c

    def greet_x(r, c):
        pl.semaphore_signal(barrier, inc=1, device_id=x_peer(r)[1], device_id_type=MESH)
        return c

    lax.fori_loop(1, 16, greet_yz, 0)
    lax.fori_loop(1, 8, greet_x, 0)

    def halo_peer(index):
        ox, oy, oz = index // 9 - 1, index // 3 % 3 - 1, index % 3 - 1
        return (lax.rem(ix + ox + 8, 8), lax.rem(iy + oy + 4, 4), lax.rem(iz + oz + 4, 4))

    def halo_span(step, cells):
        if step == 0:
            return pl.ds(0, cells), pl.ds(1, cells)
        return (pl.ds(cells - 1, 1), pl.ds(0, 1)) if step > 0 else (pl.ds(0, 1), pl.ds(cells + 1, 1))

    halo_ids = [n for n in range(27) if n != 13]

    def halo_copies(index):
        steps = (index // 9 - 1, index // 3 % 3 - 1, index % 3 - 1)
        spans = [halo_span(step, cells) for step, cells in zip(steps, (3, 2, 8))]
        source = tuple(span[0] for span in spans)
        target = tuple(span[1] for span in spans)
        return [
            pltpu.make_async_remote_copy(
                src_ref=src.at[source],
                dst_ref=dst.at[target],
                send_sem=send.at[index],
                recv_sem=recv.at[index],
                device_id=halo_peer(index),
                device_id_type=MESH,
            )
            for src, dst, send, recv in ((feat_ref, feat_ext, sf, rf), (pos_ref, pos_ext, sq, rq))
        ]

    for index in halo_ids:
        pl.semaphore_signal(barrier, inc=1, device_id=halo_peer(index), device_id_type=MESH)

    for half in range(2):
        own_rows = feat_ref[:, half].astype(f32).reshape(192, 128).astype(bf16)
        readout = lax.dot_general(wc_ref[...], own_rows, NT, preferred_element_type=f32)[0:1]
        rows = atoms_ref[half]
        kinds = rows[6:7]
        base = jnp.where(kinds == 0.0, kind_ref[0], jnp.where(kinds == 1.0, kind_ref[1], 0.0))
        total = jnp.concatenate([base[:, 0:192] + readout, jnp.zeros((1, 64), f32)], axis=1)
        tx_atoms[half, 0:3, :] = rows[0:3] - (rows[3:6] + 1.0)
        tx_atoms[half, 3:6, :] = rows[3:6]
        tx_atoms[half, 6:7, :] = total
        tx_atoms[half, 7:8, :] = jnp.zeros((1, 256), f32)

    pl.semaphore_wait(barrier, 48)

    routes = [(0, 3, 3, 1), (0, 0, 0, 1), (0, 1, 0, 0), (0, 2, 0, 0)]
    routes += [(1, 1, 0, 1), (1, 2, 0, 1), (1, 3, 0, 0), (1, 0, 1, 0)]

    def atom_copy(half, to_z, step_y, place):
        return pltpu.make_async_remote_copy(
            src_ref=tx_atoms.at[half],
            dst_ref=rx_atoms.at[iz, place],
            send_sem=sa.at[half, to_z],
            recv_sem=ra.at[iz, place],
            device_id=(ix, lax.rem(iy + step_y, 4), to_z),
            device_id_type=MESH,
        )

    for half, to_z, step_y, place in routes:
        if step_y:
            atom_copy(half, to_z, step_y, place).start()
        else:

            @pl.when(iz != to_z)
            def _():
                atom_copy(half, to_z, step_y, place).start()

            @pl.when(iz == to_z)
            def _():
                rx_atoms[iz, place] = tx_atoms[half]

    for index in halo_ids:
        for copy in halo_copies(index):
            copy.start()
    feat_ext[1:4, 1:3, 1:9] = feat_ref[...]
    pos_ext[1:4, 1:3, 1:9] = pos_ref[...]
    first_w[:, 0:128] = (wn_ref[...].astype(f32) * 0.5).T.astype(bf16)
    first_w[:, 128:256] = (ws_ref[...].astype(f32) * 0.5).T.astype(bf16)
    pair1_w[...] = (w1_ref[...].astype(f32) * 0.5).T.astype(bf16)
    pair2_w[...] = (w2_ref[...].astype(f32) * 0.5).T.astype(bf16)
    radial_pad = jnp.concatenate(
        [jnp.zeros((88, 128), f32), wr_ref[...].astype(f32) * 0.5, jnp.zeros((32, 128), f32)], axis=0
    ).T
    cell_x0, cell_y0, cell_z0 = ix * 3, iy * 2, iz * 8
    rates = rate_ref[...]

    sub8 = lax.broadcasted_iota(jnp.int32, (8, 512), 0)
    lane8 = lax.broadcasted_iota(jnp.int32, (8, 512), 1)
    sub_l = lax.broadcasted_iota(jnp.int32, (8, 128), 0)
    own_mask = (lane8 // 64) == sub8
    own_hot = jnp.where(own_mask, 1.0, 0.0).astype(f32)
    own_hot32 = jnp.concatenate([own_hot, own_hot, jnp.zeros((16, 512), f32)], axis=0).astype(bf16)
    lane_t = lax.broadcasted_iota(jnp.int32, (128, 128), 1)
    low_part = (lane_t >= 104) & (lane_t < 112)
    half_sub = sub_l // 4
    axis_sub = sub_l % 4
    box = jnp.where(axis_sub == 0, 192.0, jnp.where(axis_sub == 1, 64.0, 256.0)).astype(f32)
    box_inv = 1.0 / box
    atom_lane = lax.broadcasted_iota(jnp.int32, (8, 128), 1) // 64


    def column(col):
        cx = col // 2
        cy = col % 2
        ids = nbr_ref[col]
        slot = ids & 7
        z = (ids >> 3) & 31
        y = (ids >> 8) & 7
        x = ids >> 11
        dz = (z - (cell_z0 + sub8) + 1) & 31
        dy = (y - (cell_y0 + cy) + 1) & 7
        dx = x - (cell_x0 + cx) + 1
        dx = jnp.where(dx < 0, dx + 24, dx)
        dx = jnp.where(dx >= 24, dx - 24, dx)
        strip = dx * 3 + dy
        hot_row[...] = strip * 24 + dz * 8 + slot
        lane_row[...] = ((dz + sub8) * 8 + slot) * 16 + strip
        counts = count_ref[col]
        pieces = []
        for g in range(4):
            owner = atom_lane + 2 * g
            count_g = jnp.take_along_axis(counts, owner, axis=1)
            slot_g = lax.broadcasted_iota(jnp.int32, (8, 128), 1) % 64
            pieces.append(jnp.where(slot_g < count_g, 1.0, 0.0).astype(f32))
        live_row[...] = jnp.concatenate(pieces, axis=1)

        def cell(cz):
            rows = []
            for dx_ in range(3):
                for dy_ in range(3):
                    base = ((cx + dx_) * 4 + cy + dy_) * 80 + cz * 8
                    rows.append(feat32[pl.ds(pl.multiple_of(base, 8), 24), :])
            own_base = ((cx + 1) * 4 + cy + 1) * 80 + cz * 8 + 8
            own = feat32[pl.ds(pl.multiple_of(own_base, 8), 8), :]
            left = jnp.concatenate(rows + [jnp.zeros((40, 128), f32)], axis=0)
            right = jnp.concatenate(
                [jnp.zeros((224, 128), f32), own, own, jnp.zeros((16, 128), f32)], axis=0
            )
            table = jnp.concatenate([left, right], axis=1).astype(bf16)
            proj = lax.dot_general(first_w[...], table, NT, preferred_element_type=f32)
            tail = proj[:, 128:256]
            tail_hi = tail.astype(bf16).astype(f32)
            tail = jnp.where(low_part, tail - tail_hi, tail_hi) + radial_pad
            lhs = jnp.concatenate([proj[:, 0:128].astype(bf16), tail.astype(bf16)], axis=1)

            place = []
            hot = hot_row[pl.ds(cz, 1), :]
            packed = lane_row[pl.ds(cz, 1), :]
            live = live_row[pl.ds(cz, 1), :]
            for g in range(4):
                packed_g = jnp.broadcast_to(packed[:, g * 128 : g * 128 + 128], (8, 128))
                where_g = packed_g >> 4
                strip_g = packed_g & 15
                got = jnp.zeros((8, 128), f32)
                for t in range(5):
                    hit = strip_g == (2 * t + half_sub)
                    got = jnp.where(
                        hit,
                        jnp.take_along_axis(pos_tab[col, t * 8 : t * 8 + 8, :], where_g, axis=1),
                        got,
                    )
                got = got + pltpu.roll(got, 4, 0)
                mine = jnp.take_along_axis(
                    pos_tab[col, 40:48, :], atom_lane + 2 * g + (cz + 1) * 8, axis=1
                )
                gap = got - mine
                gap = gap - box * jnp.floor(gap * box_inv + 0.5)
                place.append(gap * 0.125)
            scaled = jnp.concatenate(place, axis=1)
            square = scaled * scaled
            square = square[0:1] + square[1:2] + square[2:3]
            basis = jnp.exp(-jnp.broadcast_to(square, (8, 512)) * rates)
            cell_iota = lax.broadcasted_iota(jnp.int32, (216, 512), 0)
            hots = jnp.where(cell_iota == hot, 1.0, 0.0).astype(f32)
            rhs = jnp.concatenate(
                [jnp.concatenate([hots, basis], axis=0).astype(bf16), own_hot32], axis=0
            )
            half = jnp.dot(lhs, rhs, preferred_element_type=f32)
            latent = (half + half * jnp.tanh(half)).astype(bf16)
            half = jnp.dot(pair1_w[...], latent, preferred_element_type=f32)
            second = (half + half * jnp.tanh(half)).astype(bf16)
            half = jnp.dot(pair2_w[...], second, preferred_element_type=f32)
            third = (half + half * jnp.tanh(half)).astype(bf16)

            weighted = scaled * live
            w_hi = weighted.astype(bf16).astype(f32)
            w_lo = weighted - w_hi
            parts = [live]
            for d in range(3):
                parts += [w_hi[d : d + 1], w_lo[d : d + 1]]
            spread = jnp.concatenate(
                [jnp.where(own_mask, jnp.broadcast_to(p, (8, 512)), 0.0) for p in parts]
                + [jnp.zeros((8, 512), f32)],
                axis=0,
            ).astype(bf16)
            total = lax.dot_general(spread, third, NT, preferred_element_type=f32)
            at = pl.multiple_of((col * 8 + cz) * 8, 8)
            sums[0, pl.ds(at, 8), :] = total[0:8]
            for d in range(3):
                sums[1 + d, pl.ds(at, 8), :] = (
                    total[8 + 16 * d : 16 + 16 * d] + total[16 + 16 * d : 24 + 16 * d]
                )

        def step(i, c):
            for u in range(unroll):
                cell(i * unroll + u)
            return c

        lax.fori_loop(0, 8 // unroll, step, 0)

    from_y = [
        lax.rem(iy + jnp.where(iz == 0, 3, 0), 4),
        lax.rem(iy + jnp.where(iz == 3, 1, 0), 4),
    ]
    edge = jnp.where((iz == 0) | (iz == 3), 1, 0)
    from_half = [edge, 1 - edge]

    def atom_wait(s, u):
        @pl.when((s != iz) | (from_y[u] != iy))
        def _():
            pltpu.make_async_remote_copy(
                src_ref=tx_atoms.at[0],
                dst_ref=rx_atoms.at[s, u],
                send_sem=sa.at[0, 0],
                recv_sem=ra.at[s, u],
                device_id=(ix, from_y[u], s),
                device_id_type=MESH,
            ).wait_recv()

    for s in range(4):
        for u in range(2):
            atom_wait(s, u)

    z_ids = lax.broadcasted_iota(jnp.int32, (256, 256), 0)
    x_ids = lax.broadcasted_iota(jnp.int32, (32, 256), 0) + (ix * 24 - 1)
    y_first = iy * 16 + iz * 4

    def spread(slot, total):
        rows = rx_atoms[slot // 2, lax.rem(slot, 2)]
        anchor = rows[3:6].astype(jnp.int32)
        weights_z = pick_taps((z_ids - anchor[2:3]) & 255, tap_rows(rows[2:3]))
        high, low = split(weights_z)
        at = pl.ds(pl.multiple_of(slot * 256, 256), 256)
        z_high[:, at] = high
        z_low[:, at] = low
        weights_x = pick_taps(x_ids - anchor[0:1], tap_rows(rows[0:1]))
        taps_y = tap_rows(rows[1:2])
        blocks = [
            weights_x * pick_taps((y_first + i - anchor[1:2]) & 63, taps_y) for i in range(4)
        ]
        both = jnp.concatenate(blocks, axis=0)
        stencil[:, at] = both
        return total + dot3((high, low), split(both * rows[6:7]), NT)

    lines = lax.fori_loop(0, 8, spread, jnp.zeros((256, 128), f32))
    spectrum = dot3((bz_ref[0], bz_ref[1]), split(lines))
    tx_b[...] = spectrum.reshape(16, 16, 128)
    rx_b[me] = tx_b[me]

    def exchange(tx, rx, send, recv, peer, count, mine):
        def copy(r):
            other, where = peer(r)
            return pltpu.make_async_remote_copy(
                src_ref=tx.at[other],
                dst_ref=rx.at[mine],
                send_sem=send.at[other],
                recv_sem=recv.at[mine],
                device_id=where,
                device_id_type=MESH,
            )

        def arrival(r):
            other, where = peer(r)
            return pltpu.make_async_remote_copy(
                src_ref=tx.at[other],
                dst_ref=rx.at[other],
                send_sem=send.at[other],
                recv_sem=recv.at[other],
                device_id=where,
                device_id_type=MESH,
            )

        def start(r, c):
            copy(r).start()
            return c

        def wait(r, c):
            arrival(r).wait_recv()
            return c

        def drain(r, c):
            copy(r).wait_send()
            return c

        lax.fori_loop(1, count, start, 0)
        return (
            lambda: lax.fori_loop(1, count, wait, 0),
            lambda: lax.fori_loop(1, count, drain, 0),
        )

    arrive_b, drain_b = exchange(tx_b, rx_b, sb, rb, yz_peer, 16, me)

    for index in halo_ids:
        for copy in halo_copies(26 - index):
            copy.wait_recv()
    feat32[...] = feat_ext[...].astype(f32).reshape(1600, 128)
    strip_axis = axis_sub * 8 + lax.broadcasted_iota(jnp.int32, (8, 128), 1) % 8
    strip_cell = lax.broadcasted_iota(jnp.int32, (8, 128), 1) // 8
    strips = []
    for sx in range(5):
        for sy in range(4):
            rows = pos_ext[sx, sy].reshape(10, 128)
            table = jnp.zeros((8, 128), f32)
            for z in range(10):
                row = jnp.broadcast_to(rows[z : z + 1], (8, 128))
                moved = jnp.take_along_axis(row, strip_axis, axis=1)
                table = jnp.where(strip_cell == z, moved, table)
            strips.append(table)
    for n in range(6):
        near = [strips[(n // 2 + d // 3) * 4 + n % 2 + d % 3] for d in range(9)]
        near += [near[4]] * 3
        for t in range(6):
            pos_tab[n, 8 * t : 8 * t + 8, :] = jnp.where(half_sub == 0, near[2 * t], near[2 * t + 1])
    column(0)
    arrive_b()
    flat_b = rx_b.reshape(256, 128)
    columns = []
    for group in range(4):
        pieces = [flat_b[pl.ds(group * 4 + k, 16, 16), :] for k in range(4)]
        columns.append(jnp.concatenate([swap_groups(pieces, i) for i in range(4)], axis=0))
    lines_y = jnp.concatenate(columns, axis=1)
    modes_y = dot3((by_ref[0, 0], by_ref[0, 1]), split(lines_y))
    tx_c[...] = modes_y.reshape(8, 8, 512)
    rx_c[ix] = tx_c[ix]
    arrive_c, drain_c = exchange(tx_c, rx_c, sc, rc, x_peer, 8, ix)

    gain_z = gz_ref[0, pl.ds(pl.multiple_of(me * 16, 16), 16), :]
    square_z = gz_ref[1, pl.ds(pl.multiple_of(me * 16, 16), 16), :]
    gain_y = gy_ref[0, pl.ds(pl.multiple_of(ix * 8, 8), 8), :]
    square_y = gy_ref[1, pl.ds(pl.multiple_of(ix * 8, 8), 8), :]
    gain_yz = (gain_z[:, None, :] * gain_y[None, :, :]).reshape(128, 128)
    square_yz = (square_z[:, None, :] + square_y[None, :, :]).reshape(128, 128)
    greens = []
    for h in range(2):
        lanes = slice(128 * h, 128 * h + 128)
        total = square_yz + gx_ref[1, 0:1, lanes]
        value = gain_yz * gx_ref[0, 0:1, lanes] / (total + 1.0 / 1024.0)
        greens.append(jnp.where(total == 0.0, 0.0, value))
    green = jnp.concatenate(greens, axis=1)
    column(1)

    arrive_c()
    rows_x = []
    for group in range(4):
        for k in range(4):
            halves = [
                swap_groups(
                    [rx_c[4 * h + g, :, group * 128 : group * 128 + 128] for g in range(4)], k
                )
                for h in range(2)
            ]
            rows_x.append(jnp.concatenate(halves, axis=1))
    lines_x = jnp.concatenate(rows_x, axis=0)
    basis_x = (bx_ref[0], bx_ref[1])
    filtered = dot3(split(lines_x), basis_x, NT) * green
    back_x = dot3(split(filtered), basis_x)
    for g in range(8):
        half = g // 4
        for group in range(4):
            pieces = [
                back_x[(group * 4 + k) * 8 : (group * 4 + k) * 8 + 8, half * 128 : half * 128 + 128]
                for k in range(4)
            ]
            tx_c2[g, :, group * 128 : group * 128 + 128] = swap_groups(pieces, g % 4)
    rx_c2[ix] = tx_c2[ix]
    arrive_c2, drain_c2 = exchange(tx_c2, rx_c2, sc2, rc2, x_peer, 8, ix)
    column(2)
    arrive_c2()
    back_y = dot3((by_ref[1, 0], by_ref[1, 1]), split(rx_c2[...].reshape(64, 512)))
    flat_b2 = tx_b2.reshape(256, 128)
    for group in range(4):
        pieces = [back_y[16 * i : 16 * i + 16, group * 128 : group * 128 + 128] for i in range(4)]
        for k in range(4):
            flat_b2[pl.ds(group * 4 + k, 16, 16), :] = swap_groups(pieces, k)
    rx_b2[me] = tx_b2[me]
    arrive_b2, drain_b2 = exchange(tx_b2, rx_b2, sb2, rb2, yz_peer, 16, me)
    column(3)
    arrive_b2()
    back_z = rx_b2[...].reshape(256, 128).T
    potential = split(dot3(split(back_z), (bz_ref[0], bz_ref[1])))

    def sample(slot, c):
        at = pl.ds(pl.multiple_of(slot * 256, 256), 256)
        values = dot3(potential, (z_high[:, at], z_low[:, at]))
        parts[slot] = jnp.sum(values * stencil[:, at], axis=0, keepdims=True)
        return c

    lax.fori_loop(0, 8, sample, 0)

    def part_copy(s, u):
        return pltpu.make_async_remote_copy(
            src_ref=parts.at[2 * s + u],
            dst_ref=rx_parts.at[from_half[u], iz],
            send_sem=sp.at[s, u],
            recv_sem=rp.at[from_half[u], iz],
            device_id=(ix, from_y[u], s),
            device_id_type=MESH,
        )

    for s in range(4):
        for u in range(2):

            @pl.when((s != iz) | (from_y[u] != iy))
            def _():
                part_copy(s, u).start()

            @pl.when((s == iz) & (from_y[u] == iy))
            def _():
                rx_parts[from_half[u], iz] = parts[2 * s + u]

    column(4)
    column(5)
    wv = wv_ref[...]
    invariant = jnp.zeros((384, 128), f32)
    for d in range(3):
        t = sums[1 + d]
        hi = t.astype(bf16)
        lo = (t - hi.astype(f32)).astype(bf16)
        vec = jnp.dot(hi, wv, preferred_element_type=f32) + jnp.dot(
            lo, wv, preferred_element_type=f32
        )
        invariant = invariant + vec * vec
    update = (sums[0] * (1.0 / 64.0) + invariant * (1.0 / 64.0)).astype(bf16)
    out_ref[...] = (
        feat_ref[...].astype(f32).reshape(384, 128) + jnp.dot(update, wo_ref[...], preferred_element_type=f32)
    ).astype(bf16)

    def part_wait(half, to_z, step_y):
        pltpu.make_async_remote_copy(
            src_ref=parts.at[0],
            dst_ref=rx_parts.at[half, to_z],
            send_sem=sp.at[0, 0],
            recv_sem=rp.at[half, to_z],
            device_id=(ix, lax.rem(iy + step_y, 4), to_z),
            device_id_type=MESH,
        ).wait_recv()

    for half, to_z, step_y, place in routes:
        if step_y:
            part_wait(half, to_z, step_y)
        else:

            @pl.when(iz != to_z)
            def _():
                part_wait(half, to_z, step_y)

    for half in range(2):
        site_ref[half] = (
            (rx_parts[half, 0] + rx_parts[half, 1]) + (rx_parts[half, 2] + rx_parts[half, 3])
        )

    for half, to_z, step_y, place in routes:
        if step_y:
            atom_copy(half, to_z, step_y, place).wait_send()
        else:

            @pl.when(iz != to_z)
            def _():
                atom_copy(half, to_z, step_y, place).wait_send()

    drain_b()
    drain_c()
    drain_c2()
    drain_b2()
    for s in range(4):
        for u in range(2):

            @pl.when((s != iz) | (from_y[u] != iy))
            def _():
                part_copy(s, u).wait_send()
    for index in halo_ids:
        for copy in halo_copies(index):
            copy.wait_send()


def layer(operands, unroll=2):
    f32, bf16 = jnp.float32, jnp.bfloat16
    vm = pl.BlockSpec(memory_space=pltpu.VMEM)
    dma = pltpu.SemaphoreType.DMA
    tables = [jnp.asarray(t) for t in ewald_tables()]
    specs = [vm] * 14 + [pl.BlockSpec(memory_space=pltpu.SMEM)] + [vm] * 6
    return pl.pallas_call(
        functools.partial(layer_kernel, unroll),
        out_shape=(
            jax.ShapeDtypeStruct((384, 128), bf16),
            jax.ShapeDtypeStruct((2, 1, 256), f32),
        ),
        in_specs=specs,
        out_specs=(vm, vm),
        scratch_shapes=[
            pltpu.VMEM((5, 4, 10, 8, 128), bf16),
            pltpu.VMEM((5, 4, 10, 1, 128), f32),
            pltpu.VMEM((6, 48, 128), f32),
            pltpu.VMEM((1600, 128), f32),
            pltpu.VMEM((128, 256), bf16),
            pltpu.VMEM((128, 128), bf16),
            pltpu.VMEM((128, 128), bf16),
            pltpu.VMEM((8, 512), jnp.int32),
            pltpu.VMEM((8, 512), jnp.int32),
            pltpu.VMEM((8, 512), f32),
            pltpu.VMEM((4, 384, 128), f32),
            pltpu.VMEM((2, 8, 256), f32),
            pltpu.VMEM((4, 2, 8, 256), f32),
            pltpu.VMEM((256, 2048), bf16),
            pltpu.VMEM((256, 2048), bf16),
            pltpu.VMEM((128, 2048), f32),
            pltpu.VMEM((16, 16, 128), f32),
            pltpu.VMEM((16, 16, 128), f32),
            pltpu.VMEM((8, 8, 512), f32),
            pltpu.VMEM((8, 8, 512), f32),
            pltpu.VMEM((8, 8, 512), f32),
            pltpu.VMEM((8, 8, 512), f32),
            pltpu.VMEM((16, 16, 128), f32),
            pltpu.VMEM((16, 16, 128), f32),
            pltpu.VMEM((8, 1, 256), f32),
            pltpu.VMEM((2, 4, 1, 256), f32),
            dma((2, 4)),
            dma((4, 2)),
            dma((16,)),
            dma((16,)),
            dma((8,)),
            dma((8,)),
            dma((8,)),
            dma((8,)),
            dma((16,)),
            dma((16,)),
            dma((4, 2)),
            dma((2, 4)),
            dma((27,)),
            dma((27,)),
            dma((27,)),
            dma((27,)),
        ],
        compiler_params=pltpu.CompilerParams(
            collective_id=0, has_side_effects=True, vmem_limit_bytes=40 * 1024 * 1024
        ),
        cost_estimate=pl.CostEstimate(flops=4 * 10**9, bytes_accessed=4 * 10**6, transcendentals=10**7),
        name="layer",
    )(*operands, *tables)


def shards(
    features,
    positions,
    grid_anchor,
    species,
    neighbours,
    neighbour_count,
    w_self,
    w_neighbour,
    w_radial,
    radial_rates,
    w_pair1,
    w_pair2,
    w_vector,
    w_out,
    w_charge,
    species_charge,
):
    cells_x, cells_y, cells_z, slot_count, channels = features.shape

    def by_half(values, width):
        grouped = values.reshape(cells_x, cells_y, cells_z, width, slot_count)
        return grouped.transpose(1, 3, 0, 2, 4).reshape(cells_y, width, -1)

    atoms = jnp.concatenate(
        [
            by_half(positions, 3),
            by_half(grid_anchor, 3).astype(jnp.float32),
            by_half(species, 1).astype(jnp.float32),
        ],
        axis=1,
    )
    counts = neighbour_count.reshape(6, 8, 8)
    pos_rows = positions.reshape(cells_x, cells_y, cells_z, 1, 24)
    updated, site = layer(
        (
            features,
            jnp.pad(pos_rows, ((0, 0),) * 4 + ((0, 104),)),
            jnp.pad(atoms, ((0, 0), (0, 1), (0, 64))),
            neighbours.reshape(6, 8, 512),
            jnp.pad(counts, ((0, 0), (0, 0), (0, 120))),
            w_neighbour,
            w_self,
            w_radial,
            radial_rates.reshape(8, 1),
            w_pair1,
            w_pair2,
            w_vector,
            w_out,
            jnp.broadcast_to(w_charge[None, :], (8, channels)),
            species_charge,
        )
    )
    features_out = updated.reshape(cells_x, cells_y, cells_z, slot_count, channels)
    site_potential = site[:, 0, :192].reshape(cells_y, cells_x, cells_z, slot_count)
    site_potential = site_potential.transpose(1, 0, 2, 3)
    return (features_out, site_potential)


def solution(mesh):
    return jax.shard_map(
        shards,
        mesh=mesh,
        in_specs=(
            P("gx", "gy", "gz", None, None),
            P("gx", "gy", "gz", None),
            P("gx", "gy", "gz", None),
            P("gx", "gy", "gz", None),
            P("gx", "gy", "gz", None),
            P("gx", "gy", "gz", None),
            P(),
            P(),
            P(),
            P(),
            P(),
            P(),
            P(),
            P(),
            P(),
            P(),
        ),
        out_specs=(P("gx", "gy", "gz", None, None), P("gx", "gy", "gz", None)),
        check_vma=False,
    )
```

time: 117 us -> 69.3 us (0.59)
  starting transfers between devices: 21.2 us -> 0 us
  Pallas kernels: 75.7 us -> 59.5 us
  waiting for transfers between devices: 10.3 us -> 0 us
    ppermute x12 -> x0, starting transfers between devices: 21.2 us -> none  [the longest x6 11.2 us: padded_2(): lax.ppermute(lax.slice_in_dim(block, block.shape[dim] - width, None, axis...]
    pallas_call x2 -> x1, Pallas kernels: 75.7 us -> 59.5 us  [layer(): pl.pallas_call(functools.partial(layer_kernel, unroll), out_shape=(jax.Sh...]
    ppermute x12 -> x0, waiting for transfers between devices: 10.3 us -> none  [the longest x6 6.05 us: padded_2(): lax.ppermute(lax.slice_in_dim(block, block.shape[dim] - width, None, axis...]
    slice x18 -> x0, local copies, waits for them, and re-layouts: 1.72 us -> none  [the longest x2 1.5 us: padded_2(): lax.slice_in_dim(block, 0, width, axis=dim)]
    convert_element_type x1 -> x2, other arithmetic: 0.01 us -> 1.52 us  [the longest x1 0.77 us: shards(): by_half(grid_anchor, 3).astype(jnp.float32)]
    pad x2, local copies, waits for them, and re-layouts: 0.01 us -> 1.5 us  [the longest x1 0.76 us: shards(): jnp.pad(pos_rows, ((0, 0),) * 4 + ((0, 104),))]
    unnamed x53 -> x37, local copies, waits for them, and re-layouts: 2.85 us -> 3.45 us
  transfers between devices with their start and end apart: 12 -> 0, of which waited for: 5 -> 0; matrix products, arithmetic and copies ran while one was open for 3% -> 0% of each run, Pallas kernels for 35% -> 0%
where the time goes in v1:
time: 69.3 us; the launch traced here: 69 us
  Pallas kernels  59.5 us (86%)
  local copies, waits for them, and re-layouts  6.98 us (10%)
  other arithmetic  1.54 us (2%)
  between operations  0.89 us (1%)
    pallas_call x1, Pallas kernels, layer(): pl.pallas_call(functools.partial(layer_kernel, unroll), out_shape=(jax.Sh...  59.5 us
    unnamed x37, local copies, waits for them, and re-layouts  3.45 us

profile of v1, /device:TPU:1, one launch (start us, length us, event | category | flops | bytes accessed | tf_op | source)
XLA Modules:
  0.0 69.0 jit_solution(17243892590965462945)
XLA Ops:
  0.6 0.0 copy-start.14
  0.6 0.8 %convert_element_type.36 = f32[3,2,8,24]{3,2,1,0:T(8,128)S(1)} convert(s32[3,2,8,24]{3,2,1,0:T(8,128)} %param.24) | non-fusion elementwise | flops 1152 | bytes 9216 | tf_op jit(solution)/shard_map/convert_element_type | solution.py:782
  1.4 0.1 convert_element_type.37
  1.5 0.0 copy-start.15
  1.5 0.0 copy-start.10
  1.6 0.1 reshape.54
  1.7 0.8 %reshape.47 = f32[3,2,8,3,8]{4,3,2,1,0:T(4,128)S(1)} reshape(f32[3,2,8,24]{3,2,1,0:T(8,128)} %param.23) | data formatting | bytes 9216 | tf_op jit(solution)/shard_map/reshape | solution.py:776
  2.5 0.0 copy-start.6
  2.5 0.0 copy-start.7
  2.5 0.0 copy-start.13
  2.6 0.0 copy-start.4
  2.6 0.0 copy-start.5
  2.6 0.1 reshape.53
  2.7 0.0 copy-start.2
  2.7 0.0 copy-start.3
  2.7 0.8 %convert_bitcast_fusion = f32[2,1,3,8,8]{4,3,0,2,1:T(8,128)S(1)} fusion(s32[3,2,8,8]{3,2,1,0:T(8,128)} %param.25), kind=kLoop, calls=%fused_computation.1 | loop fusion | flops 384 | bytes 3072 | tf_op jit(solution)/shard_map/convert_element_type | solution.py:783
  3.5 0.1 convert_element_type.43
  3.6 0.8 %pad.12.pos_ref = f32[3,2,8,1,128]{4,3,2,1,0:T(1,128)S(1)} pad(f32[3,2,8,1,24]{4,3,2,1,0:T(1,128)} %bitcast.30, f32[]{:T(128)} %constant.14.clone.1), padding=0_0x0_0x0_0x0_0x0_104 | pad | bytes 29188 | tf_op jit(solution)/shard_map/jit(_pad)/pad | solution.py:792
  4.3 0.7 %pad.14.count_ref = s32[6,8,128]{2,1,0:T(8,128)S(1)} pad(s32[6,8,8]{2,1,0:T(8,128)} %bitcast.31, s32[]{:T(128)} %constant.15.clone.1), padding=0_0x0_0x0_120 | pad | bytes 26116 | tf_op jit(solution)/shard_map/jit(_pad)/pad | solution.py:795
  5.1 0.7 copy-done.16
  5.7 0.1 copy.34.rate_ref
  5.8 0.6 copy-done.17
  6.4 0.0 copy-done.14
  6.4 0.0 copy-done.11
  6.4 0.0 copy-done.15
  6.5 0.5 copy-done.8
  7.1 0.0 copy-done.9
  7.1 0.9 %copy-done.12 = f32[2,256,128]{2,1,0:T(8,128)S(1)} copy-done((f32[2,256,128]{2,1,0:T(8,128)S(1)}, f32[2,256,128]{2,1,0:T(8,128)}, u32[]{:S(2)}) %copy-start.12) | copy-done | bytes 262168
  8.0 59.5 %layer.1 = (bf16[384,128]{1,0:T(8,128)(2,1)S(1)}, f32[2,1,256]{2,1,0:T(1,128)S(1)}) custom-call(bf16[3,2,8,8,128]{4,3,2,1,0:T(8,128)(2,1)S(1)} %copy-done, f32[3,2,8,1,128]{4,3,2,1,0:T(1,128)S(1)} %pad.12.pos_ref, f32[2,8,256]{2,1,0:T(8,128)S(1)} %select_maximum_fusion.atoms_ref, s32[6,8,512]{2,1,0:T(8,128)S(1)} %bitcast.27, ...), custom_call_target="tpu_custom_call" | custom-call | flops 4000000000 | bytes 4000000 | tf_op jit(solution)/shard_map/layer/pallas_call | solution.py:695
  67.6 0.1 reshape_squeeze.3
  67.7 0.6 copy.41
  68.3 0.6 copy.43
  (24 shorter events, 0.1 us)
Async XLA Ops:
  0.6 5.8 %copy-start.14 = (f32[2,64,128]{2,1,0:T(8,128)S(1)}, f32[2,64,128]{2,1,0:T(8,128)}, u32[]{:S(2)}) copy-start(f32[2,64,128]{2,1,0:T(8,128)} %constant.20.clone.gy_ref) | copy-start | bytes 196612
  1.4 5.0 %copy-start.11 = (bf16[2,256,256]{2,1,0:T(8,128)(2,1)S(1)}, bf16[2,256,256]{2,1,0:T(8,128)(2,1)}, u32[]{:S(2)}) copy-start(bf16[2,256,256]{2,1,0:T(8,128)(2,1)} %constant.18.clone.bx_ref) | copy-start | bytes 786436
  1.5 4.9 %copy-start.15 = (f32[2,8,256]{2,1,0:T(8,128)S(1)}, f32[2,8,256]{2,1,0:T(8,128)}, u32[]{:S(2)}) copy-start(f32[2,8,256]{2,1,0:T(8,128)} %constant.19.clone.gx_ref) | copy-start | bytes 49156
  1.5 4.9 %copy-start.10 = (bf16[2,256,256]{2,1,0:T(8,128)(2,1)S(1)}, bf16[2,256,256]{2,1,0:T(8,128)(2,1)}, u32[]{:S(2)}) copy-start(bf16[2,256,256]{2,1,0:T(8,128)(2,1)} %constant.16.clone.bz_ref) | copy-start | bytes 786436
  2.5 3.9 %copy-start.6 = (bf16[128,128]{1,0:T(8,128)(2,1)S(1)}, bf16[128,128]{1,0:T(8,128)(2,1)}, u32[]{:S(2)}) copy-start(bf16[128,128]{1,0:T(8,128)(2,1)} %wv_ref.1) | copy-start | bytes 98308
  2.5 3.9 %copy-start.7 = (bf16[128,128]{1,0:T(8,128)(2,1)S(1)}, bf16[128,128]{1,0:T(8,128)(2,1)}, u32[]{:S(2)}) copy-start(bf16[128,128]{1,0:T(8,128)(2,1)} %wo_ref.1) | copy-start | bytes 98308
  2.5 3.9 %copy-start.13 = (bf16[2,2,64,64]{3,2,1,0:T(8,128)(2,1)S(1)}, bf16[2,2,64,64]{3,2,1,0:T(8,128)(2,1)}, u32[]{:S(2)}) copy-start(bf16[2,2,64,64]{3,2,1,0:T(8,128)(2,1)} %constant.17.clone.by_ref) | copy-start | bytes 98308
  2.6 3.9 %copy-start.4 = (bf16[128,128]{1,0:T(8,128)(2,1)S(1)}, bf16[128,128]{1,0:T(8,128)(2,1)}, u32[]{:S(2)}) copy-start(bf16[128,128]{1,0:T(8,128)(2,1)} %w1_ref.1) | copy-start | bytes 98308
  2.6 3.9 %copy-start.5 = (bf16[128,128]{1,0:T(8,128)(2,1)S(1)}, bf16[128,128]{1,0:T(8,128)(2,1)}, u32[]{:S(2)}) copy-start(bf16[128,128]{1,0:T(8,128)(2,1)} %w2_ref.1) | copy-start | bytes 98308
  2.7 3.8 %copy-start.2 = (bf16[128,128]{1,0:T(8,128)(2,1)S(1)}, bf16[128,128]{1,0:T(8,128)(2,1)}, u32[]{:S(2)}) copy-start(bf16[128,128]{1,0:T(8,128)(2,1)} %wn_ref.1) | copy-start | bytes 98308
  2.7 3.8 %copy-start.3 = (bf16[128,128]{1,0:T(8,128)(2,1)S(1)}, bf16[128,128]{1,0:T(8,128)(2,1)}, u32[]{:S(2)}) copy-start(bf16[128,128]{1,0:T(8,128)(2,1)} %ws_ref.1) | copy-start | bytes 98308
  3.5 3.1 %copy-start.1 = (s32[3,2,8,512]{3,2,1,0:T(8,128)S(1)}, s32[3,2,8,512]{3,2,1,0:T(8,128)}, u32[]{:S(2)}) copy-start(s32[3,2,8,512]{3,2,1,0:T(8,128)} %param.26) | copy-start | bytes 294916
  3.5 3.1 %copy-start = (bf16[3,2,8,8,128]{4,3,2,1,0:T(8,128)(2,1)S(1)}, bf16[3,2,8,8,128]{4,3,2,1,0:T(8,128)(2,1)}, u32[]{:S(2)}) copy-start(bf16[3,2,8,8,128]{4,3,2,1,0:T(8,128)(2,1)} %feat_ref.1) | copy-start | bytes 294916
  5.1 0.7 copy-start.16
  5.7 0.7 copy-start.17
  6.4 0.7 copy-start.8
  6.4 0.7 copy-start.9
  7.1 1.0 %copy-start.12 = (f32[2,256,128]{2,1,0:T(8,128)S(1)}, f32[2,256,128]{2,1,0:T(8,128)}, u32[]{:S(2)}) copy-start(f32[2,256,128]{2,1,0:T(8,128)} %constant.21.clone.gz_ref) | copy-start | bytes 786436

commit v2 on v1

--- a/solution.py
+++ b/solution.py
@@ -1,5 +1,3 @@
-import functools
-
 import jax
 import jax.numpy as jnp
 import numpy as np
@@ -14,6 +12,7 @@
 
 
 NT = (((1,), (1,)), ((), ()))
+CUTS = (0, 2, 5, 7, 10)
 
 
 def real_basis(length):
@@ -108,11 +107,11 @@
 
 
 def layer_kernel(
-    unroll,
     feat_ref,
-    pos_ref,
-    atoms_ref,
-    nbr_ref,
+    place_ref,
+    anchor_ref,
+    species_ref,
+    nbr_hbm,
     count_ref,
     wn_ref,
     ws_ref,
@@ -124,14 +123,22 @@
     wo_ref,
     wc_ref,
     kind_ref,
+    bz_hbm,
+    by_hbm,
+    bx_hbm,
+    gx_ref,
+    gy_hbm,
+    gz_hbm,
+    out_ref,
+    site_ref,
+    nbr,
     bz_ref,
     by_ref,
     bx_ref,
-    gx_ref,
     gy_ref,
     gz_ref,
-    out_ref,
-    site_ref,
+    load_sem,
+    pos_ref,
     feat_ext,
     pos_ext,
     pos_tab,
@@ -181,6 +188,21 @@
     ix, iy, iz = lax.axis_index("gx"), lax.axis_index("gy"), lax.axis_index("gz")
     me = iy * 4 + iz
     barrier = pltpu.get_barrier_semaphore()
+    loads = [
+        pltpu.make_async_copy(src, dst, load_sem.at[n])
+        for n, (src, dst) in enumerate(
+            (
+                (bz_hbm, bz_ref),
+                (nbr_hbm, nbr),
+                (by_hbm, by_ref),
+                (bx_hbm, bx_ref),
+                (gy_hbm, gy_ref),
+                (gz_hbm, gz_ref),
+            )
+        )
+    ]
+    for load in loads:
+        load.start()
 
     def yz_peer(r):
         other = lax.rem(me + r, 16)
@@ -232,13 +254,41 @@
     for index in halo_ids:
         pl.semaphore_signal(barrier, inc=1, device_id=halo_peer(index), device_id_type=MESH)
 
+    sub_l = lax.broadcasted_iota(jnp.int32, (8, 128), 0)
+    lane_l = lax.broadcasted_iota(jnp.int32, (8, 128), 1)
     for half in range(2):
         own_rows = feat_ref[:, half].astype(f32).reshape(192, 128).astype(bf16)
-        readout = lax.dot_general(wc_ref[...], own_rows, NT, preferred_element_type=f32)[0:1]
-        rows = atoms_ref[half]
+        weights = jnp.broadcast_to(wc_ref[...].astype(f32), (16, 128)).astype(bf16)
+        readout = lax.dot_general(weights, own_rows, NT, preferred_element_type=f32)[0:8]
+        laid = []
+        for cx in range(3):
+            place = place_ref[cx, half]
+            for cz in range(8):
+                pos_ref[cx, half, cz, :, 0:24] = place[cz : cz + 1]
+                pos_ref[cx, half, cz, :, 24:128] = jnp.zeros((1, 104), f32)
+            source = jnp.concatenate(
+                [
+                    place,
+                    anchor_ref[cx, half].astype(f32),
+                    species_ref[cx, half].astype(f32),
+                    jnp.zeros((8, 72), f32),
+                ],
+                axis=1,
+            )
+            rows = jnp.zeros((8, 128), f32)
+            for cz in range(8):
+                row = jnp.broadcast_to(source[cz : cz + 1], (8, 128))
+                moved = jnp.take_along_axis(row, sub_l * 8 + lane_l % 8, axis=1)
+                rows = jnp.where(lane_l // 8 == cz, moved, rows)
+            laid.append(rows)
+        rows = jnp.concatenate(
+            [jnp.where(lane_l < 64, laid[0], pltpu.roll(laid[1], 64, 1)), laid[2]], axis=1
+        )
         kinds = rows[6:7]
         base = jnp.where(kinds == 0.0, kind_ref[0], jnp.where(kinds == 1.0, kind_ref[1], 0.0))
-        total = jnp.concatenate([base[:, 0:192] + readout, jnp.zeros((1, 64), f32)], axis=1)
+        total = jnp.concatenate(
+            [base[:, 0:192] + readout[0:1, :], jnp.zeros((1, 64), f32)], axis=1
+        )
         tx_atoms[half, 0:3, :] = rows[0:3] - (rows[3:6] + 1.0)
         tx_atoms[half, 3:6, :] = rows[3:6]
         tx_atoms[half, 6:7, :] = total
@@ -285,10 +335,12 @@
         [jnp.zeros((88, 128), f32), wr_ref[...].astype(f32) * 0.5, jnp.zeros((32, 128), f32)], axis=0
     ).T
     cell_x0, cell_y0, cell_z0 = ix * 3, iy * 2, iz * 8
-    rates = rate_ref[...]
 
     sub8 = lax.broadcasted_iota(jnp.int32, (8, 512), 0)
     lane8 = lax.broadcasted_iota(jnp.int32, (8, 512), 1)
+    rates = jnp.zeros((8, 512), f32)
+    for k in range(8):
+        rates = jnp.where(sub8 == k, rate_ref[k], rates)
     sub_l = lax.broadcasted_iota(jnp.int32, (8, 128), 0)
     own_mask = (lane8 // 64) == sub8
     own_hot = jnp.where(own_mask, 1.0, 0.0).astype(f32)
@@ -302,10 +354,11 @@
     atom_lane = lax.broadcasted_iota(jnp.int32, (8, 128), 1) // 64
 
 
-    def column(col):
+    def half_column(index, carry):
+        col = index // 2
         cx = col // 2
-        cy = col % 2
-        ids = nbr_ref[col]
+        cy = lax.rem(col, 2)
+        ids = nbr[cx, cy]
         slot = ids & 7
         z = (ids >> 3) & 31
         y = (ids >> 8) & 7
@@ -318,7 +371,7 @@
         strip = dx * 3 + dy
         hot_row[...] = strip * 24 + dz * 8 + slot
         lane_row[...] = ((dz + sub8) * 8 + slot) * 16 + strip
-        counts = count_ref[col]
+        counts = jnp.concatenate([count_ref[cx, cy], jnp.zeros((8, 120), jnp.int32)], axis=1)
         pieces = []
         for g in range(4):
             owner = atom_lane + 2 * g
@@ -379,10 +432,13 @@
                 [jnp.concatenate([hots, basis], axis=0).astype(bf16), own_hot32], axis=0
             )
             half = jnp.dot(lhs, rhs, preferred_element_type=f32)
+            yield
             latent = (half + half * jnp.tanh(half)).astype(bf16)
             half = jnp.dot(pair1_w[...], latent, preferred_element_type=f32)
+            yield
             second = (half + half * jnp.tanh(half)).astype(bf16)
             half = jnp.dot(pair2_w[...], second, preferred_element_type=f32)
+            yield
             third = (half + half * jnp.tanh(half)).astype(bf16)
 
             weighted = scaled * live
@@ -397,6 +453,7 @@
                 axis=0,
             ).astype(bf16)
             total = lax.dot_general(spread, third, NT, preferred_element_type=f32)
+            yield
             at = pl.multiple_of((col * 8 + cz) * 8, 8)
             sums[0, pl.ds(at, 8), :] = total[0:8]
             for d in range(3):
@@ -404,12 +461,13 @@
                     total[8 + 16 * d : 16 + 16 * d] + total[16 + 16 * d : 24 + 16 * d]
                 )
 
-        def step(i, c):
-            for u in range(unroll):
-                cell(i * unroll + u)
-            return c
-
-        lax.fori_loop(0, 8 // unroll, step, 0)
+        running = [cell(lax.rem(index, 2) * 4 + u) for u in range(4)]
+        while running:
+            running = [one for one in running if next(one, 1) is None]
+        return carry
+
+    def half_columns(first, last):
+        lax.fori_loop(first, last, half_column, 0)
 
     from_y = [
         lax.rem(iy + jnp.where(iz == 0, 3, 0), 4),
@@ -430,16 +488,21 @@
                 device_id_type=MESH,
             ).wait_recv()
 
-    for s in range(4):
-        for u in range(2):
-            atom_wait(s, u)
-
     z_ids = lax.broadcasted_iota(jnp.int32, (256, 256), 0)
     x_ids = lax.broadcasted_iota(jnp.int32, (32, 256), 0) + (ix * 24 - 1)
     y_first = iy * 16 + iz * 4
 
-    def spread(slot, total):
-        rows = rx_atoms[slot // 2, lax.rem(slot, 2)]
+    loads[0].wait()
+
+    def spread(turn, total):
+        source = lax.rem(iz + turn, 4)
+        for u in range(2):
+            atom_wait(source, u)
+        for u in range(2):
+            total = spread_one(source * 2 + u, rx_atoms[source, u], total)
+        return total
+
+    def spread_one(slot, rows, total):
         anchor = rows[3:6].astype(jnp.int32)
         weights_z = pick_taps((z_ids - anchor[2:3]) & 255, tap_rows(rows[2:3]))
         high, low = split(weights_z)
@@ -455,7 +518,7 @@
         stencil[:, at] = both
         return total + dot3((high, low), split(both * rows[6:7]), NT)
 
-    lines = lax.fori_loop(0, 8, spread, jnp.zeros((256, 128), f32))
+    lines = lax.fori_loop(0, 4, spread, jnp.zeros((256, 128), f32))
     spectrum = dot3((bz_ref[0], bz_ref[1]), split(lines))
     tx_b[...] = spectrum.reshape(16, 16, 128)
     rx_b[me] = tx_b[me]
@@ -506,6 +569,8 @@
     for index in halo_ids:
         for copy in halo_copies(26 - index):
             copy.wait_recv()
+    for load in loads[1:]:
+        load.wait()
     feat32[...] = feat_ext[...].astype(f32).reshape(1600, 128)
     strip_axis = axis_sub * 8 + lax.broadcasted_iota(jnp.int32, (8, 128), 1) % 8
     strip_cell = lax.broadcasted_iota(jnp.int32, (8, 128), 1) // 8
@@ -524,7 +589,7 @@
         near += [near[4]] * 3
         for t in range(6):
             pos_tab[n, 8 * t : 8 * t + 8, :] = jnp.where(half_sub == 0, near[2 * t], near[2 * t + 1])
-    column(0)
+    half_columns(CUTS[0], CUTS[1])
     arrive_b()
     flat_b = rx_b.reshape(256, 128)
     columns = []
@@ -550,7 +615,7 @@
         value = gain_yz * gx_ref[0, 0:1, lanes] / (total + 1.0 / 1024.0)
         greens.append(jnp.where(total == 0.0, 0.0, value))
     green = jnp.concatenate(greens, axis=1)
-    column(1)
+    half_columns(CUTS[1], CUTS[2])
 
     arrive_c()
     rows_x = []
@@ -577,7 +642,7 @@
             tx_c2[g, :, group * 128 : group * 128 + 128] = swap_groups(pieces, g % 4)
     rx_c2[ix] = tx_c2[ix]
     arrive_c2, drain_c2 = exchange(tx_c2, rx_c2, sc2, rc2, x_peer, 8, ix)
-    column(2)
+    half_columns(CUTS[2], CUTS[3])
     arrive_c2()
     back_y = dot3((by_ref[1, 0], by_ref[1, 1]), split(rx_c2[...].reshape(64, 512)))
     flat_b2 = tx_b2.reshape(256, 128)
@@ -587,7 +652,7 @@
             flat_b2[pl.ds(group * 4 + k, 16, 16), :] = swap_groups(pieces, k)
     rx_b2[me] = tx_b2[me]
     arrive_b2, drain_b2 = exchange(tx_b2, rx_b2, sb2, rb2, yz_peer, 16, me)
-    column(3)
+    half_columns(CUTS[3], CUTS[4])
     arrive_b2()
     back_z = rx_b2[...].reshape(256, 128).T
     potential = split(dot3(split(back_z), (bz_ref[0], bz_ref[1])))
@@ -621,8 +686,7 @@
             def _():
                 rx_parts[from_half[u], iz] = parts[2 * s + u]
 
-    column(4)
-    column(5)
+    half_columns(CUTS[4], 12)
     wv = wv_ref[...]
     invariant = jnp.zeros((384, 128), f32)
     for d in range(3):
@@ -658,9 +722,12 @@
                 part_wait(half, to_z, step_y)
 
     for half in range(2):
-        site_ref[half] = (
-            (rx_parts[half, 0] + rx_parts[half, 1]) + (rx_parts[half, 2] + rx_parts[half, 3])
-        )
+        site = (rx_parts[half, 0] + rx_parts[half, 1]) + (rx_parts[half, 2] + rx_parts[half, 3])
+        for cx in range(3):
+            block = site[:, 0:128] if cx < 2 else site[:, 128:256]
+            block = jnp.broadcast_to(block, (8, 128))
+            at = sub_l * 8 + lane_l % 8 + 64 * (cx % 2)
+            site_ref[cx, half] = jnp.take_along_axis(block, at, axis=1)[:, 0:8]
 
     for half, to_z, step_y, place in routes:
         if step_y:
@@ -686,21 +753,32 @@
             copy.wait_send()
 
 
-def layer(operands, unroll=2):
+def layer(operands):
     f32, bf16 = jnp.float32, jnp.bfloat16
     vm = pl.BlockSpec(memory_space=pltpu.VMEM)
     dma = pltpu.SemaphoreType.DMA
     tables = [jnp.asarray(t) for t in ewald_tables()]
-    specs = [vm] * 14 + [pl.BlockSpec(memory_space=pltpu.SMEM)] + [vm] * 6
+    hbm = pl.BlockSpec(memory_space=pltpu.HBM)
+    smem = pl.BlockSpec(memory_space=pltpu.SMEM)
+    specs = [vm] * 4 + [hbm] + [vm] * 4 + [smem] + [vm] * 5 + [smem]
+    specs += [hbm] * 3 + [vm] + [hbm] * 2
     return pl.pallas_call(
-        functools.partial(layer_kernel, unroll),
+        layer_kernel,
         out_shape=(
             jax.ShapeDtypeStruct((384, 128), bf16),
-            jax.ShapeDtypeStruct((2, 1, 256), f32),
+            jax.ShapeDtypeStruct((3, 2, 8, 8), f32),
         ),
         in_specs=specs,
         out_specs=(vm, vm),
         scratch_shapes=[
+            pltpu.VMEM((3, 2, 8, 512), jnp.int32),
+            pltpu.VMEM((2, 256, 256), bf16),
+            pltpu.VMEM((2, 2, 64, 64), bf16),
+            pltpu.VMEM((2, 256, 256), bf16),
+            pltpu.VMEM((2, 64, 128), f32),
+            pltpu.VMEM((2, 256, 128), f32),
+            dma((6,)),
+            pltpu.VMEM((3, 2, 8, 1, 128), f32),
             pltpu.VMEM((5, 4, 10, 8, 128), bf16),
             pltpu.VMEM((5, 4, 10, 1, 128), f32),
             pltpu.VMEM((6, 48, 128), f32),
@@ -745,7 +823,7 @@
             dma((27,)),
         ],
         compiler_params=pltpu.CompilerParams(
-            collective_id=0, has_side_effects=True, vmem_limit_bytes=40 * 1024 * 1024
+            collective_id=0, has_side_effects=True, vmem_limit_bytes=67043328
         ),
         cost_estimate=pl.CostEstimate(flops=4 * 10**9, bytes_accessed=4 * 10**6, transcendentals=10**7),
         name="layer",
@@ -770,45 +848,27 @@
     w_charge,
     species_charge,
 ):
-    cells_x, cells_y, cells_z, slot_count, channels = features.shape
-
-    def by_half(values, width):
-        grouped = values.reshape(cells_x, cells_y, cells_z, width, slot_count)
-        return grouped.transpose(1, 3, 0, 2, 4).reshape(cells_y, width, -1)
-
-    atoms = jnp.concatenate(
-        [
-            by_half(positions, 3),
-            by_half(grid_anchor, 3).astype(jnp.float32),
-            by_half(species, 1).astype(jnp.float32),
-        ],
-        axis=1,
-    )
-    counts = neighbour_count.reshape(6, 8, 8)
-    pos_rows = positions.reshape(cells_x, cells_y, cells_z, 1, 24)
-    updated, site = layer(
+    updated, site_potential = layer(
         (
             features,
-            jnp.pad(pos_rows, ((0, 0),) * 4 + ((0, 104),)),
-            jnp.pad(atoms, ((0, 0), (0, 1), (0, 64))),
-            neighbours.reshape(6, 8, 512),
-            jnp.pad(counts, ((0, 0), (0, 0), (0, 120))),
+            positions,
+            grid_anchor,
+            species,
+            neighbours,
+            neighbour_count,
             w_neighbour,
             w_self,
             w_radial,
-            radial_rates.reshape(8, 1),
+            radial_rates,
             w_pair1,
             w_pair2,
             w_vector,
             w_out,
-            jnp.broadcast_to(w_charge[None, :], (8, channels)),
+            w_charge.reshape(1, 128),
             species_charge,
         )
     )
-    features_out = updated.reshape(cells_x, cells_y, cells_z, slot_count, channels)
-    site_potential = site[:, 0, :192].reshape(cells_y, cells_x, cells_z, slot_count)
-    site_potential = site_potential.transpose(1, 0, 2, 3)
-    return (features_out, site_potential)
+    return (updated.reshape(features.shape), site_potential)
 
 
 def solution(mesh):

time: 69.3 us -> 49 us (0.71)
  Pallas kernels: 59.5 us -> 46 us
  local copies, waits for them, and re-layouts: 6.98 us -> 2.16 us
  other arithmetic: 1.54 us -> 0 us
    pallas_call x1, Pallas kernels: 59.5 us -> 46 us  [layer(): pl.pallas_call(layer_kernel, out_shape=(jax.ShapeDtypeStruct((384, 128),...]
    convert_element_type x2 -> x0, other arithmetic: 1.52 us -> none  [the longest x1 0.77 us: shards(): by_half(grid_anchor, 3).astype(jnp.float32)]
    pad x2 -> x0, local copies, waits for them, and re-layouts: 1.5 us -> none  [the longest x1 0.76 us: shards(): jnp.pad(pos_rows, ((0, 0),) * 4 + ((0, 104),))]
    unnamed x37 -> x4, local copies, waits for them, and re-layouts: 3.45 us -> 2.16 us
    reshape x4 -> x0, local copies, waits for them, and re-layouts: 1.02 us -> none  [the longest x1 0.83 us: by_half(): grouped = values.reshape(cells_x, cells_y, cells_z, width, slot_count)]
    another operation x2 -> x0, local copies, waits for them, and re-layouts: 0.7 us -> none  [shards(): site[:, 0, :192].reshape(cells_y, cells_x, cells_z, slot_count)]
where the time goes in v2:
time: 49 us; the launch traced here: 48.8 us
  Pallas kernels  46 us (94%)
  local copies, waits for them, and re-layouts  2.16 us (4%)
  between operations  0.65 us (1%)
    pallas_call x1, Pallas kernels, layer(): pl.pallas_call(layer_kernel, out_shape=(jax.ShapeDtypeStruct((384, 128),...  46 us
    unnamed x4, local copies, waits for them, and re-layouts  2.16 us

profile of v2, /device:TPU:1, one launch (start us, length us, event | category | flops | bytes accessed | tf_op | source)
XLA Modules:
  0.0 48.8 jit_solution(10148893439761080188)
XLA Ops:
  0.6 46.0 %layer.1 = (bf16[384,128]{1,0:T(8,128)(2,1)}, f32[3,2,8,8]{3,2,1,0:T(8,128)}) custom-call(bf16[3,2,8,8,128]{4,3,2,1,0:T(8,128)(2,1)} %feat_ref.1, f32[3,2,8,24]{3,2,1,0:T(8,128)} %place_ref.1, s32[3,2,8,24]{3,2,1,0:T(8,128)} %anchor_ref.1, s32[3,2,8,8]{3,2,1,0:T(8,128)} %species_ref.1, s32[3,2,8,512]{3,2,1,0:T(8,128)} %nbr_hbm.1, s32[3,2,8,8]{3,2,1,0:T(8,128)} %count_ref.1, ...), custom_call_target="tpu_custom_call" | custom-call | flops 4000000000 | bytes 4000000 | tf_op jit(solution)/shard_map/layer/pallas_call | solution.py:765
  46.6 0.0 copy-start
  46.6 1.5 %copy.26 = bf16[3,2,8,8,128]{4,3,2,1,0:T(8,128)(2,1)} copy(bf16[3,2,8,8,128]{4,3,2,1,0:T(8,128)(2,1)} %bitcast.2) | data formatting | bytes 196608
  48.2 0.0 copy-done
  48.2 0.6 %copy.27 = f32[3,2,8,8]{3,2,1,0:T(8,128)} copy(f32[3,2,8,8]{3,2,1,0:T(8,128)S(1)} %copy-done) | data formatting | bytes 3072
Async XLA Ops:
  46.6 1.6 %copy-start = (f32[3,2,8,8]{3,2,1,0:T(8,128)S(1)}, f32[3,2,8,8]{3,2,1,0:T(8,128)}, u32[]{:S(2)}) copy-start(f32[3,2,8,8]{3,2,1,0:T(8,128)} %get-tuple-element.9) | copy-start | bytes 4612

commit v3 on v2

--- a/solution.py
+++ b/solution.py
@@ -12,7 +12,7 @@
 
 
 NT = (((1,), (1,)), ((), ()))
-CUTS = (0, 2, 5, 7, 10)
+CUTS = (0, 4, 6, 8, 11)
 
 
 def real_basis(length):
@@ -107,36 +107,50 @@
 
 
 def layer_kernel(
+    feat_hbm,
+    place_hbm,
+    anchor_hbm,
+    species_hbm,
+    nbr_hbm,
+    count_hbm,
+    wn_hbm,
+    ws_hbm,
+    wr_hbm,
+    rate_ref,
+    w1_hbm,
+    w2_hbm,
+    wv_hbm,
+    wo_hbm,
+    wc_hbm,
+    kind_ref,
+    bz_hbm,
+    by_hbm,
+    bx_hbm,
+    gx_hbm,
+    gy_hbm,
+    gz_hbm,
+    out_ref,
+    site_ref,
     feat_ref,
     place_ref,
     anchor_ref,
     species_ref,
-    nbr_hbm,
-    count_ref,
+    wc_ref,
     wn_ref,
     ws_ref,
     wr_ref,
-    rate_ref,
     w1_ref,
     w2_ref,
-    wv_ref,
-    wo_ref,
-    wc_ref,
-    kind_ref,
-    bz_hbm,
-    by_hbm,
-    bx_hbm,
-    gx_ref,
-    gy_hbm,
-    gz_hbm,
-    out_ref,
-    site_ref,
-    nbr,
+    nbr_ref,
+    count_ref,
     bz_ref,
     by_ref,
     bx_ref,
+    gx_ref,
     gy_ref,
     gz_ref,
+    wv_ref,
+    wo_ref,
     load_sem,
     pos_ref,
     feat_ext,
@@ -188,18 +202,30 @@
     ix, iy, iz = lax.axis_index("gx"), lax.axis_index("gy"), lax.axis_index("gz")
     me = iy * 4 + iz
     barrier = pltpu.get_barrier_semaphore()
+    pairs = (
+        (feat_hbm, feat_ref),
+        (place_hbm, place_ref),
+        (anchor_hbm, anchor_ref),
+        (species_hbm, species_ref),
+        (wc_hbm, wc_ref),
+        (wn_hbm, wn_ref),
+        (ws_hbm, ws_ref),
+        (wr_hbm, wr_ref),
+        (w1_hbm, w1_ref),
+        (w2_hbm, w2_ref),
+        (nbr_hbm, nbr_ref),
+        (count_hbm, count_ref),
+        (bz_hbm, bz_ref),
+        (by_hbm, by_ref),
+        (bx_hbm, bx_ref),
+        (gx_hbm, gx_ref),
+        (gy_hbm, gy_ref),
+        (gz_hbm, gz_ref),
+        (wv_hbm, wv_ref),
+        (wo_hbm, wo_ref),
+    )
     loads = [
-        pltpu.make_async_copy(src, dst, load_sem.at[n])
-        for n, (src, dst) in enumerate(
-            (
-                (bz_hbm, bz_ref),
-                (nbr_hbm, nbr),
-                (by_hbm, by_ref),
-                (bx_hbm, bx_ref),
-                (gy_hbm, gy_ref),
-                (gz_hbm, gz_ref),
-            )
-        )
+        pltpu.make_async_copy(src, dst, load_sem.at[n]) for n, (src, dst) in enumerate(pairs)
     ]
     for load in loads:
         load.start()
@@ -233,26 +259,35 @@
         return (pl.ds(cells - 1, 1), pl.ds(0, 1)) if step > 0 else (pl.ds(0, 1), pl.ds(cells + 1, 1))
 
     halo_ids = [n for n in range(27) if n != 13]
+    near_ids = [n for n in halo_ids if n // 9 == 1]
+    far_ids = [n for n in halo_ids if n // 9 != 1]
 
     def halo_copies(index):
         steps = (index // 9 - 1, index // 3 % 3 - 1, index % 3 - 1)
         spans = [halo_span(step, cells) for step, cells in zip(steps, (3, 2, 8))]
         source = tuple(span[0] for span in spans)
         target = tuple(span[1] for span in spans)
+        row = {0: pl.ds(1, 2), 1: pl.ds(0, 1), -1: pl.ds(3, 1)}[steps[2]]
         return [
             pltpu.make_async_remote_copy(
-                src_ref=src.at[source],
-                dst_ref=dst.at[target],
+                src_ref=src.at[source[:2] + (from_z,)],
+                dst_ref=dst.at[target[:2] + (to_z,)],
                 send_sem=send.at[index],
                 recv_sem=recv.at[index],
                 device_id=halo_peer(index),
                 device_id_type=MESH,
             )
-            for src, dst, send, recv in ((feat_ref, feat_ext, sf, rf), (pos_ref, pos_ext, sq, rq))
+            for src, dst, send, recv, from_z, to_z in (
+                (feat_ref, feat_ext, sf, rf, source[2], target[2]),
+                (pos_ref, pos_ext, sq, rq, row, row),
+            )
         ]
 
     for index in halo_ids:
         pl.semaphore_signal(barrier, inc=1, device_id=halo_peer(index), device_id_type=MESH)
+
+    for load in loads[:5]:
+        load.wait()
 
     sub_l = lax.broadcasted_iota(jnp.int32, (8, 128), 0)
     lane_l = lax.broadcasted_iota(jnp.int32, (8, 128), 1)
@@ -263,9 +298,10 @@
         laid = []
         for cx in range(3):
             place = place_ref[cx, half]
-            for cz in range(8):
-                pos_ref[cx, half, cz, :, 0:24] = place[cz : cz + 1]
-                pos_ref[cx, half, cz, :, 24:128] = jnp.zeros((1, 104), f32)
+            for row, cells in ((0, (7,)), (1, (0, 1, 2, 3)), (2, (4, 5, 6, 7)), (3, (0,))):
+                pieces = [place[cz : cz + 1] for cz in cells]
+                pieces.append(jnp.zeros((1, 128 - 24 * len(cells)), f32))
+                pos_ref[cx, half, row] = jnp.concatenate(pieces, axis=1)
             source = jnp.concatenate(
                 [
                     place,
@@ -294,39 +330,8 @@
         tx_atoms[half, 6:7, :] = total
         tx_atoms[half, 7:8, :] = jnp.zeros((1, 256), f32)
 
-    pl.semaphore_wait(barrier, 48)
-
-    routes = [(0, 3, 3, 1), (0, 0, 0, 1), (0, 1, 0, 0), (0, 2, 0, 0)]
-    routes += [(1, 1, 0, 1), (1, 2, 0, 1), (1, 3, 0, 0), (1, 0, 1, 0)]
-
-    def atom_copy(half, to_z, step_y, place):
-        return pltpu.make_async_remote_copy(
-            src_ref=tx_atoms.at[half],
-            dst_ref=rx_atoms.at[iz, place],
-            send_sem=sa.at[half, to_z],
-            recv_sem=ra.at[iz, place],
-            device_id=(ix, lax.rem(iy + step_y, 4), to_z),
-            device_id_type=MESH,
-        )
-
-    for half, to_z, step_y, place in routes:
-        if step_y:
-            atom_copy(half, to_z, step_y, place).start()
-        else:
-
-            @pl.when(iz != to_z)
-            def _():
-                atom_copy(half, to_z, step_y, place).start()
-
-            @pl.when(iz == to_z)
-            def _():
-                rx_atoms[iz, place] = tx_atoms[half]
-
-    for index in halo_ids:
-        for copy in halo_copies(index):
-            copy.start()
-    feat_ext[1:4, 1:3, 1:9] = feat_ref[...]
-    pos_ext[1:4, 1:3, 1:9] = pos_ref[...]
+    for load in loads[5:10]:
+        load.wait()
     first_w[:, 0:128] = (wn_ref[...].astype(f32) * 0.5).T.astype(bf16)
     first_w[:, 128:256] = (ws_ref[...].astype(f32) * 0.5).T.astype(bf16)
     pair1_w[...] = (w1_ref[...].astype(f32) * 0.5).T.astype(bf16)
@@ -341,7 +346,6 @@
     rates = jnp.zeros((8, 512), f32)
     for k in range(8):
         rates = jnp.where(sub8 == k, rate_ref[k], rates)
-    sub_l = lax.broadcasted_iota(jnp.int32, (8, 128), 0)
     own_mask = (lane8 // 64) == sub8
     own_hot = jnp.where(own_mask, 1.0, 0.0).astype(f32)
     own_hot32 = jnp.concatenate([own_hot, own_hot, jnp.zeros((16, 512), f32)], axis=0).astype(bf16)
@@ -352,13 +356,45 @@
     box = jnp.where(axis_sub == 0, 192.0, jnp.where(axis_sub == 1, 64.0, 256.0)).astype(f32)
     box_inv = 1.0 / box
     atom_lane = lax.broadcasted_iota(jnp.int32, (8, 128), 1) // 64
-
-
+    pl.semaphore_wait(barrier, 48)
+
+    routes = [(0, 3, 3, 1), (0, 0, 0, 1), (0, 1, 0, 0), (0, 2, 0, 0)]
+    routes += [(1, 1, 0, 1), (1, 2, 0, 1), (1, 3, 0, 0), (1, 0, 1, 0)]
+
+    def atom_copy(half, to_z, step_y, place):
+        return pltpu.make_async_remote_copy(
+            src_ref=tx_atoms.at[half],
+            dst_ref=rx_atoms.at[iz, place],
+            send_sem=sa.at[half, to_z],
+            recv_sem=ra.at[iz, place],
+            device_id=(ix, lax.rem(iy + step_y, 4), to_z),
+            device_id_type=MESH,
+        )
+
+    for half, to_z, step_y, place in routes:
+        if step_y:
+            atom_copy(half, to_z, step_y, place).start()
+        else:
+
+            @pl.when(iz != to_z)
+            def _():
+                atom_copy(half, to_z, step_y, place).start()
+
+            @pl.when(iz == to_z)
+            def _():
+                rx_atoms[iz, place] = tx_atoms[half]
+
+    for index in near_ids:
+        for copy in halo_copies(index):
+            copy.start()
+    feat_ext[1:4, 1:3, 1:9] = feat_ref[...]
+    pos_ext[1:4, 1:3, 1:3] = pos_ref[:, :, 1:3]
     def half_column(index, carry):
-        col = index // 2
+        later = (index - 4) // 2
+        col = jnp.where(index < 4, 2 + index // 2, jnp.where(later < 2, later, later + 2))
         cx = col // 2
         cy = lax.rem(col, 2)
-        ids = nbr[cx, cy]
+        ids = nbr_ref[cx, cy]
         slot = ids & 7
         z = (ids >> 3) & 31
         y = (ids >> 8) & 7
@@ -488,34 +524,40 @@
                 device_id_type=MESH,
             ).wait_recv()
 
-    z_ids = lax.broadcasted_iota(jnp.int32, (256, 256), 0)
-    x_ids = lax.broadcasted_iota(jnp.int32, (32, 256), 0) + (ix * 24 - 1)
     y_first = iy * 16 + iz * 4
 
-    loads[0].wait()
+    for load in loads[10:]:
+        load.wait()
+    z_ids = lax.broadcasted_iota(jnp.int32, (256, 384), 0)
+    x_ids = lax.broadcasted_iota(jnp.int32, (32, 384), 0) + (ix * 24 - 1)
+    lane_384 = lax.broadcasted_iota(jnp.int32, (8, 128), 1)
 
     def spread(turn, total):
         source = lax.rem(iz + turn, 4)
         for u in range(2):
             atom_wait(source, u)
-        for u in range(2):
-            total = spread_one(source * 2 + u, rx_atoms[source, u], total)
-        return total
-
-    def spread_one(slot, rows, total):
+        low_part_, high_part_ = rx_atoms[source, 0], rx_atoms[source, 1]
+        moved = pltpu.roll(high_part_, 64, 1)
+        rows = jnp.concatenate(
+            [
+                low_part_[:, 0:128],
+                jnp.where(lane_384 < 64, low_part_[:, 128:256], moved[:, 0:128]),
+                moved[:, 128:256],
+            ],
+            axis=1,
+        )
         anchor = rows[3:6].astype(jnp.int32)
         weights_z = pick_taps((z_ids - anchor[2:3]) & 255, tap_rows(rows[2:3]))
         high, low = split(weights_z)
-        at = pl.ds(pl.multiple_of(slot * 256, 256), 256)
-        z_high[:, at] = high
-        z_low[:, at] = low
+        z_high[source] = high
+        z_low[source] = low
         weights_x = pick_taps(x_ids - anchor[0:1], tap_rows(rows[0:1]))
         taps_y = tap_rows(rows[1:2])
         blocks = [
             weights_x * pick_taps((y_first + i - anchor[1:2]) & 63, taps_y) for i in range(4)
         ]
         both = jnp.concatenate(blocks, axis=0)
-        stencil[:, at] = both
+        stencil[source] = both
         return total + dot3((high, low), split(both * rows[6:7]), NT)
 
     lines = lax.fori_loop(0, 4, spread, jnp.zeros((256, 128), f32))
@@ -566,29 +608,39 @@
 
     arrive_b, drain_b = exchange(tx_b, rx_b, sb, rb, yz_peer, 16, me)
 
-    for index in halo_ids:
-        for copy in halo_copies(26 - index):
-            copy.wait_recv()
-    for load in loads[1:]:
-        load.wait()
-    feat32[...] = feat_ext[...].astype(f32).reshape(1600, 128)
-    strip_axis = axis_sub * 8 + lax.broadcasted_iota(jnp.int32, (8, 128), 1) % 8
-    strip_cell = lax.broadcasted_iota(jnp.int32, (8, 128), 1) // 8
-    strips = []
-    for sx in range(5):
+    for index in far_ids:
+        for copy in halo_copies(index):
+            copy.start()
+    strip_lane = lax.broadcasted_iota(jnp.int32, (8, 128), 1)
+    strip_cell = strip_lane // 8
+    within = axis_sub * 8 + strip_lane % 8
+    starts = jnp.where(strip_cell == 0, 0, jnp.where(strip_cell == 9, 0, lax.rem(strip_cell + 3, 4)))
+    strip_at = jnp.where(axis_sub == 3, 127, jnp.minimum(starts * 24 + within, 127))
+    strips = {}
+
+    def lay_strips(sx):
+        feat32[320 * sx : 320 * sx + 320, :] = feat_ext[sx].astype(f32).reshape(320, 128)
         for sy in range(4):
-            rows = pos_ext[sx, sy].reshape(10, 128)
             table = jnp.zeros((8, 128), f32)
-            for z in range(10):
-                row = jnp.broadcast_to(rows[z : z + 1], (8, 128))
-                moved = jnp.take_along_axis(row, strip_axis, axis=1)
-                table = jnp.where(strip_cell == z, moved, table)
-            strips.append(table)
-    for n in range(6):
-        near = [strips[(n // 2 + d // 3) * 4 + n % 2 + d % 3] for d in range(9)]
+            for row, first, last in ((0, 0, 1), (1, 1, 5), (2, 5, 9), (3, 9, 10)):
+                source = jnp.broadcast_to(pos_ext[sx, sy, row], (8, 128))
+                moved = jnp.take_along_axis(source, strip_at, axis=1)
+                table = jnp.where((strip_cell >= first) & (strip_cell < last), moved, table)
+            strips[sx, sy] = table
+
+    def lay_column(n):
+        near = [strips[n // 2 + d // 3, n % 2 + d % 3] for d in range(9)]
         near += [near[4]] * 3
         for t in range(6):
             pos_tab[n, 8 * t : 8 * t + 8, :] = jnp.where(half_sub == 0, near[2 * t], near[2 * t + 1])
+
+    for index in near_ids:
+        for copy in halo_copies(26 - index):
+            copy.wait_recv()
+    for sx in (1, 2, 3):
+        lay_strips(sx)
+    for n in (2, 3):
+        lay_column(n)
     half_columns(CUTS[0], CUTS[1])
     arrive_b()
     flat_b = rx_b.reshape(256, 128)
@@ -615,6 +667,13 @@
         value = gain_yz * gx_ref[0, 0:1, lanes] / (total + 1.0 / 1024.0)
         greens.append(jnp.where(total == 0.0, 0.0, value))
     green = jnp.concatenate(greens, axis=1)
+    for index in far_ids:
+        for copy in halo_copies(26 - index):
+            copy.wait_recv()
+    for sx in (0, 4):
+        lay_strips(sx)
+    for n in (0, 1, 4, 5):
+        lay_column(n)
     half_columns(CUTS[1], CUTS[2])
 
     arrive_c()
@@ -657,13 +716,15 @@
     back_z = rx_b2[...].reshape(256, 128).T
     potential = split(dot3(split(back_z), (bz_ref[0], bz_ref[1])))
 
-    def sample(slot, c):
-        at = pl.ds(pl.multiple_of(slot * 256, 256), 256)
-        values = dot3(potential, (z_high[:, at], z_low[:, at]))
-        parts[slot] = jnp.sum(values * stencil[:, at], axis=0, keepdims=True)
+    def sample(source, c):
+        values = dot3(potential, (z_high[source], z_low[source]))
+        sums_ = jnp.sum(values * stencil[source], axis=0, keepdims=True)
+        parts[2 * source] = sums_[:, 0:256]
+        tail = jnp.broadcast_to(sums_[:, 128:384], (8, 256))
+        parts[2 * source + 1] = pltpu.roll(tail, 192, 1)[0:1]
         return c
 
-    lax.fori_loop(0, 8, sample, 0)
+    lax.fori_loop(0, 4, sample, 0)
 
     def part_copy(s, u):
         return pltpu.make_async_remote_copy(
@@ -702,6 +763,23 @@
         feat_ref[...].astype(f32).reshape(384, 128) + jnp.dot(update, wo_ref[...], preferred_element_type=f32)
     ).astype(bf16)
 
+    for half, to_z, step_y, place in routes:
+        if step_y:
+            atom_copy(half, to_z, step_y, place).wait_send()
+        else:
+
+            @pl.when(iz != to_z)
+            def _():
+                atom_copy(half, to_z, step_y, place).wait_send()
+
+    drain_b()
+    drain_c()
+    drain_c2()
+    drain_b2()
+    for index in halo_ids:
+        for copy in halo_copies(index):
+            copy.wait_send()
+
     def part_wait(half, to_z, step_y):
         pltpu.make_async_remote_copy(
             src_ref=parts.at[0],
@@ -729,28 +807,12 @@
             at = sub_l * 8 + lane_l % 8 + 64 * (cx % 2)
             site_ref[cx, half] = jnp.take_along_axis(block, at, axis=1)[:, 0:8]
 
-    for half, to_z, step_y, place in routes:
-        if step_y:
-            atom_copy(half, to_z, step_y, place).wait_send()
-        else:
-
-            @pl.when(iz != to_z)
-            def _():
-                atom_copy(half, to_z, step_y, place).wait_send()
-
-    drain_b()
-    drain_c()
-    drain_c2()
-    drain_b2()
     for s in range(4):
         for u in range(2):
 
             @pl.when((s != iz) | (from_y[u] != iy))
             def _():
                 part_copy(s, u).wait_send()
-    for index in halo_ids:
-        for copy in halo_copies(index):
-            copy.wait_send()
 
 
 def layer(operands):
@@ -760,8 +822,10 @@
     tables = [jnp.asarray(t) for t in ewald_tables()]
     hbm = pl.BlockSpec(memory_space=pltpu.HBM)
     smem = pl.BlockSpec(memory_space=pltpu.SMEM)
-    specs = [vm] * 4 + [hbm] + [vm] * 4 + [smem] + [vm] * 5 + [smem]
-    specs += [hbm] * 3 + [vm] + [hbm] * 2
+    specs = [hbm] * 9 + [smem] + [hbm] * 5 + [smem] + [hbm] * 6
+    shapes = [operands[n] for n in (0, 1, 2, 3, 14, 6, 7, 8, 10, 11, 4, 5)] + tables
+    shapes += [operands[n] for n in (12, 13)]
+    staged = [pltpu.VMEM(x.shape, x.dtype) for x in shapes]
     return pl.pallas_call(
         layer_kernel,
         out_shape=(
@@ -770,17 +834,12 @@
         ),
         in_specs=specs,
         out_specs=(vm, vm),
-        scratch_shapes=[
-            pltpu.VMEM((3, 2, 8, 512), jnp.int32),
-            pltpu.VMEM((2, 256, 256), bf16),
-            pltpu.VMEM((2, 2, 64, 64), bf16),
-            pltpu.VMEM((2, 256, 256), bf16),
-            pltpu.VMEM((2, 64, 128), f32),
-            pltpu.VMEM((2, 256, 128), f32),
-            dma((6,)),
-            pltpu.VMEM((3, 2, 8, 1, 128), f32),
+        scratch_shapes=staged
+        + [
+            dma((20,)),
+            pltpu.VMEM((3, 2, 4, 1, 128), f32),
             pltpu.VMEM((5, 4, 10, 8, 128), bf16),
-            pltpu.VMEM((5, 4, 10, 1, 128), f32),
+            pltpu.VMEM((5, 4, 4, 1, 128), f32),
             pltpu.VMEM((6, 48, 128), f32),
             pltpu.VMEM((1600, 128), f32),
             pltpu.VMEM((128, 256), bf16),
@@ -792,9 +851,9 @@
             pltpu.VMEM((4, 384, 128), f32),
             pltpu.VMEM((2, 8, 256), f32),
             pltpu.VMEM((4, 2, 8, 256), f32),
-            pltpu.VMEM((256, 2048), bf16),
-            pltpu.VMEM((256, 2048), bf16),
-            pltpu.VMEM((128, 2048), f32),
+            pltpu.VMEM((4, 256, 384), bf16),
+            pltpu.VMEM((4, 256, 384), bf16),
+            pltpu.VMEM((4, 128, 384), f32),
             pltpu.VMEM((16, 16, 128), f32),
             pltpu.VMEM((16, 16, 128), f32),
             pltpu.VMEM((8, 8, 512), f32),

time: 49 us -> 47.7 us (0.973)
  Pallas kernels: 46 us -> 44.8 us
    pallas_call x1, Pallas kernels: 46 us -> 44.8 us  [layer(): pl.pallas_call(layer_kernel, out_shape=(jax.ShapeDtypeStruct((384, 128),...]
where the time goes in v3:
time: 47.7 us; the launch traced here: 47.6 us
  Pallas kernels  44.8 us (94%)
  local copies, waits for them, and re-layouts  2.16 us (5%)
  between operations  0.65 us (1%)
    pallas_call x1, Pallas kernels, layer(): pl.pallas_call(layer_kernel, out_shape=(jax.ShapeDtypeStruct((384, 128),...  44.8 us
    unnamed x4, local copies, waits for them, and re-layouts  2.16 us

profile of v3, /device:TPU:1, one launch (start us, length us, event | category | flops | bytes accessed | tf_op | source)
XLA Modules:
  0.0 47.6 jit_solution(8698268699197529887)
XLA Ops:
  0.6 44.8 %layer.1 = (bf16[384,128]{1,0:T(8,128)(2,1)}, f32[3,2,8,8]{3,2,1,0:T(8,128)}) custom-call(bf16[3,2,8,8,128]{4,3,2,1,0:T(8,128)(2,1)} %feat_hbm.1, f32[3,2,8,24]{3,2,1,0:T(8,128)} %place_hbm.1, s32[3,2,8,24]{3,2,1,0:T(8,128)} %anchor_hbm.1, s32[3,2,8,8]{3,2,1,0:T(8,128)} %species_hbm.1, s32[3,2,8,512]{3,2,1,0:T(8,128)} %nbr_hbm.1, s32[3,2,8,8]{3,2,1,0:T(8,128)} %count_hbm.1, ...), custom_call_target="tpu_custom_call" | custom-call | flops 4000000000 | bytes 4000000 | tf_op jit(solution)/shard_map/layer/pallas_call | solution.py:829
  45.4 0.0 copy-start
  45.4 1.5 %copy.26 = bf16[3,2,8,8,128]{4,3,2,1,0:T(8,128)(2,1)} copy(bf16[3,2,8,8,128]{4,3,2,1,0:T(8,128)(2,1)} %bitcast.2) | data formatting | bytes 196608
  47.0 0.0 copy-done
  47.0 0.6 %copy.27 = f32[3,2,8,8]{3,2,1,0:T(8,128)} copy(f32[3,2,8,8]{3,2,1,0:T(8,128)S(1)} %copy-done) | data formatting | bytes 3072
Async XLA Ops:
  45.4 1.6 %copy-start = (f32[3,2,8,8]{3,2,1,0:T(8,128)S(1)}, f32[3,2,8,8]{3,2,1,0:T(8,128)}, u32[]{:S(2)}) copy-start(f32[3,2,8,8]{3,2,1,0:T(8,128)} %get-tuple-element.9) | copy-start | bytes 4612

commit v4 on v3

--- a/solution.py
+++ b/solution.py
@@ -116,13 +116,13 @@
     wn_hbm,
     ws_hbm,
     wr_hbm,
-    rate_ref,
+    rate_hbm,
     w1_hbm,
     w2_hbm,
     wv_hbm,
     wo_hbm,
     wc_hbm,
-    kind_ref,
+    kind_hbm,
     bz_hbm,
     by_hbm,
     bx_hbm,
@@ -151,7 +151,10 @@
     gz_ref,
     wv_ref,
     wo_ref,
+    kind_ref,
+    rate_ref,
     load_sem,
+    small_sem,
     pos_ref,
     feat_ext,
     pos_ext,
@@ -202,6 +205,78 @@
     ix, iy, iz = lax.axis_index("gx"), lax.axis_index("gy"), lax.axis_index("gz")
     me = iy * 4 + iz
     barrier = pltpu.get_barrier_semaphore()
+    def yz_peer(r):
+        other = lax.rem(me + r, 16)
+        return other, (ix, other // 4, lax.rem(other, 4))
+
+    def x_peer(r):
+        other = lax.rem(ix + r, 8)
+        return other, (other, iy, iz)
+
+    def greet_yz(r, c):
+        pl.semaphore_signal(barrier, inc=1, device_id=yz_peer(r)[1], device_id_type=MESH)
+        return c
+
+    def greet_x(r, c):
+        pl.semaphore_signal(barrier, inc=1, device_id=x_peer(r)[1], device_id_type=MESH)
+        return c
+
+    lax.fori_loop(1, 16, greet_yz, 0)
+    lax.fori_loop(1, 8, greet_x, 0)
+
+    def halo_peer(index):
+        ox, oy, oz = index // 9 - 1, index // 3 % 3 - 1, index % 3 - 1
+        return (lax.rem(ix + ox + 8, 8), lax.rem(iy + oy + 4, 4), lax.rem(iz + oz + 4, 4))
+
+    def halo_span(step, cells):
+        if step == 0:
+            return pl.ds(0, cells), pl.ds(1, cells)
+        return (pl.ds(cells - 1, 1), pl.ds(0, 1)) if step > 0 else (pl.ds(0, 1), pl.ds(cells + 1, 1))
+
+    halo_ids = [n for n in range(27) if n != 13]
+    near_ids = [n for n in halo_ids if n // 9 == 1]
+    far_ids = [n for n in halo_ids if n // 9 != 1]
+
+    def halo_copies(index):
+        steps = (index // 9 - 1, index // 3 % 3 - 1, index % 3 - 1)
+        spans = [halo_span(step, cells) for step, cells in zip(steps, (3, 2, 8))]
+        group = 0 if steps[0] == 0 else 1
+        source = tuple(span[0] for span in spans)
+        target = tuple(span[1] for span in spans)
+        row = {0: pl.ds(1, 2), 1: pl.ds(0, 1), -1: pl.ds(3, 1)}[steps[2]]
+        return [
+            pltpu.make_async_remote_copy(
+                src_ref=src.at[source[:2] + (from_z,)],
+                dst_ref=dst.at[target[:2] + (to_z,)],
+                send_sem=send.at[group],
+                recv_sem=recv.at[group],
+                device_id=halo_peer(index),
+                device_id_type=MESH,
+            )
+            for src, dst, send, recv, from_z, to_z in (
+                (feat_ref, feat_ext, sf, rf, source[2], target[2]),
+                (pos_ref, pos_ext, sq, rq, row, row),
+            )
+        ]
+
+    def halo_group(group):
+        cells = (pl.ds(0, 2 if group else 3), pl.ds(0, 4), pl.ds(0, 10 if group else 6))
+        rows = (pl.ds(0, 2 if group else 3), pl.ds(0, 4), pl.ds(0, 4 if group else 3))
+        return [
+            pltpu.make_async_remote_copy(
+                src_ref=ext.at[part],
+                dst_ref=ext.at[part],
+                send_sem=send.at[group],
+                recv_sem=recv.at[group],
+                device_id=halo_peer(0),
+                device_id_type=MESH,
+            )
+            for ext, part, send, recv in ((feat_ext, cells, sf, rf), (pos_ext, rows, sq, rq))
+        ]
+
+    for index in halo_ids:
+        pl.semaphore_signal(barrier, inc=1, device_id=halo_peer(index), device_id_type=MESH)
+
     pairs = (
         (feat_hbm, feat_ref),
         (place_hbm, place_ref),
@@ -227,66 +302,14 @@
     loads = [
         pltpu.make_async_copy(src, dst, load_sem.at[n]) for n, (src, dst) in enumerate(pairs)
     ]
-    for load in loads:
+    small = [
+        pltpu.make_async_copy(kind_hbm, kind_ref, small_sem.at[0]),
+        pltpu.make_async_copy(rate_hbm, rate_ref, small_sem.at[1]),
+    ]
+    for load in small + loads:
         load.start()
 
-    def yz_peer(r):
-        other = lax.rem(me + r, 16)
-        return other, (ix, other // 4, lax.rem(other, 4))
-
-    def x_peer(r):
-        other = lax.rem(ix + r, 8)
-        return other, (other, iy, iz)
-
-    def greet_yz(r, c):
-        pl.semaphore_signal(barrier, inc=1, device_id=yz_peer(r)[1], device_id_type=MESH)
-        return c
-
-    def greet_x(r, c):
-        pl.semaphore_signal(barrier, inc=1, device_id=x_peer(r)[1], device_id_type=MESH)
-        return c
-
-    lax.fori_loop(1, 16, greet_yz, 0)
-    lax.fori_loop(1, 8, greet_x, 0)
-
-    def halo_peer(index):
-        ox, oy, oz = index // 9 - 1, index // 3 % 3 - 1, index % 3 - 1
-        return (lax.rem(ix + ox + 8, 8), lax.rem(iy + oy + 4, 4), lax.rem(iz + oz + 4, 4))
-
-    def halo_span(step, cells):
-        if step == 0:
-            return pl.ds(0, cells), pl.ds(1, cells)
-        return (pl.ds(cells - 1, 1), pl.ds(0, 1)) if step > 0 else (pl.ds(0, 1), pl.ds(cells + 1, 1))
-
-    halo_ids = [n for n in range(27) if n != 13]
-    near_ids = [n for n in halo_ids if n // 9 == 1]
-    far_ids = [n for n in halo_ids if n // 9 != 1]
-
-    def halo_copies(index):
-        steps = (index // 9 - 1, index // 3 % 3 - 1, index % 3 - 1)
-        spans = [halo_span(step, cells) for step, cells in zip(steps, (3, 2, 8))]
-        source = tuple(span[0] for span in spans)
-        target = tuple(span[1] for span in spans)
-        row = {0: pl.ds(1, 2), 1: pl.ds(0, 1), -1: pl.ds(3, 1)}[steps[2]]
-        return [
-            pltpu.make_async_remote_copy(
-                src_ref=src.at[source[:2] + (from_z,)],
-                dst_ref=dst.at[target[:2] + (to_z,)],
-                send_sem=send.at[index],
-                recv_sem=recv.at[index],
-                device_id=halo_peer(index),
-                device_id_type=MESH,
-            )
-            for src, dst, send, recv, from_z, to_z in (
-                (feat_ref, feat_ext, sf, rf, source[2], target[2]),
-                (pos_ref, pos_ext, sq, rq, row, row),
-            )
-        ]
-
-    for index in halo_ids:
-        pl.semaphore_signal(barrier, inc=1, device_id=halo_peer(index), device_id_type=MESH)
-
-    for load in loads[:5]:
+    for load in small + loads[:5]:
         load.wait()
 
     sub_l = lax.broadcasted_iota(jnp.int32, (8, 128), 0)
@@ -533,7 +556,8 @@
     lane_384 = lax.broadcasted_iota(jnp.int32, (8, 128), 1)
 
     def spread(turn, total):
-        source = lax.rem(iz + turn, 4)
+        step = jnp.where(turn < 2, turn, 5 - turn)
+        source = lax.rem(iz + step, 4)
         for u in range(2):
             atom_wait(source, u)
         low_part_, high_part_ = rx_atoms[source, 0], rx_atoms[source, 1]
@@ -558,53 +582,36 @@
         ]
         both = jnp.concatenate(blocks, axis=0)
         stencil[source] = both
-        return total + dot3((high, low), split(both * rows[6:7]), NT)
-
-    lines = lax.fori_loop(0, 4, spread, jnp.zeros((256, 128), f32))
-    spectrum = dot3((bz_ref[0], bz_ref[1]), split(lines))
+        return total + dot3(split(both * rows[6:7]), (high, low), NT)
+
+    lines = lax.fori_loop(0, 4, spread, jnp.zeros((128, 256), f32))
+    spectrum = dot3((bz_ref[0], bz_ref[1]), split(lines), NT)
     tx_b[...] = spectrum.reshape(16, 16, 128)
     rx_b[me] = tx_b[me]
 
     def exchange(tx, rx, send, recv, peer, count, mine):
-        def copy(r):
+        def start(r, c):
             other, where = peer(r)
-            return pltpu.make_async_remote_copy(
+            pltpu.make_async_remote_copy(
                 src_ref=tx.at[other],
                 dst_ref=rx.at[mine],
-                send_sem=send.at[other],
-                recv_sem=recv.at[mine],
+                send_sem=send,
+                recv_sem=recv,
                 device_id=where,
                 device_id_type=MESH,
-            )
-
-        def arrival(r):
-            other, where = peer(r)
-            return pltpu.make_async_remote_copy(
-                src_ref=tx.at[other],
-                dst_ref=rx.at[other],
-                send_sem=send.at[other],
-                recv_sem=recv.at[other],
-                device_id=where,
-                device_id_type=MESH,
-            )
-
-        def start(r, c):
-            copy(r).start()
+            ).start()
             return c
 
-        def wait(r, c):
-            arrival(r).wait_recv()
-            return c
-
-        def drain(r, c):
-            copy(r).wait_send()
-            return c
-
         lax.fori_loop(1, count, start, 0)
-        return (
-            lambda: lax.fori_loop(1, count, wait, 0),
-            lambda: lax.fori_loop(1, count, drain, 0),
+        whole = pltpu.make_async_remote_copy(
+            src_ref=tx.at[pl.ds(0, count - 1)],
+            dst_ref=rx.at[pl.ds(0, count - 1)],
+            send_sem=send,
+            recv_sem=recv,
+            device_id=peer(1)[1],
+            device_id_type=MESH,
         )
+        return whole.wait_recv, whole.wait_send
 
     arrive_b, drain_b = exchange(tx_b, rx_b, sb, rb, yz_peer, 16, me)
 
@@ -634,9 +641,8 @@
         for t in range(6):
             pos_tab[n, 8 * t : 8 * t + 8, :] = jnp.where(half_sub == 0, near[2 * t], near[2 * t + 1])
 
-    for index in near_ids:
-        for copy in halo_copies(26 - index):
-            copy.wait_recv()
+    for copy in halo_group(0):
+        copy.wait_recv()
     for sx in (1, 2, 3):
         lay_strips(sx)
     for n in (2, 3):
@@ -667,9 +673,8 @@
         value = gain_yz * gx_ref[0, 0:1, lanes] / (total + 1.0 / 1024.0)
         greens.append(jnp.where(total == 0.0, 0.0, value))
     green = jnp.concatenate(greens, axis=1)
-    for index in far_ids:
-        for copy in halo_copies(26 - index):
-            copy.wait_recv()
+    for copy in halo_group(1):
+        copy.wait_recv()
     for sx in (0, 4):
         lay_strips(sx)
     for n in (0, 1, 4, 5):
@@ -776,8 +781,8 @@
     drain_c()
     drain_c2()
     drain_b2()
-    for index in halo_ids:
-        for copy in halo_copies(index):
+    for group in range(2):
+        for copy in halo_group(group):
             copy.wait_send()
 
     def part_wait(half, to_z, step_y):
@@ -821,8 +826,7 @@
     dma = pltpu.SemaphoreType.DMA
     tables = [jnp.asarray(t) for t in ewald_tables()]
     hbm = pl.BlockSpec(memory_space=pltpu.HBM)
-    smem = pl.BlockSpec(memory_space=pltpu.SMEM)
-    specs = [hbm] * 9 + [smem] + [hbm] * 5 + [smem] + [hbm] * 6
+    specs = [hbm] * 22
     shapes = [operands[n] for n in (0, 1, 2, 3, 14, 6, 7, 8, 10, 11, 4, 5)] + tables
     shapes += [operands[n] for n in (12, 13)]
     staged = [pltpu.VMEM(x.shape, x.dtype) for x in shapes]
@@ -836,7 +840,10 @@
         out_specs=(vm, vm),
         scratch_shapes=staged
         + [
+            pltpu.SMEM((2,), f32),
+            pltpu.SMEM((8,), f32),
             dma((20,)),
+            dma((2,)),
             pltpu.VMEM((3, 2, 4, 1, 128), f32),
             pltpu.VMEM((5, 4, 10, 8, 128), bf16),
             pltpu.VMEM((5, 4, 4, 1, 128), f32),
@@ -866,27 +873,20 @@
             pltpu.VMEM((2, 4, 1, 256), f32),
             dma((2, 4)),
             dma((4, 2)),
-            dma((16,)),
-            dma((16,)),
-            dma((8,)),
-            dma((8,)),
-            dma((8,)),
-            dma((8,)),
-            dma((16,)),
-            dma((16,)),
+            *[pltpu.SemaphoreType.DMA] * 8,
             dma((4, 2)),
             dma((2, 4)),
-            dma((27,)),
-            dma((27,)),
-            dma((27,)),
-            dma((27,)),
+            dma((2,)),
+            dma((2,)),
+            dma((2,)),
+            dma((2,)),
         ],
         compiler_params=pltpu.CompilerParams(
-            collective_id=0, has_side_effects=True, vmem_limit_bytes=67043328
+            collective_id=0, has_side_effects=True, vmem_limit_bytes=48 * 1024 * 1024
         ),
         cost_estimate=pl.CostEstimate(flops=4 * 10**9, bytes_accessed=4 * 10**6, transcendentals=10**7),
         name="layer",
-    )(*operands, *tables)
+    )(*[pltpu.with_memory_space_constraint(x, pltpu.HBM) for x in (*operands, *tables)])
 
 
 def shards(

time: 47.7 us -> 43.5 us (0.912)
  Pallas kernels: 44.8 us -> 41.5 us
  local copies, waits for them, and re-layouts: 2.16 us -> 1.25 us
    pallas_call x1, Pallas kernels: 44.8 us -> 41.5 us  [layer(): pl.pallas_call(layer_kernel, out_shape=(jax.ShapeDtypeStruct((384, 128),...]
    unnamed x4 -> x2, local copies, waits for them, and re-layouts: 2.16 us -> 1.25 us
where the time goes in v4:
time: 43.5 us; the launch traced here: 43.4 us
  Pallas kernels  41.5 us (95%)
  local copies, waits for them, and re-layouts  1.25 us (3%)
  between operations  0.65 us (1%)
    pallas_call x1, Pallas kernels, layer(): pl.pallas_call(layer_kernel, out_shape=(jax.ShapeDtypeStruct((384, 128),...  41.5 us
    unnamed x2, local copies, waits for them, and re-layouts  1.25 us

profile of v4, /device:TPU:1, one launch (start us, length us, event | category | flops | bytes accessed | tf_op | source)
XLA Modules:
  0.0 43.4 jit_solution(11748937496907304682)
XLA Ops:
  0.6 41.5 %layer.1 = (bf16[384,128]{1,0:T(8,128)(2,1)S(1)}, f32[3,2,8,8]{3,2,1,0:T(8,128)S(1)}) custom-call(bf16[3,2,8,8,128]{4,3,2,1,0:T(8,128)(2,1)} %feat_hbm.1, f32[3,2,8,24]{3,2,1,0:T(8,128)} %place_hbm.1, s32[3,2,8,24]{3,2,1,0:T(8,128)} %anchor_hbm.1, s32[3,2,8,8]{3,2,1,0:T(8,128)} %species_hbm.1, s32[3,2,8,512]{3,2,1,0:T(8,128)} %nbr_hbm.1, ...), custom_call_target="tpu_custom_call" | custom-call | flops 4000000000 | bytes 4000000 | tf_op jit(solution)/shard_map/layer/pallas_call | solution.py:833
  42.1 0.6 %copy.26 = bf16[3,2,8,8,128]{4,3,2,1,0:T(8,128)(2,1)} copy(bf16[3,2,8,8,128]{4,3,2,1,0:T(8,128)(2,1)S(1)} %bitcast.2) | data formatting | bytes 196608
  42.8 0.6 %copy.27 = f32[3,2,8,8]{3,2,1,0:T(8,128)} copy(f32[3,2,8,8]{3,2,1,0:T(8,128)S(1)} %get-tuple-element.9) | data formatting | bytes 3072

commit v5 on v4

--- a/solution.py
+++ b/solution.py
@@ -180,6 +180,7 @@
     rx_c2,
     tx_b2,
     rx_b2,
+    flat_b,
     parts,
     rx_parts,
     sa,
@@ -586,7 +587,7 @@
 
     lines = lax.fori_loop(0, 4, spread, jnp.zeros((128, 256), f32))
     spectrum = dot3((bz_ref[0], bz_ref[1]), split(lines), NT)
-    tx_b[...] = spectrum.reshape(16, 16, 128)
+    tx_b[...] = spectrum.astype(bf16).reshape(16, 16, 128)
     rx_b[me] = tx_b[me]
 
     def exchange(tx, rx, send, recv, peer, count, mine):
@@ -649,13 +650,15 @@
         lay_column(n)
     half_columns(CUTS[0], CUTS[1])
     arrive_b()
-    flat_b = rx_b.reshape(256, 128)
+    flat_b[...] = rx_b[...].astype(f32).reshape(256, 128)
     columns = []
     for group in range(4):
         pieces = [flat_b[pl.ds(group * 4 + k, 16, 16), :] for k in range(4)]
         columns.append(jnp.concatenate([swap_groups(pieces, i) for i in range(4)], axis=0))
     lines_y = jnp.concatenate(columns, axis=1)
-    modes_y = dot3((by_ref[0, 0], by_ref[0, 1]), split(lines_y))
+    lines_y = lines_y.astype(bf16)
+    modes_y = jnp.dot(by_ref[0, 0], lines_y, preferred_element_type=f32)
+    modes_y = modes_y + jnp.dot(by_ref[0, 1], lines_y, preferred_element_type=f32)
     tx_c[...] = modes_y.reshape(8, 8, 512)
     rx_c[ix] = tx_c[ix]
     arrive_c, drain_c = exchange(tx_c, rx_c, sc, rc, x_peer, 8, ix)
@@ -709,27 +712,25 @@
     half_columns(CUTS[2], CUTS[3])
     arrive_c2()
     back_y = dot3((by_ref[1, 0], by_ref[1, 1]), split(rx_c2[...].reshape(64, 512)))
-    flat_b2 = tx_b2.reshape(256, 128)
     for group in range(4):
         pieces = [back_y[16 * i : 16 * i + 16, group * 128 : group * 128 + 128] for i in range(4)]
         for k in range(4):
-            flat_b2[pl.ds(group * 4 + k, 16, 16), :] = swap_groups(pieces, k)
+            flat_b[pl.ds(group * 4 + k, 16, 16), :] = swap_groups(pieces, k)
+    tx_b2[...] = flat_b[...].astype(bf16).reshape(16, 16, 128)
     rx_b2[me] = tx_b2[me]
     arrive_b2, drain_b2 = exchange(tx_b2, rx_b2, sb2, rb2, yz_peer, 16, me)
     half_columns(CUTS[3], CUTS[4])
     arrive_b2()
-    back_z = rx_b2[...].reshape(256, 128).T
-    potential = split(dot3(split(back_z), (bz_ref[0], bz_ref[1])))
-
-    def sample(source, c):
-        values = dot3(potential, (z_high[source], z_low[source]))
-        sums_ = jnp.sum(values * stencil[source], axis=0, keepdims=True)
-        parts[2 * source] = sums_[:, 0:256]
-        tail = jnp.broadcast_to(sums_[:, 128:384], (8, 256))
-        parts[2 * source + 1] = pltpu.roll(tail, 192, 1)[0:1]
-        return c
-
-    lax.fori_loop(0, 4, sample, 0)
+    back_z = rx_b2[...].astype(f32).reshape(256, 128).T.astype(bf16)
+    lines_z = jnp.dot(back_z, bz_ref[0], preferred_element_type=f32)
+    potential = split(lines_z + jnp.dot(back_z, bz_ref[1], preferred_element_type=f32))
+
+    sampled = [dot3(potential, (z_high[n], z_low[n])) for n in range(4)]
+    for n in range(4):
+        total = jnp.sum(sampled[n] * stencil[n], axis=0, keepdims=True)
+        parts[2 * n] = total[:, 0:256]
+        tail = jnp.broadcast_to(total[:, 128:384], (8, 256))
+        parts[2 * n + 1] = pltpu.roll(tail, 192, 1)[0:1]
 
     def part_copy(s, u):
         return pltpu.make_async_remote_copy(
@@ -861,14 +862,15 @@
             pltpu.VMEM((4, 256, 384), bf16),
             pltpu.VMEM((4, 256, 384), bf16),
             pltpu.VMEM((4, 128, 384), f32),
-            pltpu.VMEM((16, 16, 128), f32),
-            pltpu.VMEM((16, 16, 128), f32),
+            pltpu.VMEM((16, 16, 128), bf16),
+            pltpu.VMEM((16, 16, 128), bf16),
             pltpu.VMEM((8, 8, 512), f32),
             pltpu.VMEM((8, 8, 512), f32),
             pltpu.VMEM((8, 8, 512), f32),
             pltpu.VMEM((8, 8, 512), f32),
-            pltpu.VMEM((16, 16, 128), f32),
-            pltpu.VMEM((16, 16, 128), f32),
+            pltpu.VMEM((16, 16, 128), bf16),
+            pltpu.VMEM((16, 16, 128), bf16),
+            pltpu.VMEM((256, 128), f32),
             pltpu.VMEM((8, 1, 256), f32),
             pltpu.VMEM((2, 4, 1, 256), f32),
             dma((2, 4)),

time: 43.5 us -> 42.3 us (0.972)
  Pallas kernels: 41.5 us -> 40.3 us
    pallas_call x1, Pallas kernels: 41.5 us -> 40.3 us  [layer(): pl.pallas_call(layer_kernel, out_shape=(jax.ShapeDtypeStruct((384, 128),...]
where the time goes in v5:
time: 42.3 us; the launch traced here: 42.2 us
  Pallas kernels  40.3 us (95%)
  local copies, waits for them, and re-layouts  1.25 us (3%)
  between operations  0.65 us (2%)
    pallas_call x1, Pallas kernels, layer(): pl.pallas_call(layer_kernel, out_shape=(jax.ShapeDtypeStruct((384, 128),...  40.3 us
    unnamed x2, local copies, waits for them, and re-layouts  1.25 us

profile of v5, /device:TPU:1, one launch (start us, length us, event | category | flops | bytes accessed | tf_op | source)
XLA Modules:
  0.0 42.2 jit_solution(261053839988505066)
XLA Ops:
  0.6 40.3 %layer.1 = (bf16[384,128]{1,0:T(8,128)(2,1)S(1)}, f32[3,2,8,8]{3,2,1,0:T(8,128)S(1)}) custom-call(bf16[3,2,8,8,128]{4,3,2,1,0:T(8,128)(2,1)} %feat_hbm.1, f32[3,2,8,24]{3,2,1,0:T(8,128)} %place_hbm.1, s32[3,2,8,24]{3,2,1,0:T(8,128)} %anchor_hbm.1, s32[3,2,8,8]{3,2,1,0:T(8,128)} %species_hbm.1, s32[3,2,8,512]{3,2,1,0:T(8,128)} %nbr_hbm.1, ...), custom_call_target="tpu_custom_call" | custom-call | flops 4000000000 | bytes 4000000 | tf_op jit(solution)/shard_map/layer/pallas_call | solution.py:834
  40.9 0.6 %copy.26 = bf16[3,2,8,8,128]{4,3,2,1,0:T(8,128)(2,1)} copy(bf16[3,2,8,8,128]{4,3,2,1,0:T(8,128)(2,1)S(1)} %bitcast.2) | data formatting | bytes 196608
  41.6 0.6 %copy.27 = f32[3,2,8,8]{3,2,1,0:T(8,128)} copy(f32[3,2,8,8]{3,2,1,0:T(8,128)S(1)} %get-tuple-element.9) | data formatting | bytes 3072

commit v6 on v5

--- a/solution.py
+++ b/solution.py
@@ -75,7 +75,9 @@
     def one(u, v):
         return lax.dot_general(u, v, dims, preferred_element_type=jnp.float32)
 
-    return one(a[0], b[0]) + (one(a[0], b[1]) + one(a[1], b[0]))
+    rows = a[0].shape[0]
+    both = one(jnp.concatenate([a[0], a[1]], axis=0), b[0])
+    return both[0:rows] + (one(a[0], b[1]) + both[rows : 2 * rows])
 
 
 def swap_groups(pieces, shift):
@@ -181,6 +183,7 @@
     tx_b2,
     rx_b2,
     flat_b,
+    flat_c,
     parts,
     rx_parts,
     sa,
@@ -206,78 +209,6 @@
     ix, iy, iz = lax.axis_index("gx"), lax.axis_index("gy"), lax.axis_index("gz")
     me = iy * 4 + iz
     barrier = pltpu.get_barrier_semaphore()
-    def yz_peer(r):
-        other = lax.rem(me + r, 16)
-        return other, (ix, other // 4, lax.rem(other, 4))
-
-    def x_peer(r):
-        other = lax.rem(ix + r, 8)
-        return other, (other, iy, iz)
-
-    def greet_yz(r, c):
-        pl.semaphore_signal(barrier, inc=1, device_id=yz_peer(r)[1], device_id_type=MESH)
-        return c
-
-    def greet_x(r, c):
-        pl.semaphore_signal(barrier, inc=1, device_id=x_peer(r)[1], device_id_type=MESH)
-        return c
-
-    lax.fori_loop(1, 16, greet_yz, 0)
-    lax.fori_loop(1, 8, greet_x, 0)
-
-    def halo_peer(index):
-        ox, oy, oz = index // 9 - 1, index // 3 % 3 - 1, index % 3 - 1
-        return (lax.rem(ix + ox + 8, 8), lax.rem(iy + oy + 4, 4), lax.rem(iz + oz + 4, 4))
-
-    def halo_span(step, cells):
-        if step == 0:
-            return pl.ds(0, cells), pl.ds(1, cells)
-        return (pl.ds(cells - 1, 1), pl.ds(0, 1)) if step > 0 else (pl.ds(0, 1), pl.ds(cells + 1, 1))
-
-    halo_ids = [n for n in range(27) if n != 13]
-    near_ids = [n for n in halo_ids if n // 9 == 1]
-    far_ids = [n for n in halo_ids if n // 9 != 1]
-
-    def halo_copies(index):
-        steps = (index // 9 - 1, index // 3 % 3 - 1, index % 3 - 1)
-        spans = [halo_span(step, cells) for step, cells in zip(steps, (3, 2, 8))]
-        group = 0 if steps[0] == 0 else 1
-        source = tuple(span[0] for span in spans)
-        target = tuple(span[1] for span in spans)
-        row = {0: pl.ds(1, 2), 1: pl.ds(0, 1), -1: pl.ds(3, 1)}[steps[2]]
-        return [
-            pltpu.make_async_remote_copy(
-                src_ref=src.at[source[:2] + (from_z,)],
-                dst_ref=dst.at[target[:2] + (to_z,)],
-                send_sem=send.at[group],
-                recv_sem=recv.at[group],
-                device_id=halo_peer(index),
-                device_id_type=MESH,
-            )
-            for src, dst, send, recv, from_z, to_z in (
-                (feat_ref, feat_ext, sf, rf, source[2], target[2]),
-                (pos_ref, pos_ext, sq, rq, row, row),
-            )
-        ]
-
-    def halo_group(group):
-        cells = (pl.ds(0, 2 if group else 3), pl.ds(0, 4), pl.ds(0, 10 if group else 6))
-        rows = (pl.ds(0, 2 if group else 3), pl.ds(0, 4), pl.ds(0, 4 if group else 3))
-        return [
-            pltpu.make_async_remote_copy(
-                src_ref=ext.at[part],
-                dst_ref=ext.at[part],
-                send_sem=send.at[group],
-                recv_sem=recv.at[group],
-                device_id=halo_peer(0),
-                device_id_type=MESH,
-            )
-            for ext, part, send, recv in ((feat_ext, cells, sf, rf), (pos_ext, rows, sq, rq))
-        ]
-
-    for index in halo_ids:
-        pl.semaphore_signal(barrier, inc=1, device_id=halo_peer(index), device_id_type=MESH)
-
     pairs = (
         (feat_hbm, feat_ref),
         (place_hbm, place_ref),
@@ -307,10 +238,85 @@
         pltpu.make_async_copy(kind_hbm, kind_ref, small_sem.at[0]),
         pltpu.make_async_copy(rate_hbm, rate_ref, small_sem.at[1]),
     ]
-    for load in small + loads:
+    for load in loads[:5] + small[:1]:
         load.start()
 
-    for load in small + loads[:5]:
+    def yz_peer(r):
+        other = lax.rem(me + r, 16)
+        return other, (ix, other // 4, lax.rem(other, 4))
+
+    def x_peer(r):
+        other = lax.rem(ix + r, 8)
+        return other, (other, iy, iz)
+
+    def greet_yz(r, c):
+        pl.semaphore_signal(barrier, inc=1, device_id=yz_peer(r)[1], device_id_type=MESH)
+        return c
+
+    def greet_x(r, c):
+        pl.semaphore_signal(barrier, inc=1, device_id=x_peer(r)[1], device_id_type=MESH)
+        return c
+
+    lax.fori_loop(1, 16, greet_yz, 0)
+    lax.fori_loop(1, 8, greet_x, 0)
+
+    def halo_peer(index):
+        ox, oy, oz = index // 9 - 1, index // 3 % 3 - 1, index % 3 - 1
+        return (lax.rem(ix + ox + 8, 8), lax.rem(iy + oy + 4, 4), lax.rem(iz + oz + 4, 4))
+
+    def halo_span(step, cells):
+        if step == 0:
+            return pl.ds(0, cells), pl.ds(1, cells)
+        return (pl.ds(cells - 1, 1), pl.ds(0, 1)) if step > 0 else (pl.ds(0, 1), pl.ds(cells + 1, 1))
+
+    halo_ids = [n for n in range(27) if n != 13]
+    near_ids = [n for n in halo_ids if n // 9 == 1]
+    far_ids = [n for n in halo_ids if n // 9 != 1]
+
+    def halo_copies(index):
+        steps = (index // 9 - 1, index // 3 % 3 - 1, index % 3 - 1)
+        spans = [halo_span(step, cells) for step, cells in zip(steps, (3, 2, 8))]
+        group = 0 if steps[0] == 0 else 1
+        source = tuple(span[0] for span in spans)
+        target = tuple(span[1] for span in spans)
+        row = {0: pl.ds(1, 2), 1: pl.ds(0, 1), -1: pl.ds(3, 1)}[steps[2]]
+        return [
+            pltpu.make_async_remote_copy(
+                src_ref=src.at[source[:2] + (from_z,)],
+                dst_ref=dst.at[target[:2] + (to_z,)],
+                send_sem=send.at[group],
+                recv_sem=recv.at[group],
+                device_id=halo_peer(index),
+                device_id_type=MESH,
+            )
+            for src, dst, send, recv, from_z, to_z in (
+                (feat_ref, feat_ext, sf, rf, source[2], target[2]),
+                (pos_ref, pos_ext, sq, rq, row, row),
+            )
+        ]
+
+    def halo_group(group):
+        cells = (pl.ds(0, 2 if group else 3), pl.ds(0, 4), pl.ds(0, 10 if group else 6))
+        rows = (pl.ds(0, 2 if group else 3), pl.ds(0, 4), pl.ds(0, 4 if group else 3))
+        return [
+            pltpu.make_async_remote_copy(
+                src_ref=ext.at[part],
+                dst_ref=ext.at[part],
+                send_sem=send.at[group],
+                recv_sem=recv.at[group],
+                device_id=halo_peer(0),
+                device_id_type=MESH,
+            )
+            for ext, part, send, recv in ((feat_ext, cells, sf, rf), (pos_ext, rows, sq, rq))
+        ]
+
+    for index in far_ids:
+        if index % 9 != 4:
+            pl.semaphore_signal(
+                barrier, inc=1, device_id=halo_peer(index), device_id_type=MESH
+            )
+
+    for load in loads[:5] + small[:1]:
         load.wait()
 
     sub_l = lax.broadcasted_iota(jnp.int32, (8, 128), 0)
@@ -354,7 +360,42 @@
         tx_atoms[half, 6:7, :] = total
         tx_atoms[half, 7:8, :] = jnp.zeros((1, 256), f32)
 
-    for load in loads[5:10]:
+    pl.semaphore_wait(barrier, 38)
+
+    routes = [(0, 3, 3, 1), (0, 0, 0, 1), (0, 1, 0, 0), (0, 2, 0, 0)]
+    routes += [(1, 1, 0, 1), (1, 2, 0, 1), (1, 3, 0, 0), (1, 0, 1, 0)]
+
+    def atom_copy(half, to_z, step_y, place):
+        return pltpu.make_async_remote_copy(
+            src_ref=tx_atoms.at[half],
+            dst_ref=rx_atoms.at[iz * 2 + place],
+            send_sem=sa,
+            recv_sem=ra.at[iz, place],
+            device_id=(ix, lax.rem(iy + step_y, 4), to_z),
+            device_id_type=MESH,
+        )
+
+    for half, to_z, step_y, place in routes:
+        if step_y:
+            atom_copy(half, to_z, step_y, place).start()
+        else:
+
+            @pl.when(iz != to_z)
+            def _():
+                atom_copy(half, to_z, step_y, place).start()
+
+            @pl.when(iz == to_z)
+            def _():
+                rx_atoms[iz * 2 + place] = tx_atoms[half]
+
+    for index in near_ids:
+        for copy in halo_copies(index):
+            copy.start()
+    for load in loads[5:] + small[1:]:
+        load.start()
+    feat_ext[1:4, 1:3, 1:9] = feat_ref[...]
+    pos_ext[1:4, 1:3, 1:3] = pos_ref[:, :, 1:3]
+    for load in loads[5:] + small[1:]:
         load.wait()
     first_w[:, 0:128] = (wn_ref[...].astype(f32) * 0.5).T.astype(bf16)
     first_w[:, 128:256] = (ws_ref[...].astype(f32) * 0.5).T.astype(bf16)
@@ -380,39 +421,6 @@
     box = jnp.where(axis_sub == 0, 192.0, jnp.where(axis_sub == 1, 64.0, 256.0)).astype(f32)
     box_inv = 1.0 / box
     atom_lane = lax.broadcasted_iota(jnp.int32, (8, 128), 1) // 64
-    pl.semaphore_wait(barrier, 48)
-
-    routes = [(0, 3, 3, 1), (0, 0, 0, 1), (0, 1, 0, 0), (0, 2, 0, 0)]
-    routes += [(1, 1, 0, 1), (1, 2, 0, 1), (1, 3, 0, 0), (1, 0, 1, 0)]
-
-    def atom_copy(half, to_z, step_y, place):
-        return pltpu.make_async_remote_copy(
-            src_ref=tx_atoms.at[half],
-            dst_ref=rx_atoms.at[iz, place],
-            send_sem=sa.at[half, to_z],
-            recv_sem=ra.at[iz, place],
-            device_id=(ix, lax.rem(iy + step_y, 4), to_z),
-            device_id_type=MESH,
-        )
-
-    for half, to_z, step_y, place in routes:
-        if step_y:
-            atom_copy(half, to_z, step_y, place).start()
-        else:
-
-            @pl.when(iz != to_z)
-            def _():
-                atom_copy(half, to_z, step_y, place).start()
-
-            @pl.when(iz == to_z)
-            def _():
-                rx_atoms[iz, place] = tx_atoms[half]
-
-    for index in near_ids:
-        for copy in halo_copies(index):
-            copy.start()
-    feat_ext[1:4, 1:3, 1:9] = feat_ref[...]
-    pos_ext[1:4, 1:3, 1:3] = pos_ref[:, :, 1:3]
     def half_column(index, carry):
         later = (index - 4) // 2
         col = jnp.where(index < 4, 2 + index // 2, jnp.where(later < 2, later, later + 2))
@@ -541,8 +549,8 @@
         def _():
             pltpu.make_async_remote_copy(
                 src_ref=tx_atoms.at[0],
-                dst_ref=rx_atoms.at[s, u],
-                send_sem=sa.at[0, 0],
+                dst_ref=rx_atoms.at[s * 2 + u],
+                send_sem=sa,
                 recv_sem=ra.at[s, u],
                 device_id=(ix, from_y[u], s),
                 device_id_type=MESH,
@@ -550,18 +558,12 @@
 
     y_first = iy * 16 + iz * 4
 
-    for load in loads[10:]:
-        load.wait()
     z_ids = lax.broadcasted_iota(jnp.int32, (256, 384), 0)
     x_ids = lax.broadcasted_iota(jnp.int32, (32, 384), 0) + (ix * 24 - 1)
     lane_384 = lax.broadcasted_iota(jnp.int32, (8, 128), 1)
 
-    def spread(turn, total):
-        step = jnp.where(turn < 2, turn, 5 - turn)
-        source = lax.rem(iz + step, 4)
-        for u in range(2):
-            atom_wait(source, u)
-        low_part_, high_part_ = rx_atoms[source, 0], rx_atoms[source, 1]
+    def spread(source):
+        low_part_, high_part_ = rx_atoms[source * 2], rx_atoms[source * 2 + 1]
         moved = pltpu.roll(high_part_, 64, 1)
         rows = jnp.concatenate(
             [
@@ -583,15 +585,23 @@
         ]
         both = jnp.concatenate(blocks, axis=0)
         stencil[source] = both
-        return total + dot3(split(both * rows[6:7]), (high, low), NT)
-
-    lines = lax.fori_loop(0, 4, spread, jnp.zeros((128, 256), f32))
+        return dot3(split(both * rows[6:7]), (high, low), NT)
+
+    lines = None
+    for steps in ((1, 3), (0, 2)):
+        sources = [lax.rem(iz + step, 4) for step in steps]
+        for source in sources:
+            for u in range(2):
+                atom_wait(source, u)
+        for source in sources:
+            part = spread(source)
+            lines = part if lines is None else lines + part
     spectrum = dot3((bz_ref[0], bz_ref[1]), split(lines), NT)
-    tx_b[...] = spectrum.astype(bf16).reshape(16, 16, 128)
+    tx_b[...] = spectrum.reshape(16, 16, 128)
     rx_b[me] = tx_b[me]
 
     def exchange(tx, rx, send, recv, peer, count, mine):
-        def start(r, c):
+        for r in range(1, count):
             other, where = peer(r)
             pltpu.make_async_remote_copy(
                 src_ref=tx.at[other],
@@ -601,9 +611,6 @@
                 device_id=where,
                 device_id_type=MESH,
             ).start()
-            return c
-
-        lax.fori_loop(1, count, start, 0)
         whole = pltpu.make_async_remote_copy(
             src_ref=tx.at[pl.ds(0, count - 1)],
             dst_ref=rx.at[pl.ds(0, count - 1)],
@@ -650,15 +657,13 @@
         lay_column(n)
     half_columns(CUTS[0], CUTS[1])
     arrive_b()
-    flat_b[...] = rx_b[...].astype(f32).reshape(256, 128)
+    rows_b = rx_b.reshape(256, 128)
     columns = []
     for group in range(4):
-        pieces = [flat_b[pl.ds(group * 4 + k, 16, 16), :] for k in range(4)]
+        pieces = [rows_b[pl.ds(group * 4 + k, 16, 16), :] for k in range(4)]
         columns.append(jnp.concatenate([swap_groups(pieces, i) for i in range(4)], axis=0))
     lines_y = jnp.concatenate(columns, axis=1)
-    lines_y = lines_y.astype(bf16)
-    modes_y = jnp.dot(by_ref[0, 0], lines_y, preferred_element_type=f32)
-    modes_y = modes_y + jnp.dot(by_ref[0, 1], lines_y, preferred_element_type=f32)
+    modes_y = dot3((by_ref[0, 0], by_ref[0, 1]), split(lines_y))
     tx_c[...] = modes_y.reshape(8, 8, 512)
     rx_c[ix] = tx_c[ix]
     arrive_c, drain_c = exchange(tx_c, rx_c, sc, rc, x_peer, 8, ix)
@@ -706,12 +711,15 @@
                 back_x[(group * 4 + k) * 8 : (group * 4 + k) * 8 + 8, half * 128 : half * 128 + 128]
                 for k in range(4)
             ]
-            tx_c2[g, :, group * 128 : group * 128 + 128] = swap_groups(pieces, g % 4)
+            flat_c[g, :, group * 128 : group * 128 + 128] = swap_groups(pieces, g % 4)
+    tx_c2[...] = flat_c[...].astype(bf16)
     rx_c2[ix] = tx_c2[ix]
     arrive_c2, drain_c2 = exchange(tx_c2, rx_c2, sc2, rc2, x_peer, 8, ix)
     half_columns(CUTS[2], CUTS[3])
     arrive_c2()
-    back_y = dot3((by_ref[1, 0], by_ref[1, 1]), split(rx_c2[...].reshape(64, 512)))
+    lines_y2 = rx_c2[...].astype(f32).reshape(64, 512).astype(bf16)
+    back_y = jnp.dot(by_ref[1, 0], lines_y2, preferred_element_type=f32)
+    back_y = back_y + jnp.dot(by_ref[1, 1], lines_y2, preferred_element_type=f32)
     for group in range(4):
         pieces = [back_y[16 * i : 16 * i + 16, group * 128 : group * 128 + 128] for i in range(4)]
         for k in range(4):
@@ -735,9 +743,9 @@
     def part_copy(s, u):
         return pltpu.make_async_remote_copy(
             src_ref=parts.at[2 * s + u],
-            dst_ref=rx_parts.at[from_half[u], iz],
-            send_sem=sp.at[s, u],
-            recv_sem=rp.at[from_half[u], iz],
+            dst_ref=rx_parts.at[from_half[u] * 4 + iz],
+            send_sem=sp,
+            recv_sem=rp,
             device_id=(ix, from_y[u], s),
             device_id_type=MESH,
         )
@@ -751,7 +759,7 @@
 
             @pl.when((s == iz) & (from_y[u] == iy))
             def _():
-                rx_parts[from_half[u], iz] = parts[2 * s + u]
+                rx_parts[from_half[u] * 4 + iz] = parts[2 * s + u]
 
     half_columns(CUTS[4], 12)
     wv = wv_ref[...]
@@ -769,15 +777,25 @@
         feat_ref[...].astype(f32).reshape(384, 128) + jnp.dot(update, wo_ref[...], preferred_element_type=f32)
     ).astype(bf16)
 
-    for half, to_z, step_y, place in routes:
-        if step_y:
-            atom_copy(half, to_z, step_y, place).wait_send()
-        else:
-
-            @pl.when(iz != to_z)
+    def bulk(ref, send, recv, arriving):
+        for blocks, ends in ((7, 1), (6, 0)):
+
+            @pl.when(edge == ends)
             def _():
-                atom_copy(half, to_z, step_y, place).wait_send()
-
+                whole = pltpu.make_async_remote_copy(
+                    src_ref=ref.at[pl.ds(0, blocks)],
+                    dst_ref=ref.at[pl.ds(0, blocks)],
+                    send_sem=send,
+                    recv_sem=recv,
+                    device_id=yz_peer(1)[1],
+                    device_id_type=MESH,
+                )
+                if arriving:
+                    whole.wait_recv()
+                else:
+                    whole.wait_send()
+
+    bulk(rx_atoms, sa, ra.at[0, 0], False)
     drain_b()
     drain_c()
     drain_c2()
@@ -786,39 +804,19 @@
         for copy in halo_group(group):
             copy.wait_send()
 
-    def part_wait(half, to_z, step_y):
-        pltpu.make_async_remote_copy(
-            src_ref=parts.at[0],
-            dst_ref=rx_parts.at[half, to_z],
-            send_sem=sp.at[0, 0],
-            recv_sem=rp.at[half, to_z],
-            device_id=(ix, lax.rem(iy + step_y, 4), to_z),
-            device_id_type=MESH,
-        ).wait_recv()
-
-    for half, to_z, step_y, place in routes:
-        if step_y:
-            part_wait(half, to_z, step_y)
-        else:
-
-            @pl.when(iz != to_z)
-            def _():
-                part_wait(half, to_z, step_y)
+    bulk(rx_parts, sp, rp, True)
 
     for half in range(2):
-        site = (rx_parts[half, 0] + rx_parts[half, 1]) + (rx_parts[half, 2] + rx_parts[half, 3])
+        site = (rx_parts[half * 4] + rx_parts[half * 4 + 1]) + (
+            rx_parts[half * 4 + 2] + rx_parts[half * 4 + 3]
+        )
         for cx in range(3):
             block = site[:, 0:128] if cx < 2 else site[:, 128:256]
             block = jnp.broadcast_to(block, (8, 128))
             at = sub_l * 8 + lane_l % 8 + 64 * (cx % 2)
             site_ref[cx, half] = jnp.take_along_axis(block, at, axis=1)[:, 0:8]
 
-    for s in range(4):
-        for u in range(2):
-
-            @pl.when((s != iz) | (from_y[u] != iy))
-            def _():
-                part_copy(s, u).wait_send()
+    bulk(rx_parts, sp, rp, False)
 
 
 def layer(operands):
@@ -858,26 +856,25 @@
             pltpu.VMEM((8, 512), f32),
             pltpu.VMEM((4, 384, 128), f32),
             pltpu.VMEM((2, 8, 256), f32),
-            pltpu.VMEM((4, 2, 8, 256), f32),
+            pltpu.VMEM((8, 8, 256), f32),
             pltpu.VMEM((4, 256, 384), bf16),
             pltpu.VMEM((4, 256, 384), bf16),
             pltpu.VMEM((4, 128, 384), f32),
-            pltpu.VMEM((16, 16, 128), bf16),
-            pltpu.VMEM((16, 16, 128), bf16),
+            pltpu.VMEM((16, 16, 128), f32),
+            pltpu.VMEM((16, 16, 128), f32),
             pltpu.VMEM((8, 8, 512), f32),
             pltpu.VMEM((8, 8, 512), f32),
-            pltpu.VMEM((8, 8, 512), f32),
-            pltpu.VMEM((8, 8, 512), f32),
+            pltpu.VMEM((8, 8, 512), bf16),
+            pltpu.VMEM((8, 8, 512), bf16),
             pltpu.VMEM((16, 16, 128), bf16),
             pltpu.VMEM((16, 16, 128), bf16),
             pltpu.VMEM((256, 128), f32),
+            pltpu.VMEM((8, 8, 512), f32),
             pltpu.VMEM((8, 1, 256), f32),
-            pltpu.VMEM((2, 4, 1, 256), f32),
-            dma((2, 4)),
+            pltpu.VMEM((8, 1, 256), f32),
+            pltpu.SemaphoreType.DMA,
             dma((4, 2)),
-            *[pltpu.SemaphoreType.DMA] * 8,
-            dma((4, 2)),
-            dma((2, 4)),
+            *[pltpu.SemaphoreType.DMA] * 10,
             dma((2,)),
             dma((2,)),
             dma((2,)),

time: 42.3 us -> 42.1 us (level)
  no operation moved by 1% of the time
where the time goes in v6:
time: 42.1 us; the launch traced here: 41.9 us
  Pallas kernels  40 us (95%)
  local copies, waits for them, and re-layouts  1.25 us (3%)
  between operations  0.65 us (2%)
    pallas_call x1, Pallas kernels, layer(): pl.pallas_call(layer_kernel, out_shape=(jax.ShapeDtypeStruct((384, 128),...  40 us
    unnamed x2, local copies, waits for them, and re-layouts  1.25 us

profile of v6, /device:TPU:1, one launch (start us, length us, event | category | flops | bytes accessed | tf_op | source)
XLA Modules:
  0.0 41.9 jit_solution(5564806094510765873)
XLA Ops:
  0.6 40.0 %layer.1 = (bf16[384,128]{1,0:T(8,128)(2,1)S(1)}, f32[3,2,8,8]{3,2,1,0:T(8,128)S(1)}) custom-call(bf16[3,2,8,8,128]{4,3,2,1,0:T(8,128)(2,1)} %feat_hbm.1, f32[3,2,8,24]{3,2,1,0:T(8,128)} %place_hbm.1, s32[3,2,8,24]{3,2,1,0:T(8,128)} %anchor_hbm.1, s32[3,2,8,8]{3,2,1,0:T(8,128)} %species_hbm.1, s32[3,2,8,512]{3,2,1,0:T(8,128)} %nbr_hbm.1, ...), custom_call_target="tpu_custom_call" | custom-call | flops 4000000000 | bytes 4000000 | tf_op jit(solution)/shard_map/layer/pallas_call | solution.py:832
  40.6 0.6 %copy.26 = bf16[3,2,8,8,128]{4,3,2,1,0:T(8,128)(2,1)} copy(bf16[3,2,8,8,128]{4,3,2,1,0:T(8,128)(2,1)S(1)} %bitcast.2) | data formatting | bytes 196608
  41.3 0.6 %copy.27 = f32[3,2,8,8]{3,2,1,0:T(8,128)} copy(f32[3,2,8,8]{3,2,1,0:T(8,128)S(1)} %get-tuple-element.9) | data formatting | bytes 3072

commit v7 on v6

--- a/solution.py
+++ b/solution.py
@@ -12,7 +12,7 @@
 
 
 NT = (((1,), (1,)), ((), ()))
-CUTS = (0, 4, 6, 8, 11)
+CUTS = (0, 4, 7, 9, 11)
 
 
 def real_basis(length):
@@ -241,24 +241,24 @@
     for load in loads[:5] + small[:1]:
         load.start()
 
+    yz_steps = [(x, c, z) for x in (1, 0) for z in (2, 1, 3, 0) for c in (1, 0)]
+    x_steps = [(2, 1), (2, 0), (1, 1), (3, 1), (1, 0), (3, 0), (0, 1)]
+
     def yz_peer(r):
-        other = lax.rem(me + r, 16)
-        return other, (ix, other // 4, lax.rem(other, 4))
+        x, c, z = yz_steps[r - 1]
+        other_y = lax.rem(iy // 2 + x, 2) * 2 + lax.rem(lax.rem(iy, 2) + c, 2)
+        other_z = lax.rem(iz + z, 4)
+        return other_y * 4 + other_z, (ix, other_y, other_z)
 
     def x_peer(r):
-        other = lax.rem(ix + r, 8)
+        y, x = x_steps[r - 1]
+        other = lax.rem(ix // 2 + y, 4) * 2 + lax.rem(lax.rem(ix, 2) + x, 2)
         return other, (other, iy, iz)
 
-    def greet_yz(r, c):
+    for r in range(1, 16):
         pl.semaphore_signal(barrier, inc=1, device_id=yz_peer(r)[1], device_id_type=MESH)
-        return c
-
-    def greet_x(r, c):
+    for r in range(1, 8):
         pl.semaphore_signal(barrier, inc=1, device_id=x_peer(r)[1], device_id_type=MESH)
-        return c
-
-    lax.fori_loop(1, 16, greet_yz, 0)
-    lax.fori_loop(1, 8, greet_x, 0)
 
     def halo_peer(index):
         ox, oy, oz = index // 9 - 1, index // 3 % 3 - 1, index % 3 - 1
@@ -389,6 +389,9 @@
                 rx_atoms[iz * 2 + place] = tx_atoms[half]
 
     for index in near_ids:
+        for copy in halo_copies(index):
+            copy.start()
+    for index in far_ids:
         for copy in halo_copies(index):
             copy.start()
     for load in loads[5:] + small[1:]:
@@ -623,9 +626,6 @@
 
     arrive_b, drain_b = exchange(tx_b, rx_b, sb, rb, yz_peer, 16, me)
 
-    for index in far_ids:
-        for copy in halo_copies(index):
-            copy.start()
     strip_lane = lax.broadcasted_iota(jnp.int32, (8, 128), 1)
     strip_cell = strip_lane // 8
     within = axis_sub * 8 + strip_lane % 8

time: 42.1 us -> 41.1 us (0.976)
  Pallas kernels: 40 us -> 39 us
    pallas_call x1, Pallas kernels: 40 us -> 39 us  [layer(): pl.pallas_call(layer_kernel, out_shape=(jax.ShapeDtypeStruct((384, 128),...]
where the time goes in v7:
time: 41.1 us; the launch traced here: 40.9 us
  Pallas kernels  39 us (95%)
  local copies, waits for them, and re-layouts  1.25 us (3%)
  between operations  0.65 us (2%)
    pallas_call x1, Pallas kernels, layer(): pl.pallas_call(layer_kernel, out_shape=(jax.ShapeDtypeStruct((384, 128),...  39 us
    unnamed x2, local copies, waits for them, and re-layouts  1.25 us

profile of v7, /device:TPU:1, one launch (start us, length us, event | category | flops | bytes accessed | tf_op | source)
XLA Modules:
  0.0 40.9 jit_solution(1660935344200062135)
XLA Ops:
  0.6 39.0 %layer.1 = (bf16[384,128]{1,0:T(8,128)(2,1)S(1)}, f32[3,2,8,8]{3,2,1,0:T(8,128)S(1)}) custom-call(bf16[3,2,8,8,128]{4,3,2,1,0:T(8,128)(2,1)} %feat_hbm.1, f32[3,2,8,24]{3,2,1,0:T(8,128)} %place_hbm.1, s32[3,2,8,24]{3,2,1,0:T(8,128)} %anchor_hbm.1, s32[3,2,8,8]{3,2,1,0:T(8,128)} %species_hbm.1, s32[3,2,8,512]{3,2,1,0:T(8,128)} %nbr_hbm.1, ...), custom_call_target="tpu_custom_call" | custom-call | flops 4000000000 | bytes 4000000 | tf_op jit(solution)/shard_map/layer/pallas_call | solution.py:832
  39.7 0.6 %copy.26 = bf16[3,2,8,8,128]{4,3,2,1,0:T(8,128)(2,1)} copy(bf16[3,2,8,8,128]{4,3,2,1,0:T(8,128)(2,1)S(1)} %bitcast.2) | data formatting | bytes 196608
  40.3 0.6 %copy.27 = f32[3,2,8,8]{3,2,1,0:T(8,128)} copy(f32[3,2,8,8]{3,2,1,0:T(8,128)S(1)} %get-tuple-element.9) | data formatting | bytes 3072

commit v8 on v7

--- a/solution.py
+++ b/solution.py
@@ -12,7 +12,7 @@
 
 
 NT = (((1,), (1,)), ((), ()))
-CUTS = (0, 4, 7, 9, 11)
+CUTS = (0, 4, 6, 8, 11)
 
 
 def real_basis(length):
@@ -238,8 +238,6 @@
         pltpu.make_async_copy(kind_hbm, kind_ref, small_sem.at[0]),
         pltpu.make_async_copy(rate_hbm, rate_ref, small_sem.at[1]),
     ]
-    for load in loads[:5] + small[:1]:
-        load.start()
 
     yz_steps = [(x, c, z) for x in (1, 0) for z in (2, 1, 3, 0) for c in (1, 0)]
     x_steps = [(2, 1), (2, 0), (1, 1), (3, 1), (1, 0), (3, 0), (0, 1)]
@@ -310,6 +308,8 @@
             for ext, part, send, recv in ((feat_ext, cells, sf, rf), (pos_ext, rows, sq, rq))
         ]
 
+    for load in loads[:5] + small[:1]:
+        load.start()
     for index in far_ids:
         if index % 9 != 4:
             pl.semaphore_signal(
@@ -750,16 +750,18 @@
             device_id_type=MESH,
         )
 
-    for s in range(4):
+    for step in (2, 1, 3):
         for u in range(2):
-
-            @pl.when((s != iz) | (from_y[u] != iy))
-            def _():
-                part_copy(s, u).start()
-
-            @pl.when((s == iz) & (from_y[u] == iy))
-            def _():
-                rx_parts[from_half[u] * 4 + iz] = parts[2 * s + u]
+            part_copy(lax.rem(iz + step, 4), u).start()
+    for u in range(2):
+
+        @pl.when(from_y[u] != iy)
+        def _():
+            part_copy(iz, u).start()
+
+        @pl.when(from_y[u] == iy)
+        def _():
+            rx_parts[from_half[u] * 4 + iz] = parts[2 * iz + u]
 
     half_columns(CUTS[4], 12)
     wv = wv_ref[...]

time: 41.1 us -> 41.1 us (level)
  no operation moved by 1% of the time
where the time goes in v8:
time: 41.1 us; the launch traced here: 41 us
  Pallas kernels  39.1 us (95%)
  local copies, waits for them, and re-layouts  1.25 us (3%)
  between operations  0.65 us (2%)
    pallas_call x1, Pallas kernels, layer(): pl.pallas_call(layer_kernel, out_shape=(jax.ShapeDtypeStruct((384, 128),...  39.1 us
    unnamed x2, local copies, waits for them, and re-layouts  1.25 us

profile of v8, /device:TPU:1, one launch (start us, length us, event | category | flops | bytes accessed | tf_op | source)
XLA Modules:
  0.0 41.0 jit_solution(12329701119478911852)
XLA Ops:
  0.6 39.1 %layer.1 = (bf16[384,128]{1,0:T(8,128)(2,1)S(1)}, f32[3,2,8,8]{3,2,1,0:T(8,128)S(1)}) custom-call(bf16[3,2,8,8,128]{4,3,2,1,0:T(8,128)(2,1)} %feat_hbm.1, f32[3,2,8,24]{3,2,1,0:T(8,128)} %place_hbm.1, s32[3,2,8,24]{3,2,1,0:T(8,128)} %anchor_hbm.1, s32[3,2,8,8]{3,2,1,0:T(8,128)} %species_hbm.1, s32[3,2,8,512]{3,2,1,0:T(8,128)} %nbr_hbm.1, ...), custom_call_target="tpu_custom_call" | custom-call | flops 4000000000 | bytes 4000000 | tf_op jit(solution)/shard_map/layer/pallas_call | solution.py:834
  39.7 0.6 %copy.26 = bf16[3,2,8,8,128]{4,3,2,1,0:T(8,128)(2,1)} copy(bf16[3,2,8,8,128]{4,3,2,1,0:T(8,128)(2,1)S(1)} %bitcast.2) | data formatting | bytes 196608
  40.4 0.6 %copy.27 = f32[3,2,8,8]{3,2,1,0:T(8,128)} copy(f32[3,2,8,8]{3,2,1,0:T(8,128)S(1)} %get-tuple-element.9) | data formatting | bytes 3072

commit v9 on v7

--- a/solution.py
+++ b/solution.py
@@ -370,7 +370,7 @@
             src_ref=tx_atoms.at[half],
             dst_ref=rx_atoms.at[iz * 2 + place],
             send_sem=sa,
-            recv_sem=ra.at[iz, place],
+            recv_sem=ra,
             device_id=(ix, lax.rem(iy + step_y, 4), to_z),
             device_id_type=MESH,
         )
@@ -547,17 +547,23 @@
     edge = jnp.where((iz == 0) | (iz == 3), 1, 0)
     from_half = [edge, 1 - edge]
 
-    def atom_wait(s, u):
-        @pl.when((s != iz) | (from_y[u] != iy))
-        def _():
-            pltpu.make_async_remote_copy(
-                src_ref=tx_atoms.at[0],
-                dst_ref=rx_atoms.at[s * 2 + u],
-                send_sem=sa,
-                recv_sem=ra.at[s, u],
-                device_id=(ix, from_y[u], s),
-                device_id_type=MESH,
-            ).wait_recv()
+    def bulk(ref, send, recv, arriving):
+        for blocks, ends in ((7, 1), (6, 0)):
+
+            @pl.when(edge == ends)
+            def _():
+                whole = pltpu.make_async_remote_copy(
+                    src_ref=ref.at[pl.ds(0, blocks)],
+                    dst_ref=ref.at[pl.ds(0, blocks)],
+                    send_sem=send,
+                    recv_sem=recv,
+                    device_id=yz_peer(1)[1],
+                    device_id_type=MESH,
+                )
+                if arriving:
+                    whole.wait_recv()
+                else:
+                    whole.wait_send()
 
     y_first = iy * 16 + iz * 4
 
@@ -590,12 +596,10 @@
         stencil[source] = both
         return dot3(split(both * rows[6:7]), (high, low), NT)
 
+    bulk(rx_atoms, sa, ra, True)
     lines = None
     for steps in ((1, 3), (0, 2)):
         sources = [lax.rem(iz + step, 4) for step in steps]
-        for source in sources:
-            for u in range(2):
-                atom_wait(source, u)
         for source in sources:
             part = spread(source)
             lines = part if lines is None else lines + part
@@ -777,25 +781,7 @@
         feat_ref[...].astype(f32).reshape(384, 128) + jnp.dot(update, wo_ref[...], preferred_element_type=f32)
     ).astype(bf16)
 
-    def bulk(ref, send, recv, arriving):
-        for blocks, ends in ((7, 1), (6, 0)):
-
-            @pl.when(edge == ends)
-            def _():
-                whole = pltpu.make_async_remote_copy(
-                    src_ref=ref.at[pl.ds(0, blocks)],
-                    dst_ref=ref.at[pl.ds(0, blocks)],
-                    send_sem=send,
-                    recv_sem=recv,
-                    device_id=yz_peer(1)[1],
-                    device_id_type=MESH,
-                )
-                if arriving:
-                    whole.wait_recv()
-                else:
-                    whole.wait_send()
-
-    bulk(rx_atoms, sa, ra.at[0, 0], False)
+    bulk(rx_atoms, sa, ra, False)
     drain_b()
     drain_c()
     drain_c2()
@@ -873,7 +859,7 @@
             pltpu.VMEM((8, 1, 256), f32),
             pltpu.VMEM((8, 1, 256), f32),
             pltpu.SemaphoreType.DMA,
-            dma((4, 2)),
+            pltpu.SemaphoreType.DMA,
             *[pltpu.SemaphoreType.DMA] * 10,
             dma((2,)),
             dma((2,)),

time: 41.1 us -> 41.3 us (level)
  no operation moved by 1% of the time
where the time goes in v9:
time: 41.3 us; the launch traced here: 41.1 us
  Pallas kernels  39.2 us (95%)
  local copies, waits for them, and re-layouts  1.25 us (3%)
  between operations  0.65 us (2%)
    pallas_call x1, Pallas kernels, layer(): pl.pallas_call(layer_kernel, out_shape=(jax.ShapeDtypeStruct((384, 128),...  39.2 us
    unnamed x2, local copies, waits for them, and re-layouts  1.25 us

profile of v9, /device:TPU:1, one launch (start us, length us, event | category | flops | bytes accessed | tf_op | source)
XLA Modules:
  0.0 41.1 jit_solution(3630746270887657230)
XLA Ops:
  0.6 39.2 %layer.1 = (bf16[384,128]{1,0:T(8,128)(2,1)S(1)}, f32[3,2,8,8]{3,2,1,0:T(8,128)S(1)}) custom-call(bf16[3,2,8,8,128]{4,3,2,1,0:T(8,128)(2,1)} %feat_hbm.1, f32[3,2,8,24]{3,2,1,0:T(8,128)} %place_hbm.1, s32[3,2,8,24]{3,2,1,0:T(8,128)} %anchor_hbm.1, s32[3,2,8,8]{3,2,1,0:T(8,128)} %species_hbm.1, s32[3,2,8,512]{3,2,1,0:T(8,128)} %nbr_hbm.1, ...), custom_call_target="tpu_custom_call" | custom-call | flops 4000000000 | bytes 4000000 | tf_op jit(solution)/shard_map/layer/pallas_call | solution.py:818
  39.9 0.6 %copy.26 = bf16[3,2,8,8,128]{4,3,2,1,0:T(8,128)(2,1)} copy(bf16[3,2,8,8,128]{4,3,2,1,0:T(8,128)(2,1)S(1)} %bitcast.2) | data formatting | bytes 196608
  40.5 0.6 %copy.27 = f32[3,2,8,8]{3,2,1,0:T(8,128)} copy(f32[3,2,8,8]{3,2,1,0:T(8,128)S(1)} %get-tuple-element.9) | data formatting | bytes 3072

commit v10 on v9

--- a/solution.py
+++ b/solution.py
@@ -12,7 +12,7 @@
 
 
 NT = (((1,), (1,)), ((), ()))
-CUTS = (0, 4, 7, 9, 11)
+CUTS = (0, 4, 6, 8, 11)
 
 
 def real_basis(length):
@@ -238,8 +238,6 @@
         pltpu.make_async_copy(kind_hbm, kind_ref, small_sem.at[0]),
         pltpu.make_async_copy(rate_hbm, rate_ref, small_sem.at[1]),
     ]
-    for load in loads[:5] + small[:1]:
-        load.start()
 
     yz_steps = [(x, c, z) for x in (1, 0) for z in (2, 1, 3, 0) for c in (1, 0)]
     x_steps = [(2, 1), (2, 0), (1, 1), (3, 1), (1, 0), (3, 0), (0, 1)]
@@ -310,6 +308,8 @@
             for ext, part, send, recv in ((feat_ext, cells, sf, rf), (pos_ext, rows, sq, rq))
         ]
 
+    for load in loads[:5] + small[:1]:
+        load.start()
     for index in far_ids:
         if index % 9 != 4:
             pl.semaphore_signal(
@@ -754,16 +754,18 @@
             device_id_type=MESH,
         )
 
-    for s in range(4):
+    for step in (2, 1, 3):
         for u in range(2):
-
-            @pl.when((s != iz) | (from_y[u] != iy))
-            def _():
-                part_copy(s, u).start()
-
-            @pl.when((s == iz) & (from_y[u] == iy))
-            def _():
-                rx_parts[from_half[u] * 4 + iz] = parts[2 * s + u]
+            part_copy(lax.rem(iz + step, 4), u).start()
+    for u in range(2):
+
+        @pl.when(from_y[u] != iy)
+        def _():
+            part_copy(iz, u).start()
+
+        @pl.when(from_y[u] == iy)
+        def _():
+            rx_parts[from_half[u] * 4 + iz] = parts[2 * iz + u]
 
     half_columns(CUTS[4], 12)
     wv = wv_ref[...]

time: 41.3 us -> 41.3 us (level)
  no operation moved by 1% of the time
where the time goes in v10:
time: 41.3 us; the launch traced here: 41.2 us
  Pallas kernels  39.3 us (95%)
  local copies, waits for them, and re-layouts  1.25 us (3%)
  between operations  0.65 us (2%)
    pallas_call x1, Pallas kernels, layer(): pl.pallas_call(layer_kernel, out_shape=(jax.ShapeDtypeStruct((384, 128),...  39.3 us
    unnamed x2, local copies, waits for them, and re-layouts  1.25 us

profile of v10, /device:TPU:1, one launch (start us, length us, event | category | flops | bytes accessed | tf_op | source)
XLA Modules:
  0.0 41.2 jit_solution(4150903822756965895)
XLA Ops:
  0.6 39.3 %layer.1 = (bf16[384,128]{1,0:T(8,128)(2,1)S(1)}, f32[3,2,8,8]{3,2,1,0:T(8,128)S(1)}) custom-call(bf16[3,2,8,8,128]{4,3,2,1,0:T(8,128)(2,1)} %feat_hbm.1, f32[3,2,8,24]{3,2,1,0:T(8,128)} %place_hbm.1, s32[3,2,8,24]{3,2,1,0:T(8,128)} %anchor_hbm.1, s32[3,2,8,8]{3,2,1,0:T(8,128)} %species_hbm.1, s32[3,2,8,512]{3,2,1,0:T(8,128)} %nbr_hbm.1, ...), custom_call_target="tpu_custom_call" | custom-call | flops 4000000000 | bytes 4000000 | tf_op jit(solution)/shard_map/layer/pallas_call | solution.py:820
  39.9 0.6 %copy.26 = bf16[3,2,8,8,128]{4,3,2,1,0:T(8,128)(2,1)} copy(bf16[3,2,8,8,128]{4,3,2,1,0:T(8,128)(2,1)S(1)} %bitcast.2) | data formatting | bytes 196608
  40.6 0.6 %copy.27 = f32[3,2,8,8]{3,2,1,0:T(8,128)} copy(f32[3,2,8,8]{3,2,1,0:T(8,128)S(1)} %get-tuple-element.9) | data formatting | bytes 3072
